TPU v7x, 128 devices: a whole 4x4x4 slice. The times are simulated.
128 devices in a mesh: blk: 128 (over y, x, z, core).
Axes of the slice: x: 4, y: 4, z: 4, core: 2. Of those that a mesh axis runs over, the one named last changes fastest.
Arguments:
- node_latent: bfloat16 [524288, 128], P('blk'), may hold values from -16 to 16
- edge_latent: bfloat16 [3145728, 128], P('blk'), may hold values from -6 to 6
- edge_ends: int32 [2, 3145728], P(None, 'blk'), may hold values from 0 to 5631, as said below
- edge_owned: int32 [3145728], P('blk'), may hold values from 0 to 1, as said below
- send_index: int32 [128, 6, 256], P('blk'), may hold values from 0 to 4095, as said below
- edge_w1: bfloat16 [2, 384, 128], replicated, may hold values from -0.3125 to 0.3125
- edge_b1: float32 [2, 128], replicated, may hold values from -3 to 3
- edge_w2: bfloat16 [2, 128, 128], replicated, may hold values from -0.5 to 0.5
- edge_gain: float32 [2, 128], replicated, may hold values from 0.5 to 1.5
- edge_shift: float32 [2, 128], replicated, may hold values from -2 to 2
- node_w1: bfloat16 [2, 256, 128], replicated, may hold values from -0.375 to 0.375
- node_b1: float32 [2, 128], replicated, may hold values from -3 to 3
- node_w2: bfloat16 [2, 128, 128], replicated, may hold values from -0.5 to 0.5
- node_gain: float32 [2, 128], replicated, may hold values from 0.5 to 1.5
- node_shift: float32 [2, 128], replicated, may hold values from -2 to 2
Outputs:
- node_out: bfloat16 [524288, 128], P('blk')
- edge_out: bfloat16 [3145728, 128], P('blk')
Inputs may be any that keep to these rules, and one draw needn't show every extreme that they name: edge_ends[0] holds each slot's sender, edge_ends[1] its receiver, as entries of the block's extended node list. Slot s of a block lies in tile t = s // 128; each of its ends is either an own node from (t // 6) * 128 to (t // 6 + 1) * 128 - 1 or a halo entry from 4096 + (t % 6) * 256 to 4096 + (t % 6 + 1) * 256 - 1; at most one end of a slot is a halo entry. `edge_owned`: in each block the slots with 1 come first; every block has at least 15360 of them. send_index[b, k] lists 256 distinct nodes of block b.
All inputs are finite; a program needn't handle non-finite values.
Results may differ from a plain program's by a relative error of at most 0.0085.
Values may be sent and summed in bfloat16 or wider, within the bound.
No kernel may reach another device: no remote copies, remote signals or barrier semaphores. Data moves between devices by JAX's collectives and lax.ppermute only.
A program may use at most 128 MiB of HBM per device.

v0:
```python
import functools

import jax
import jax.numpy as jnp
from jax import lax
from jax.sharding import Mesh
from jax.sharding import PartitionSpec as P

LAYERS = 2
FACES = 6
GX = 4
GY = 4
BLK = ("blk_0", "blk_1", "blk_2", "blk_3")


def passed_along(block, axis, distance):
    devices = range(lax.axis_size(axis))
    route = [((i - distance) % len(devices), i) for i in devices]
    return lax.ppermute(block, axis, route)


def over_axes(shard, axes):
    return functools.reduce(lax.psum, axes, shard)


def row_norm(mixed):
    centre = mixed - jnp.mean(mixed, axis=1, keepdims=True)
    spread = jnp.mean(centre * centre, axis=1, keepdims=True)
    return centre * lax.rsqrt(spread + 1e-05)


def one_hots(ends, own_rows, halo_rows, tile_rows, dtype):
    groups = own_rows // tile_rows
    index = ends.reshape(groups, FACES, tile_rows)
    own_local = index - (jnp.arange(groups, dtype=jnp.int32) * tile_rows)[:, None, None]
    halo_local = index - own_rows - (jnp.arange(FACES, dtype=jnp.int32) * halo_rows)[None, :, None]
    own_hot = (own_local[..., None] == jnp.arange(tile_rows, dtype=jnp.int32)).astype(dtype)
    halo_hot = (halo_local[..., None] == jnp.arange(halo_rows, dtype=jnp.int32)).astype(dtype)
    return (own_hot, halo_hot)


def select_rows(hots, own_table, halo_table):
    own_hot, halo_hot = hots
    groups, faces, tile_rows, _ = own_hot.shape
    columns = own_table.shape[1]
    own_view = own_table.reshape(groups, tile_rows, columns)
    halo_view = halo_table.reshape(faces, halo_hot.shape[3], columns)
    picked = jnp.einsum(
        "bken,bnc->bkec", own_hot, own_view, preferred_element_type=jnp.float32, precision=None
    )
    picked = picked + jnp.einsum(
        "bkeh,khc->bkec", halo_hot, halo_view, preferred_element_type=jnp.float32, precision=None
    )
    return picked.reshape(groups * faces * tile_rows, columns)


def per_device(
    node_latent,
    edge_latent,
    edge_ends,
    edge_owned,
    send_index,
    edge_w1,
    edge_b1,
    edge_w2,
    edge_gain,
    edge_shift,
    node_w1,
    node_b1,
    node_w2,
    node_gain,
    node_shift,
):
    width = node_latent.shape[1]
    own_rows = node_latent.shape[0]
    halo_rows = send_index.shape[2]
    tile_rows = min(128, own_rows)
    groups = own_rows // tile_rows
    offsets = (1, -1, GX, -GX, GX * GY, -GX * GY)
    face_rows = send_index[0]
    flat_faces = face_rows.reshape(-1)
    owned = edge_owned.astype(jnp.float32)[:, None]
    total_nodes = own_rows * lax.axis_size(BLK)
    recv_hots = one_hots(edge_ends[1], own_rows, halo_rows, tile_rows, jnp.bfloat16)
    latents = node_latent
    edge_state = edge_latent
    for layer_id in range(LAYERS):
        w_first = edge_w1[layer_id]
        outgoing = latents[face_rows]
        arrived = [
            passed_along(outgoing[face_id], BLK, offsets[face_id]) for face_id in range(FACES)
        ]
        halo_table = jnp.concatenate(arrived, axis=0)
        send_hots = one_hots(edge_ends[0], own_rows, halo_rows, tile_rows, jnp.bfloat16)
        from_send = select_rows(send_hots, latents, halo_table).astype(jnp.bfloat16)
        from_recv = select_rows(recv_hots, latents, halo_table).astype(jnp.bfloat16)
        joined = jnp.concatenate([edge_state, from_send, from_recv], axis=1)
        before = jnp.dot(joined, w_first, preferred_element_type=jnp.float32)
        hidden = jax.nn.relu(before + edge_b1[layer_id]).astype(jnp.bfloat16)
        mixed = jnp.dot(hidden, edge_w2[layer_id], preferred_element_type=jnp.float32)
        normed = edge_gain[layer_id] * row_norm(mixed) + edge_shift[layer_id]
        edges_new = (edge_state.astype(jnp.float32) + owned * normed).astype(jnp.bfloat16)
        message = (
            (owned * edges_new.astype(jnp.float32))
            .astype(jnp.bfloat16)
            .reshape(groups, FACES, tile_rows, width)
        )
        own_sums = jnp.einsum(
            "bken,bkec->bnc", recv_hots[0], message, preferred_element_type=jnp.float32
        ).reshape(own_rows, width)
        halo_sums = jnp.einsum(
            "bkeh,bkec->khc", recv_hots[1], message, preferred_element_type=jnp.float32
        )
        returned = [
            passed_along(halo_sums[face_id].astype(jnp.bfloat16), BLK, -offsets[face_id]).astype(
                jnp.float32
            )
            for face_id in range(FACES)
        ]
        node_sums = own_sums.at[flat_faces].add(jnp.concatenate(returned, axis=0))
        aggregate = node_sums.astype(jnp.bfloat16)
        node_in = jnp.concatenate([latents, aggregate], axis=1)
        node_hidden = jax.nn.relu(
            jnp.dot(node_in, node_w1[layer_id], preferred_element_type=jnp.float32)
            + node_b1[layer_id]
        ).astype(jnp.bfloat16)
        update = jnp.dot(node_hidden, node_w2[layer_id], preferred_element_type=jnp.float32)
        sums, squares = (
            over_axes(jnp.sum(update, axis=0), BLK),
            over_axes(jnp.sum(update * update, axis=0), BLK),
        )
        centre_mean = sums / total_nodes
        variance = jnp.maximum(squares / total_nodes - centre_mean * centre_mean, 0.0)
        deviation = update - centre_mean
        latents = (
            latents.astype(jnp.float32)
            + node_gain[layer_id] * deviation * lax.rsqrt(variance + 1e-05)
            + node_shift[layer_id]
        ).astype(jnp.bfloat16)
        edge_state = edges_new
    return (latents, edge_state)


def solution(mesh):
    torus = Mesh(mesh.devices.reshape(4, 4, 4, 2), ("blk_0", "blk_1", "blk_2", "blk_3"))
    return jax.shard_map(
        per_device,
        mesh=torus,
        in_specs=(
            P(BLK, None),
            P(BLK, None),
            P(None, BLK),
            P(BLK),
            P(BLK, None, None),
            P(),
            P(),
            P(),
            P(),
            P(),
            P(),
            P(),
            P(),
            P(),
            P(),
        ),
        out_specs=(P(BLK, None), P(BLK, None)),
        check_vma=False,
    )
```

profile of v0, /device:TPU:1, one launch (start us, length us, event | category | flops | bytes accessed | tf_op | source)
XLA Modules:
  0.0 374.6 jit_solution(3821135400010055631)
XLA Ops:
  0.6 0.8 fusion.120
  1.5 4.0 %gather_fusion = bf16[1536,128]{1,0:T(8,128)(2,1)S(1)} fusion(bf16[4096,128]{1,0:T(8,128)(2,1)} %param.15, s32[2048]{0:T(1024)S(1)} %pad_clamp_fusion), kind=kCustom, calls=%fused_computation | custom fusion | bytes 792576 | tf_op jit(solution)/shard_map/gather | solution.py:89
  5.5 6.1 %collective-permute-start.5 = (bf16[256,128]{1,0:T(8,128)(2,1)S(1)}, bf16[256,128]{1,0:T(8,128)(2,1)S(1)}, u32[]{:S(2)}, u32[]{:S(2)}) collective-permute-start(bf16[256,128]{1,0:T(8,128)(2,1)S(1)} %get-tuple-element.46), channel_id=1, source_target_pairs={{16,0},{17,1},{18,2},{19,3},{20,4},{21,5},{22,6},{23,7},{24,8},{25... | collective-permute-start | bytes 196616 | tf_op jit(solution)/shard_map/ppermute | solution.py:19
  11.6 8.1 %collective-permute-start.3 = (bf16[256,128]{1,0:T(8,128)(2,1)S(1)}, bf16[256,128]{1,0:T(8,128)(2,1)S(1)}, u32[]{:S(2)}, u32[]{:S(2)}) collective-permute-start(bf16[256,128]{1,0:T(8,128)(2,1)S(1)} %get-tuple-element.48), channel_id=1, source_target_pairs={{4,0},{5,1},{6,2},{7,3},{8,4},{9,5},{10,6},{11,7},{12,8},{13,9},{1... | collective-permute-start | bytes 196616 | tf_op jit(solution)/shard_map/ppermute | solution.py:19
  19.7 2.1 collective-permute-start
  21.9 0.8 slice_bitcast_fusion.15
  22.6 1.3 slice_bitcast_fusion.13
  23.9 0.9 convert_element_type.146
  24.8 1.5 slice_reduce_fusion
  26.4 0.1 add_subtract_fusion
  26.6 7.9 %fusion.33 = f32[32,6,128,128]{3,2,1,0:T(8,128)S(1)} fusion(bf16[32,128,128,1]{2,1,3,0:T(8,128)(2,1)S(1)} %bitcast.163, s32[32,6,128]{2,1,0:T(8,128)S(1)} %get-tuple-element.56), kind=kOutput, calls=%fused_computation.52 | convolution fusion | flops 808452096 | bytes 13729792 | tf_op jit(solution)/shard_map/bken,bnc->bkec/dot_general | solution.py:48
  34.5 3.4 fusion.37
  37.9 0.5 slice_bitcast_fusion.16
  38.4 0.6 slice_bitcast_fusion.12
  39.1 0.3 collective-permute-start.1
  39.3 3.7 collective-permute-done.1
  43.1 8.2 %fusion.29 = bf16[32,6,128,128]{3,2,1,0:T(8,128)(2,1)} fusion(f32[32,6,128,128]{3,2,1,0:T(8,128)S(1)} %fusion.33, bf16[6,256,128,1]{2,1,0,3:T(8,128)(2,1)S(1)} %bitcast.172, s32[32,6,128]{2,0,1:T(8,128)S(1)} %copy.29), kind=kOutput, calls=%fused_computation.43 | convolution fusion | flops 1623195648 | bytes 19365888 | tf_op jit(solution)/shard_map/bkeh,khc->bkec/dot_general | solution.py:51
  51.4 8.8 %fusion.28 = bf16[32,6,128,128]{3,2,1,0:T(8,128)(2,1)} fusion(f32[32,6,128,128]{3,2,1,0:T(8,128)S(1)} %fusion.37, bf16[6,256,128,1]{2,1,0,3:T(8,128)(2,1)S(1)} %bitcast.173, s32[32,6,128]{2,0,1:T(8,128)S(1)} %copy.32), kind=kOutput, calls=%fused_computation.41 | convolution fusion | flops 1623195648 | bytes 19365888 | tf_op jit(solution)/shard_map/bkeh,khc->bkec/dot_general | solution.py:51
  60.2 14.5 %fusion.139 = (f32[24576]{0:T(1024)S(1)}, f32[24576,128]{1,0:T(8,128)}) fusion(bf16[2,128,128]{2,1,0:T(8,128)(2,1)S(1)} %copy-done.15, bf16[24576,128]{1,0:T(8,128)(2,1)} %bitcast.179, bf16[24576,128]{1,0:T(8,128)(2,1)} %bitcast.178, bf16[24576,128]{1,0:T(8,128)(2,1)} %param.16, f32[128]{0:T(128)S(1)} %get-tuple-element.67, ...), kind=kOutput, calls=%fused_computation.195 | convolution fusion | flops 3290406912 | bytes 31687168 | tf_op jit(solution)/shard_map/dot_general | solution.py:100
  74.7 10.3 %multiply_reduce_fusion.1 = f32[24576]{0:T(1024)S(1)} fusion(f32[24576,128]{1,0:T(8,128)} %get-tuple-element.75, f32[24576]{0:T(1024)S(1)} %broadcast_multiply_fusion.1), kind=kLoop, calls=%fused_computation.47 | loop fusion | flops 9412608 | bytes 12779520 | tf_op jit(solution)/shard_map/reduce_sum | solution.py:28
  85.0 22.2 %fusion.24 = (bf16[24576,128]{1,0:T(8,128)(2,1)S(1)}, bf16[24576,128]{1,0:T(8,128)(2,1)}) fusion(f32[24576]{0:T(1024)S(1)} %convert_element_type.146, f32[128]{0:T(128)S(1)} %get-tuple-element.81, f32[24576]{0:T(1024)S(1)} %add_rsqrt_fusion.1, f32[24576,128]{1,0:T(8,128)S(1)} %copy-done.1, f32[24576]{0:T(1024)S(1)} %broadcast_multiply_fusion.1, ...), kind=kLoop, calls=%fused_computation.34 | loop fusion | flops 34603008 | bytes 31753216 | tf_op jit(solution)/shard_map/convert_element_type | solution.py:105
  107.2 3.7 fusion.85
  111.0 5.2 %collective-permute-start.6 = (bf16[256,128]{1,0:T(8,128)(2,1)S(1)}, bf16[256,128]{1,0:T(8,128)(2,1)S(1)}, u32[]{:S(2)}, u32[]{:S(2)}) collective-permute-start(bf16[256,128]{1,0:T(8,128)(2,1)S(1)} %get-tuple-element.45), channel_id=1, source_target_pairs={{1,0},{2,1},{3,2},{4,3},{5,4},{6,5},{7,6},{8,7},{9,8},{10,9},{11,1... | collective-permute-start | bytes 196616 | tf_op jit(solution)/shard_map/ppermute | solution.py:19
  116.2 3.7 fusion.36
  119.9 5.1 %collective-permute-start.10 = (bf16[256,128]{1,0:T(8,128)(2,1)S(1)}, bf16[256,128]{1,0:T(8,128)(2,1)S(1)}, u32[]{:S(2)}, u32[]{:S(2)}) collective-permute-start(bf16[256,128]{1,0:T(8,128)(2,1)S(1)} %get-tuple-element.41), channel_id=1, source_target_pairs={{16,0},{17,1},{18,2},{19,3},{20,4},{21,5},{22,6},{23,7},{24,8},{25... | collective-permute-start | bytes 196616 | tf_op jit(solution)/shard_map/ppermute | solution.py:19
  125.0 7.2 %collective-permute-start.8 = (bf16[256,128]{1,0:T(8,128)(2,1)S(1)}, bf16[256,128]{1,0:T(8,128)(2,1)S(1)}, u32[]{:S(2)}, u32[]{:S(2)}) collective-permute-start(bf16[256,128]{1,0:T(8,128)(2,1)S(1)} %get-tuple-element.43), channel_id=1, source_target_pairs={{4,0},{5,1},{6,2},{7,3},{8,4},{9,5},{10,6},{11,7},{12,8},{13,9},{1... | collective-permute-start | bytes 196616 | tf_op jit(solution)/shard_map/ppermute | solution.py:19
  132.2 9.1 %collective-permute-done.7 = bf16[256,128]{1,0:T(8,128)(2,1)S(1)} collective-permute-done((bf16[256,128]{1,0:T(8,128)(2,1)S(1)}, bf16[256,128]{1,0:T(8,128)(2,1)S(1)}, u32[]{:S(2)}, u32[]{:S(2)}) %collective-permute-start.7) | collective-permute-done | bytes 65568 | tf_op jit(solution)/shard_map/ppermute | solution.py:19
  141.4 10.8 %scatter_custom_fusion = f32[4096,128]{1,0:T(8,128)} fusion(f32[4096,128]{1,0:T(8,128)} %bitcast.170, s32[1536]{0:T(1024)S(1)} %fusion.121, bf16[1536,128]{1,0:T(8,128)(2,1)S(1)} %constant_dynamic-update-slice_fusion.6), kind=kCustom, calls=%fused_computation.96 | custom fusion | flops 393216 | bytes 2490368 | tf_op jit(solution)/shard_map/scatter-add | solution.py:120
  152.2 1.7 convert_element_type.162
  153.9 2.6 fusion.135
  156.5 6.0 %all-reduce.5 = (f32[128]{0:T(128)S(1)}, f32[128]{0:T(128)S(1)}) all-reduce(f32[128]{0:T(128)S(1)} %get-tuple-element.5, f32[128]{0:T(128)S(1)} %get-tuple-element.4), channel_id=1, replica_groups=mesh['blk_0'=4,'blk_1'=4,'blk_2'=4,'blk_3'=2] {'blk_0'}, use_global_device_ids=true, to_apply=%region_9.10 | all-reduce | flops 256 | bytes 2048 | tf_op jit(solution)/shard_map/psum | solution.py:23
  162.5 6.0 %all-reduce.3 = (f32[128]{0:T(128)S(1)}, f32[128]{0:T(128)S(1)}) all-reduce(f32[128]{0:T(128)S(1)} %get-tuple-element.18, f32[128]{0:T(128)S(1)} %get-tuple-element.19), channel_id=1, replica_groups=mesh['blk_0'=4,'blk_1'=4,'blk_2'=4,'blk_3'=2] {'blk_1'}, use_global_device_ids=true, to_apply=%region_10.11 | all-reduce | flops 256 | bytes 2048 | tf_op jit(solution)/shard_map/psum | solution.py:23
  168.5 13.9 %all-reduce.1 = (f32[128]{0:T(128)S(1)}, f32[128]{0:T(128)S(1)}) all-reduce(f32[128]{0:T(128)S(1)} %get-tuple-element.14, f32[128]{0:T(128)S(1)} %get-tuple-element.15), channel_id=1, replica_groups=mesh['blk_0'=4,'blk_1'=4,'blk_2'=4,'blk_3'=2] {'blk_2'}, use_global_device_ids=true, to_apply=%region_11.12 | all-reduce | flops 256 | bytes 2048 | tf_op jit(solution)/shard_map/psum | solution.py:23
  182.4 7.8 %all-reduce.7 = (f32[128]{0:T(128)S(1)}, f32[128]{0:T(128)S(1)}) all-reduce(f32[128]{0:T(128)S(1)} %get-tuple-element.10, f32[128]{0:T(128)S(1)} %get-tuple-element.11), channel_id=1, replica_groups=mesh['blk_0'=4,'blk_1'=4,'blk_2'=4,'blk_3'=2] {'blk_3'}, use_global_device_ids=true, to_apply=%region_12.13 | all-reduce | flops 256 | bytes 2048 | tf_op jit(solution)/shard_map/psum | solution.py:23
  190.2 2.1 add_convert_fusion.2
  192.3 3.2 gather_fusion.1
  195.5 2.2 collective-permute-start.12
  197.7 7.8 %fusion.32 = f32[32,6,128,128]{3,2,1,0:T(8,128)S(1)} fusion(bf16[32,128,128,1]{2,1,3,0:T(8,128)(2,1)S(1)} %bitcast.161, s32[32,6,128]{2,1,0:T(8,128)S(1)} %get-tuple-element.56), kind=kOutput, calls=%fused_computation.51 | convolution fusion | flops 808452096 | bytes 13729792 | tf_op jit(solution)/shard_map/bken,bnc->bkec/dot_general | solution.py:48
  205.5 3.4 fusion.35
  208.9 2.4 collective-permute-start.17
  211.3 0.6 collective-permute-start.16
  211.9 6.2 %collective-permute-start.15 = (bf16[256,128]{1,0:T(8,128)(2,1)S(1)}, bf16[256,128]{1,0:T(8,128)(2,1)S(1)}, u32[]{:S(2)}, u32[]{:S(2)}) collective-permute-start(bf16[256,128]{1,0:T(8,128)(2,1)S(1)} %get-tuple-element.36), channel_id=1, source_target_pairs={{4,0},{5,1},{6,2},{7,3},{8,4},{9,5},{10,6},{11,7},{12,8},{13,9},{1... | collective-permute-start | bytes 196616 | tf_op jit(solution)/shard_map/ppermute | solution.py:19
  218.2 4.0 %collective-permute-done.13 = bf16[256,128]{1,0:T(8,128)(2,1)S(1)} collective-permute-done((bf16[256,128]{1,0:T(8,128)(2,1)S(1)}, bf16[256,128]{1,0:T(8,128)(2,1)S(1)}, u32[]{:S(2)}, u32[]{:S(2)}) %collective-permute-start.13) | collective-permute-done | bytes 65568 | tf_op jit(solution)/shard_map/ppermute | solution.py:19
  222.2 5.1 %collective-permute-done.14 = bf16[256,128]{1,0:T(8,128)(2,1)S(1)} collective-permute-done((bf16[256,128]{1,0:T(8,128)(2,1)S(1)}, bf16[256,128]{1,0:T(8,128)(2,1)S(1)}, u32[]{:S(2)}, u32[]{:S(2)}) %collective-permute-start.14) | collective-permute-done | bytes 65568 | tf_op jit(solution)/shard_map/ppermute | solution.py:19
  227.3 8.3 %fusion.27 = bf16[32,6,128,128]{3,2,1,0:T(8,128)(2,1)} fusion(f32[32,6,128,128]{3,2,1,0:T(8,128)S(1)} %fusion.32, bf16[6,256,128,1]{2,1,0,3:T(8,128)(2,1)S(1)} %bitcast.174, s32[32,6,128]{2,0,1:T(8,128)S(1)} %copy.29), kind=kOutput, calls=%fused_computation.39 | convolution fusion | flops 1623195648 | bytes 19365888 | tf_op jit(solution)/shard_map/bkeh,khc->bkec/dot_general | solution.py:51
  235.6 8.8 %fusion.26 = bf16[32,6,128,128]{3,2,1,0:T(8,128)(2,1)} fusion(f32[32,6,128,128]{3,2,1,0:T(8,128)S(1)} %fusion.35, bf16[6,256,128,1]{2,1,0,3:T(8,128)(2,1)S(1)} %bitcast.175, s32[32,6,128]{2,0,1:T(8,128)S(1)} %copy.32), kind=kOutput, calls=%fused_computation.37 | convolution fusion | flops 1623195648 | bytes 19365888 | tf_op jit(solution)/shard_map/bkeh,khc->bkec/dot_general | solution.py:51
  244.4 14.5 %fusion.148 = (f32[24576]{0:T(1024)S(1)}, f32[24576,128]{1,0:T(8,128)}) fusion(bf16[2,128,128]{2,1,0:T(8,128)(2,1)S(1)} %copy-done.15, bf16[24576,128]{1,0:T(8,128)(2,1)} %bitcast.177, bf16[24576,128]{1,0:T(8,128)(2,1)} %bitcast.176, bf16[24576,128]{1,0:T(8,128)(2,1)} %get-tuple-element.27, f32[128]{0:T(128)S(1)} %get-tuple-element.66, ...), kind=kOutput, calls=%fused_computation.196 | convolution fusion | flops 3290406912 | bytes 31687168 | tf_op jit(solution)/shard_map/dot_general | solution.py:100
  258.9 10.7 %multiply_reduce_fusion = f32[24576]{0:T(1024)S(1)} fusion(f32[24576,128]{1,0:T(8,128)} %get-tuple-element.78, f32[24576]{0:T(1024)S(1)} %broadcast_multiply_fusion), kind=kLoop, calls=%fused_computation.45 | loop fusion | flops 9412608 | bytes 12779520 | tf_op jit(solution)/shard_map/reduce_sum | solution.py:28
  269.7 22.2 %multiply_convert_fusion = (bf16[24576,128]{1,0:T(8,128)(2,1)S(1)}, bf16[24576,128]{1,0:T(8,128)(2,1)}) fusion(f32[24576]{0:T(1024)S(1)} %convert_element_type.146, f32[128]{0:T(128)S(1)} %copy-done.7, f32[24576]{0:T(1024)S(1)} %add_rsqrt_fusion, f32[24576,128]{1,0:T(8,128)S(1)} %copy-done, f32[24576]{0:T(1024)S(1)} %broadcast_multiply_fusion, ...), kind=kLoop, calls=%fused_computation.44 | loop fusion | flops 34603008 | bytes 31753216 | tf_op jit(solution)/shard_map/convert_element_type | solution.py:105
  291.9 3.7 fusion.82
  295.7 1.8 collective-permute-start.18
  297.4 3.7 fusion.34
  301.1 5.1 %collective-permute-start.22 = (bf16[256,128]{1,0:T(8,128)(2,1)S(1)}, bf16[256,128]{1,0:T(8,128)(2,1)S(1)}, u32[]{:S(2)}, u32[]{:S(2)}) collective-permute-start(bf16[256,128]{1,0:T(8,128)(2,1)S(1)} %get-tuple-element.29), channel_id=1, source_target_pairs={{16,0},{17,1},{18,2},{19,3},{20,4},{21,5},{22,6},{23,7},{24,8},{25... | collective-permute-start | bytes 196616 | tf_op jit(solution)/shard_map/ppermute | solution.py:19
  306.2 7.2 %collective-permute-start.20 = (bf16[256,128]{1,0:T(8,128)(2,1)S(1)}, bf16[256,128]{1,0:T(8,128)(2,1)S(1)}, u32[]{:S(2)}, u32[]{:S(2)}) collective-permute-start(bf16[256,128]{1,0:T(8,128)(2,1)S(1)} %get-tuple-element.31), channel_id=1, source_target_pairs={{4,0},{5,1},{6,2},{7,3},{8,4},{9,5},{10,6},{11,7},{12,8},{13,9},{1... | collective-permute-start | bytes 196616 | tf_op jit(solution)/shard_map/ppermute | solution.py:19
  313.4 1.4 collective-permute-start.19
  314.7 7.7 %collective-permute-done.19 = bf16[256,128]{1,0:T(8,128)(2,1)S(1)} collective-permute-done((bf16[256,128]{1,0:T(8,128)(2,1)S(1)}, bf16[256,128]{1,0:T(8,128)(2,1)S(1)}, u32[]{:S(2)}, u32[]{:S(2)}) %collective-permute-start.19) | collective-permute-done | bytes 65568 | tf_op jit(solution)/shard_map/ppermute | solution.py:19
  322.6 10.8 %scatter_custom_fusion.1 = f32[4096,128]{1,0:T(8,128)} fusion(f32[4096,128]{1,0:T(8,128)} %bitcast.169, s32[1536]{0:T(1024)S(1)} %fusion.121, bf16[1536,128]{1,0:T(8,128)(2,1)S(1)} %constant_dynamic-update-slice_fusion.18), kind=kCustom, calls=%fused_computation.94 | custom fusion | flops 393216 | bytes 2490368 | tf_op jit(solution)/shard_map/scatter-add | solution.py:120
  333.4 1.7 convert_element_type.180
  335.1 2.6 fusion.134
  337.7 6.0 %all-reduce.4 = (f32[128]{0:T(128)S(1)}, f32[128]{0:T(128)S(1)}) all-reduce(f32[128]{0:T(128)S(1)} %get-tuple-element.3, f32[128]{0:T(128)S(1)} %get-tuple-element.2), channel_id=1, replica_groups=mesh['blk_0'=4,'blk_1'=4,'blk_2'=4,'blk_3'=2] {'blk_0'}, use_global_device_ids=true, to_apply=%region_22.23 | all-reduce | flops 256 | bytes 2048 | tf_op jit(solution)/shard_map/psum | solution.py:23
  343.7 6.0 %all-reduce.2 = (f32[128]{0:T(128)S(1)}, f32[128]{0:T(128)S(1)}) all-reduce(f32[128]{0:T(128)S(1)} %get-tuple-element.16, f32[128]{0:T(128)S(1)} %get-tuple-element.17), channel_id=1, replica_groups=mesh['blk_0'=4,'blk_1'=4,'blk_2'=4,'blk_3'=2] {'blk_1'}, use_global_device_ids=true, to_apply=%region_23.24 | all-reduce | flops 256 | bytes 2048 | tf_op jit(solution)/shard_map/psum | solution.py:23
  349.7 13.9 %all-reduce = (f32[128]{0:T(128)S(1)}, f32[128]{0:T(128)S(1)}) all-reduce(f32[128]{0:T(128)S(1)} %get-tuple-element.12, f32[128]{0:T(128)S(1)} %get-tuple-element.13), channel_id=1, replica_groups=mesh['blk_0'=4,'blk_1'=4,'blk_2'=4,'blk_3'=2] {'blk_2'}, use_global_device_ids=true, to_apply=%region_24.25 | all-reduce | flops 256 | bytes 2048 | tf_op jit(solution)/shard_map/psum | solution.py:23
  363.5 7.8 %all-reduce.6 = (f32[128]{0:T(128)S(1)}, f32[128]{0:T(128)S(1)}) all-reduce(f32[128]{0:T(128)S(1)} %get-tuple-element.8, f32[128]{0:T(128)S(1)} %get-tuple-element.9), channel_id=1, replica_groups=mesh['blk_0'=4,'blk_1'=4,'blk_2'=4,'blk_3'=2] {'blk_3'}, use_global_device_ids=true, to_apply=%region_25.26 | all-reduce | flops 256 | bytes 2048 | tf_op jit(solution)/shard_map/psum | solution.py:23
  371.4 3.0 add_convert_fusion.1
  (105 shorter events, 0.8 us)
Async XLA Ops:
  0.6 25.9 %copy-start.2 = (bf16[4096,128]{1,0:T(8,128)(2,1)S(1)}, bf16[4096,128]{1,0:T(8,128)(2,1)}, u32[]{:S(2)}) copy-start(bf16[4096,128]{1,0:T(8,128)(2,1)} %param.15) | copy-start | bytes 3145732
  5.5 37.6 %collective-permute-start.5 = (bf16[256,128]{1,0:T(8,128)(2,1)S(1)}, bf16[256,128]{1,0:T(8,128)(2,1)S(1)}, u32[]{:S(2)}, u32[]{:S(2)}) collective-permute-start(bf16[256,128]{1,0:T(8,128)(2,1)S(1)} %get-tuple-element.46), channel_id=1, source_target_pairs={{16,0},{17,1},{18,2},{19,3},{20,4},{21,5},{22,6},{23,7},{24,8},{25... | collective-permute-start | bytes 196616 | tf_op jit(solution)/shard_map/ppermute | solution.py:19
  11.6 31.5 %collective-permute-start.4 = (bf16[256,128]{1,0:T(8,128)(2,1)S(1)}, bf16[256,128]{1,0:T(8,128)(2,1)S(1)}, u32[]{:S(2)}, u32[]{:S(2)}) collective-permute-start(bf16[256,128]{1,0:T(8,128)(2,1)S(1)} %get-tuple-element.47), channel_id=1, source_target_pairs={{112,0},{113,1},{114,2},{115,3},{116,4},{117,5},{118,6},{119,7},{1... | collective-permute-start | bytes 196616 | tf_op jit(solution)/shard_map/ppermute | solution.py:19
  11.6 31.4 %collective-permute-start.3 = (bf16[256,128]{1,0:T(8,128)(2,1)S(1)}, bf16[256,128]{1,0:T(8,128)(2,1)S(1)}, u32[]{:S(2)}, u32[]{:S(2)}) collective-permute-start(bf16[256,128]{1,0:T(8,128)(2,1)S(1)} %get-tuple-element.48), channel_id=1, source_target_pairs={{4,0},{5,1},{6,2},{7,3},{8,4},{9,5},{10,6},{11,7},{12,8},{13,9},{1... | collective-permute-start | bytes 196616 | tf_op jit(solution)/shard_map/ppermute | solution.py:19
  19.7 23.3 %collective-permute-start.2 = (bf16[256,128]{1,0:T(8,128)(2,1)S(1)}, bf16[256,128]{1,0:T(8,128)(2,1)S(1)}, u32[]{:S(2)}, u32[]{:S(2)}) collective-permute-start(bf16[256,128]{1,0:T(8,128)(2,1)S(1)} %get-tuple-element.49), channel_id=1, source_target_pairs={{124,0},{125,1},{126,2},{127,3},{0,4},{1,5},{2,6},{3,7},{4,8},{5,9... | collective-permute-start | bytes 196616 | tf_op jit(solution)/shard_map/ppermute | solution.py:19
  19.7 19.3 %collective-permute-start = (bf16[256,128]{1,0:T(8,128)(2,1)S(1)}, bf16[256,128]{1,0:T(8,128)(2,1)S(1)}, u32[]{:S(2)}, u32[]{:S(2)}) collective-permute-start(bf16[256,128]{1,0:T(8,128)(2,1)S(1)} %get-tuple-element.51), channel_id=1, source_target_pairs={{127,0},{0,1},{1,2},{2,3},{3,4},{4,5},{5,6},{6,7},{7,8},{8,9},{9,1... | collective-permute-start | bytes 196616 | tf_op jit(solution)/shard_map/ppermute | solution.py:19
  34.4 3.5 copy-start.8
  34.4 3.5 copy-start.9
  34.4 4.0 %copy-start.10 = (f32[2,128]{1,0:T(2,128)S(1)}, f32[2,128]{1,0:T(2,128)}, u32[]{:S(2)}) copy-start(f32[2,128]{1,0:T(2,128)} %param.29) | copy-start | bytes 3076
  34.5 4.0 %copy-start.11 = (f32[2,128]{1,0:T(2,128)S(1)}, f32[2,128]{1,0:T(2,128)}, u32[]{:S(2)}) copy-start(f32[2,128]{1,0:T(2,128)} %param.28) | copy-start | bytes 3076
  34.5 4.5 %copy-start.3 = (s32[1,6,256]{2,0,1:T(1,128)S(1)}, s32[1,6,256]{2,0,1:T(1,128)}, u32[]{:S(2)}) copy-start(s32[1,6,256]{2,0,1:T(1,128)} %param.19) | copy-start | bytes 18436
  39.1 3.9 %collective-permute-start.1 = (bf16[256,128]{1,0:T(8,128)(2,1)S(1)}, bf16[256,128]{1,0:T(8,128)(2,1)S(1)}, u32[]{:S(2)}, u32[]{:S(2)}) collective-permute-start(bf16[256,128]{1,0:T(8,128)(2,1)S(1)} %get-tuple-element.50), channel_id=1, source_target_pairs={{1,0},{2,1},{3,2},{4,3},{5,4},{6,5},{7,6},{8,7},{9,8},{10,9},{11,1... | collective-permute-start | bytes 196616 | tf_op jit(solution)/shard_map/ppermute | solution.py:19
  51.4 8.8 %copy-start.13 = (bf16[2,384,128]{2,1,0:T(8,128)(2,1)S(1)}, bf16[2,384,128]{2,1,0:T(8,128)(2,1)}, u32[]{:S(2)}) copy-start(bf16[2,384,128]{2,1,0:T(8,128)(2,1)} %param.20) | copy-start | bytes 589828
  51.4 8.8 %copy-start.15 = (bf16[2,128,128]{2,1,0:T(8,128)(2,1)S(1)}, bf16[2,128,128]{2,1,0:T(8,128)(2,1)}, u32[]{:S(2)}) copy-start(bf16[2,128,128]{2,1,0:T(8,128)(2,1)} %param.22) | copy-start | bytes 196612
  74.7 10.3 %copy-start.1 = (f32[24576,128]{1,0:T(8,128)S(1)}, f32[24576,128]{1,0:T(8,128)}, u32[]{:S(2)}) copy-start(f32[24576,128]{1,0:T(8,128)} %get-tuple-element.75) | copy-start | bytes 37748740
  111.0 21.2 %collective-permute-start.6 = (bf16[256,128]{1,0:T(8,128)(2,1)S(1)}, bf16[256,128]{1,0:T(8,128)(2,1)S(1)}, u32[]{:S(2)}, u32[]{:S(2)}) collective-permute-start(bf16[256,128]{1,0:T(8,128)(2,1)S(1)} %get-tuple-element.45), channel_id=1, source_target_pairs={{1,0},{2,1},{3,2},{4,3},{5,4},{6,5},{7,6},{8,7},{9,8},{10,9},{11,1... | collective-permute-start | bytes 196616 | tf_op jit(solution)/shard_map/ppermute | solution.py:19
  119.9 34.0 %copy-start.14 = (bf16[2,256,128]{2,1,0:T(8,128)(2,1)S(1)}, bf16[2,256,128]{2,1,0:T(8,128)(2,1)}, u32[]{:S(2)}) copy-start(bf16[2,256,128]{2,1,0:T(8,128)(2,1)} %param.25) | copy-start | bytes 393220
  119.9 34.0 %copy-start.16 = (bf16[2,128,128]{2,1,0:T(8,128)(2,1)S(1)}, bf16[2,128,128]{2,1,0:T(8,128)(2,1)}, u32[]{:S(2)}) copy-start(bf16[2,128,128]{2,1,0:T(8,128)(2,1)} %param.27) | copy-start | bytes 196612
  119.9 21.5 %collective-permute-start.11 = (bf16[256,128]{1,0:T(8,128)(2,1)S(1)}, bf16[256,128]{1,0:T(8,128)(2,1)S(1)}, u32[]{:S(2)}, u32[]{:S(2)}) collective-permute-start(bf16[256,128]{1,0:T(8,128)(2,1)S(1)} %get-tuple-element.40), channel_id=1, source_target_pairs={{112,0},{113,1},{114,2},{115,3},{116,4},{117,5},{118,6},{119,7},{1... | collective-permute-start | bytes 196616 | tf_op jit(solution)/shard_map/ppermute | solution.py:19
  119.9 21.4 %collective-permute-start.10 = (bf16[256,128]{1,0:T(8,128)(2,1)S(1)}, bf16[256,128]{1,0:T(8,128)(2,1)S(1)}, u32[]{:S(2)}, u32[]{:S(2)}) collective-permute-start(bf16[256,128]{1,0:T(8,128)(2,1)S(1)} %get-tuple-element.41), channel_id=1, source_target_pairs={{16,0},{17,1},{18,2},{19,3},{20,4},{21,5},{22,6},{23,7},{24,8},{25... | collective-permute-start | bytes 196616 | tf_op jit(solution)/shard_map/ppermute | solution.py:19
  125.0 16.3 %collective-permute-start.9 = (bf16[256,128]{1,0:T(8,128)(2,1)S(1)}, bf16[256,128]{1,0:T(8,128)(2,1)S(1)}, u32[]{:S(2)}, u32[]{:S(2)}) collective-permute-start(bf16[256,128]{1,0:T(8,128)(2,1)S(1)} %get-tuple-element.42), channel_id=1, source_target_pairs={{124,0},{125,1},{126,2},{127,3},{0,4},{1,5},{2,6},{3,7},{4,8},{5,9... | collective-permute-start | bytes 196616 | tf_op jit(solution)/shard_map/ppermute | solution.py:19
  125.0 16.3 %collective-permute-start.8 = (bf16[256,128]{1,0:T(8,128)(2,1)S(1)}, bf16[256,128]{1,0:T(8,128)(2,1)S(1)}, u32[]{:S(2)}, u32[]{:S(2)}) collective-permute-start(bf16[256,128]{1,0:T(8,128)(2,1)S(1)} %get-tuple-element.43), channel_id=1, source_target_pairs={{4,0},{5,1},{6,2},{7,3},{8,4},{9,5},{10,6},{11,7},{12,8},{13,9},{1... | collective-permute-start | bytes 196616 | tf_op jit(solution)/shard_map/ppermute | solution.py:19
  132.2 9.1 %collective-permute-start.7 = (bf16[256,128]{1,0:T(8,128)(2,1)S(1)}, bf16[256,128]{1,0:T(8,128)(2,1)S(1)}, u32[]{:S(2)}, u32[]{:S(2)}) collective-permute-start(bf16[256,128]{1,0:T(8,128)(2,1)S(1)} %get-tuple-element.44), channel_id=1, source_target_pairs={{127,0},{0,1},{1,2},{2,3},{3,4},{4,5},{5,6},{6,7},{7,8},{8,9},{9,1... | collective-permute-start | bytes 196616 | tf_op jit(solution)/shard_map/ppermute | solution.py:19
  195.5 22.6 %collective-permute-start.12 = (bf16[256,128]{1,0:T(8,128)(2,1)S(1)}, bf16[256,128]{1,0:T(8,128)(2,1)S(1)}, u32[]{:S(2)}, u32[]{:S(2)}) collective-permute-start(bf16[256,128]{1,0:T(8,128)(2,1)S(1)} %get-tuple-element.39), channel_id=1, source_target_pairs={{127,0},{0,1},{1,2},{2,3},{3,4},{4,5},{5,6},{6,7},{7,8},{8,9},{9,1... | collective-permute-start | bytes 196616 | tf_op jit(solution)/shard_map/ppermute | solution.py:19
  208.9 18.4 %collective-permute-start.17 = (bf16[256,128]{1,0:T(8,128)(2,1)S(1)}, bf16[256,128]{1,0:T(8,128)(2,1)S(1)}, u32[]{:S(2)}, u32[]{:S(2)}) collective-permute-start(bf16[256,128]{1,0:T(8,128)(2,1)S(1)} %get-tuple-element.34), channel_id=1, source_target_pairs={{16,0},{17,1},{18,2},{19,3},{20,4},{21,5},{22,6},{23,7},{24,8},{25... | collective-permute-start | bytes 196616 | tf_op jit(solution)/shard_map/ppermute | solution.py:19
  211.3 16.0 %collective-permute-start.16 = (bf16[256,128]{1,0:T(8,128)(2,1)S(1)}, bf16[256,128]{1,0:T(8,128)(2,1)S(1)}, u32[]{:S(2)}, u32[]{:S(2)}) collective-permute-start(bf16[256,128]{1,0:T(8,128)(2,1)S(1)} %get-tuple-element.35), channel_id=1, source_target_pairs={{112,0},{113,1},{114,2},{115,3},{116,4},{117,5},{118,6},{119,7},{1... | collective-permute-start | bytes 196616 | tf_op jit(solution)/shard_map/ppermute | solution.py:19
  211.9 15.3 %collective-permute-start.15 = (bf16[256,128]{1,0:T(8,128)(2,1)S(1)}, bf16[256,128]{1,0:T(8,128)(2,1)S(1)}, u32[]{:S(2)}, u32[]{:S(2)}) collective-permute-start(bf16[256,128]{1,0:T(8,128)(2,1)S(1)} %get-tuple-element.36), channel_id=1, source_target_pairs={{4,0},{5,1},{6,2},{7,3},{8,4},{9,5},{10,6},{11,7},{12,8},{13,9},{1... | collective-permute-start | bytes 196616 | tf_op jit(solution)/shard_map/ppermute | solution.py:19
  218.1 9.1 %collective-permute-start.14 = (bf16[256,128]{1,0:T(8,128)(2,1)S(1)}, bf16[256,128]{1,0:T(8,128)(2,1)S(1)}, u32[]{:S(2)}, u32[]{:S(2)}) collective-permute-start(bf16[256,128]{1,0:T(8,128)(2,1)S(1)} %get-tuple-element.37), channel_id=1, source_target_pairs={{124,0},{125,1},{126,2},{127,3},{0,4},{1,5},{2,6},{3,7},{4,8},{5,9... | collective-permute-start | bytes 196616 | tf_op jit(solution)/shard_map/ppermute | solution.py:19
  218.1 4.0 %collective-permute-start.13 = (bf16[256,128]{1,0:T(8,128)(2,1)S(1)}, bf16[256,128]{1,0:T(8,128)(2,1)S(1)}, u32[]{:S(2)}, u32[]{:S(2)}) collective-permute-start(bf16[256,128]{1,0:T(8,128)(2,1)S(1)} %get-tuple-element.38), channel_id=1, source_target_pairs={{1,0},{2,1},{3,2},{4,3},{5,4},{6,5},{7,6},{8,7},{9,8},{10,9},{11,1... | collective-permute-start | bytes 196616 | tf_op jit(solution)/shard_map/ppermute | solution.py:19
  258.9 10.7 %copy-start = (f32[24576,128]{1,0:T(8,128)S(1)}, f32[24576,128]{1,0:T(8,128)}, u32[]{:S(2)}) copy-start(f32[24576,128]{1,0:T(8,128)} %get-tuple-element.78) | copy-start | bytes 37748740
  258.9 10.7 %copy-start.6 = (f32[128]{0:T(128)S(1)}, f32[128]{0:T(128)}, u32[]{:S(2)}) copy-start(f32[128]{0:T(128)} %get-tuple-element.64) | copy-start | bytes 1540
  258.9 10.7 %copy-start.7 = (f32[128]{0:T(128)S(1)}, f32[128]{0:T(128)}, u32[]{:S(2)}) copy-start(f32[128]{0:T(128)} %get-tuple-element.80) | copy-start | bytes 1540
  295.7 17.7 %collective-permute-start.18 = (bf16[256,128]{1,0:T(8,128)(2,1)S(1)}, bf16[256,128]{1,0:T(8,128)(2,1)S(1)}, u32[]{:S(2)}, u32[]{:S(2)}) collective-permute-start(bf16[256,128]{1,0:T(8,128)(2,1)S(1)} %get-tuple-element.33), channel_id=1, source_target_pairs={{1,0},{2,1},{3,2},{4,3},{5,4},{6,5},{7,6},{8,7},{9,8},{10,9},{11,1... | collective-permute-start | bytes 196616 | tf_op jit(solution)/shard_map/ppermute | solution.py:19
  301.1 34.0 %copy-start.12 = (f32[128]{0:T(128)S(1)}, f32[128]{0:T(128)}, u32[]{:S(2)}) copy-start(f32[128]{0:T(128)} %get-tuple-element.62) | copy-start | bytes 1540
  301.1 21.4 %collective-permute-start.23 = (bf16[256,128]{1,0:T(8,128)(2,1)S(1)}, bf16[256,128]{1,0:T(8,128)(2,1)S(1)}, u32[]{:S(2)}, u32[]{:S(2)}) collective-permute-start(bf16[256,128]{1,0:T(8,128)(2,1)S(1)} %get-tuple-element.28), channel_id=1, source_target_pairs={{112,0},{113,1},{114,2},{115,3},{116,4},{117,5},{118,6},{119,7},{1... | collective-permute-start | bytes 196616 | tf_op jit(solution)/shard_map/ppermute | solution.py:19
  301.1 21.4 %collective-permute-start.22 = (bf16[256,128]{1,0:T(8,128)(2,1)S(1)}, bf16[256,128]{1,0:T(8,128)(2,1)S(1)}, u32[]{:S(2)}, u32[]{:S(2)}) collective-permute-start(bf16[256,128]{1,0:T(8,128)(2,1)S(1)} %get-tuple-element.29), channel_id=1, source_target_pairs={{16,0},{17,1},{18,2},{19,3},{20,4},{21,5},{22,6},{23,7},{24,8},{25... | collective-permute-start | bytes 196616 | tf_op jit(solution)/shard_map/ppermute | solution.py:19
  306.2 16.3 %collective-permute-start.21 = (bf16[256,128]{1,0:T(8,128)(2,1)S(1)}, bf16[256,128]{1,0:T(8,128)(2,1)S(1)}, u32[]{:S(2)}, u32[]{:S(2)}) collective-permute-start(bf16[256,128]{1,0:T(8,128)(2,1)S(1)} %get-tuple-element.30), channel_id=1, source_target_pairs={{124,0},{125,1},{126,2},{127,3},{0,4},{1,5},{2,6},{3,7},{4,8},{5,9... | collective-permute-start | bytes 196616 | tf_op jit(solution)/shard_map/ppermute | solution.py:19
  306.2 16.3 %collective-permute-start.20 = (bf16[256,128]{1,0:T(8,128)(2,1)S(1)}, bf16[256,128]{1,0:T(8,128)(2,1)S(1)}, u32[]{:S(2)}, u32[]{:S(2)}) collective-permute-start(bf16[256,128]{1,0:T(8,128)(2,1)S(1)} %get-tuple-element.31), channel_id=1, source_target_pairs={{4,0},{5,1},{6,2},{7,3},{8,4},{9,5},{10,6},{11,7},{12,8},{13,9},{1... | collective-permute-start | bytes 196616 | tf_op jit(solution)/shard_map/ppermute | solution.py:19
  313.4 9.1 %collective-permute-start.19 = (bf16[256,128]{1,0:T(8,128)(2,1)S(1)}, bf16[256,128]{1,0:T(8,128)(2,1)S(1)}, u32[]{:S(2)}, u32[]{:S(2)}) collective-permute-start(bf16[256,128]{1,0:T(8,128)(2,1)S(1)} %get-tuple-element.32), channel_id=1, source_target_pairs={{127,0},{0,1},{1,2},{2,3},{3,4},{4,5},{5,6},{6,7},{7,8},{8,9},{9,1... | collective-permute-start | bytes 196616 | tf_op jit(solution)/shard_map/ppermute | solution.py:19
  322.5 48.8 %copy-start.4 = (f32[128]{0:T(128)S(1)}, f32[128]{0:T(128)}, u32[]{:S(2)}) copy-start(f32[128]{0:T(128)} %get-tuple-element.60) | copy-start | bytes 1540
  322.5 48.8 %copy-start.5 = (f32[128]{0:T(128)S(1)}, f32[128]{0:T(128)}, u32[]{:S(2)}) copy-start(f32[128]{0:T(128)} %get-tuple-element.83) | copy-start | bytes 1540
where the time goes:
time: 381 us; the launch traced here: 375 us
  matrix products  106 us (28%)
  other arithmetic  97.5 us (26%)
  blocking collectives  67.3 us (18%)
  starting transfers between devices  61 us (16%)
  waiting for transfers between devices  29.5 us (8%)
  local copies, waits for them, and re-layouts  12.4 us (3%)
    psum x8, blocking collectives, over_axes(): return functools.reduce(lax.psum, axes, shard)  67.3 us
    ppermute x24, starting transfers between devices, passed_along(): return lax.ppermute(block, axis, route)  61 us
    convert_element_type x2, other arithmetic, per_device(): message = (owned * edges_new.astype(jnp.float32)).astype(jnp.bfloat16).re...  44.4 us
    dot_general x4, matrix products, select_rows(): jnp.einsum('bkeh,khc->bkec', halo_hot, halo_view, preferred_element_type=...  34.1 us
    ppermute x24, waiting for transfers between devices, passed_along(): return lax.ppermute(block, axis, route)  29.5 us
    dot_general x2, matrix products, per_device(): jnp.dot(hidden, edge_w2[layer_id], preferred_element_type=jnp.float32)  28.9 us
    dot_general x4, matrix products, select_rows(): jnp.einsum('bken,bnc->bkec', own_hot, own_view, preferred_element_type=jn...  22.5 us
    scatter-add x2, other arithmetic, per_device(): node_sums = own_sums.at[flat_faces].add(jnp.concatenate(returned, axis=0))  21.7 us
  transfers between devices with their start and end apart: 24, of which 5 were waited for; matrix products, arithmetic and copies ran while one was open for 10% of the time, Pallas kernels for 0%

commit v1 on v0

v1 whole, which is shorter than its diff:
```python
import functools

import jax
import jax.numpy as jnp
from jax import lax
from jax.experimental import pallas as pl
from jax.experimental.pallas import tpu as pltpu
from jax.sharding import PartitionSpec as P

LAYERS = 2
FACES = 6
OFFSETS = (1, -1, 4, -4, 16, -16)
C = 128
NODES = 4096
HALO = 256
TILE = 128
EDGES = 24576
GROUPS = NODES // TILE
GSTEP = 2
GE = FACES * TILE
SE = GSTEP * GE
STEPS = GROUPS // GSTEP
NB = 256
BF = jnp.bfloat16
F32 = jnp.float32
FAR = -1000.0


def hot_rows(row, rows):
    n = row.shape[1]
    index = jnp.broadcast_to(row, (16, n)).astype(BF)[None]
    counter = lax.broadcasted_iota(jnp.int32, (rows, n), 0).astype(F32).astype(BF)
    counter = counter.reshape(rows // 16, 16, n)
    hot = jnp.where(counter == index, jnp.ones((), BF), jnp.zeros((), BF))
    return hot.reshape(rows, n)


def dot(a, b):
    return jnp.dot(a, b, preferred_element_type=F32)


def dot_nt(a, b):
    return lax.dot_general(a, b, (((1,), (1,)), ((), ())), preferred_element_type=F32)


def edge_kernel(moved, *refs):
    refs = list(refs)
    h_ref = refs.pop(0)
    if moved:
        upd_ref, scale_row, scale_col = refs.pop(0), refs.pop(0), refs.pop(0)
    halo = [refs.pop(0) for _ in range(FACES)]
    if moved:
        halo_upd = [refs.pop(0) for _ in range(FACES)]
    e_ref, idx_ref, wsr_ref, b_ref, we_ref, w2_ref, gain_ref, shift_ref = refs[:8]
    refs = refs[8:]
    if moved:
        h_out = refs.pop(0)
    e_out, own_out = refs.pop(0), refs.pop(0)
    halo_out = [refs.pop(0) for _ in range(FACES)]
    tab_ref, acc_ref = refs
    step = pl.program_id(0)

    @pl.when(step == 0)
    def _():
        acc_ref[...] = jnp.zeros_like(acc_ref)
        for k in range(FACES):
            ht = halo[k][...]
            if moved:
                a, b = scale_col[0], scale_col[1]
                a2 = jnp.concatenate([a, a], axis=1)
                b2 = jnp.concatenate([b, b], axis=1)
                ht = (ht.astype(F32) + halo_upd[k][...].astype(F32) * a2 + b2).astype(BF)
            t = dot(wsr_ref[...], ht)
            bias = jnp.concatenate([b_ref[...], b_ref[...]], axis=1)
            tab_ref[k, :, 0:HALO] = (t[0:C] + bias).astype(BF)
            tab_ref[k, :, HALO : 2 * HALO] = t[C : 2 * C].astype(BF)

    pre_own = []
    r_own = []
    e_t = []
    for g in range(GSTEP):
        hg = h_ref[g * TILE : (g + 1) * TILE, :]
        if moved:
            up = upd_ref[g * TILE : (g + 1) * TILE, :]
            hg = (hg.astype(F32) + up * scale_row[0:1, :] + scale_row[1:2, :]).astype(BF)
            h_out[g * TILE : (g + 1) * TILE, :] = hg
        t = dot_nt(wsr_ref[...], hg)
        ps = (t[0:C] + b_ref[...]).astype(BF)
        pr = t[C : 2 * C].astype(BF)
        lhs = jnp.concatenate([ps, pr, we_ref[...]], axis=1)
        lanes = slice(g * GE, (g + 1) * GE)
        if moved:
            et = e_ref[:, lanes]
        else:
            et = e_ref[lanes, :].T
        e_t.append(et)
        s_hot = hot_rows(idx_ref[0:1, lanes], TILE)
        r_hot = hot_rows(idx_ref[1:2, lanes], TILE)
        r_own.append(r_hot)
        pre_own.append(dot(lhs, jnp.concatenate([s_hot, r_hot, et], axis=0)))
    new = [[None] * FACES for _ in range(GSTEP)]
    for k in range(FACES):
        pieces = [slice(g * GE + k * TILE, g * GE + (k + 1) * TILE) for g in range(GSTEP)]
        s_row = jnp.concatenate([idx_ref[2:3, p] for p in pieces], axis=1)
        r_row = jnp.concatenate([idx_ref[3:4, p] for p in pieces], axis=1)
        own_row = jnp.concatenate([idx_ref[4:5, p] for p in pieces], axis=1)
        s_hot = hot_rows(s_row, HALO)
        r_hot = hot_rows(r_row, HALO)
        pre = dot(tab_ref[k], jnp.concatenate([s_hot, r_hot], axis=0))
        cut = slice(k * TILE, (k + 1) * TILE)
        pre = pre + jnp.concatenate([pre_own[g][:, cut] for g in range(GSTEP)], axis=1)
        hidden = jnp.maximum(pre, 0.0).astype(BF)
        z = dot(w2_ref[...], hidden)
        spread = jnp.sum(z * z, axis=0, keepdims=True) * (1.0 / C)
        rs = lax.rsqrt(spread + 1e-05)
        gain = jnp.concatenate([gain_ref[...]] * GSTEP, axis=1)
        shift = jnp.concatenate([shift_ref[...]] * GSTEP, axis=1)
        old = jnp.concatenate([e_t[g][:, cut] for g in range(GSTEP)], axis=1)
        value = old.astype(F32) + (z * gain) * (rs * own_row) + shift * own_row
        fresh = value.astype(BF)
        acc_ref[k] = acc_ref[k] + dot_nt(r_hot, fresh)
        for g in range(GSTEP):
            new[g][k] = fresh[:, g * TILE : (g + 1) * TILE]
    for g in range(GSTEP):
        lanes = slice(g * GE, (g + 1) * GE)
        whole = jnp.concatenate(new[g], axis=1)
        if moved:
            e_out[lanes, :] = whole.T
        else:
            e_out[:, lanes] = whole
        own_out[g * TILE : (g + 1) * TILE, :] = dot_nt(r_own[g], whole)

    @pl.when(step == STEPS - 1)
    def _():
        for k in range(FACES):
            halo_out[k][...] = acc_ref[k].astype(BF)


def full(shape):
    zeros = (0,) * len(shape)
    return pl.BlockSpec(shape, lambda i: zeros)


def edge_layer(moved, h, extra, halos, halo_upds, e, idx, weights):
    rows = pl.BlockSpec((GSTEP * TILE, C), lambda i: (i, 0))
    by_edge = pl.BlockSpec((SE, C), lambda i: (i, 0))
    by_lane = pl.BlockSpec((C, SE), lambda i: (0, i))
    args, specs = [h], [rows]
    if moved:
        upd, scale_row, scale_col = extra
        args += [upd, scale_row, scale_col]
        specs += [rows, full(scale_row.shape), full(scale_col.shape)]
    args += list(halos)
    specs += [full((C, HALO))] * FACES
    if moved:
        args += list(halo_upds)
        specs += [full((C, HALO))] * FACES
    args += [e, idx] + list(weights)
    specs += [by_lane if moved else by_edge, pl.BlockSpec((8, SE), lambda i: (0, i))]
    specs += [full(w.shape) for w in weights]
    outs, out_specs = [], []
    if moved:
        outs.append(jax.ShapeDtypeStruct((NODES, C), BF))
        out_specs.append(rows)
    outs.append(jax.ShapeDtypeStruct((EDGES, C) if moved else (C, EDGES), BF))
    out_specs.append(by_edge if moved else by_lane)
    outs.append(jax.ShapeDtypeStruct((NODES, C), F32))
    out_specs.append(rows)
    outs += [jax.ShapeDtypeStruct((HALO, C), BF)] * FACES
    out_specs += [full((HALO, C))] * FACES
    return pl.pallas_call(
        functools.partial(edge_kernel, moved),
        grid=(STEPS,),
        in_specs=specs,
        out_specs=out_specs,
        out_shape=outs,
        scratch_shapes=[
            pltpu.VMEM((FACES, C, 2 * HALO), BF),
            pltpu.VMEM((FACES, HALO, C), F32),
        ],
        name="edges",
    )(*args)


def node_kernel(send, *refs):
    refs = list(refs)
    h_ref, own_ref = refs.pop(0), refs.pop(0)
    ret = [refs.pop(0) for _ in range(FACES)]
    sidx_ref, w1_ref, b1_ref, w2_ref = refs[:4]
    upd_ref, stat_ref = refs[4], refs[5]
    sent = refs[6 : 6 + FACES] if send else None
    acc_ref = refs[6 + FACES] if send else None
    step = pl.program_id(0)

    @pl.when(step == 0)
    def _():
        stat_ref[...] = jnp.zeros_like(stat_ref)
        if send:
            acc_ref[...] = jnp.zeros_like(acc_ref)

    base = (step * NB).astype(F32)
    hots = [hot_rows(sidx_ref[k : k + 1, :] - base, NB) for k in range(FACES)]
    hot = jnp.concatenate(hots, axis=1)
    arrived = jnp.concatenate([r[...] for r in ret], axis=0)
    total = (own_ref[...] + dot(hot, arrived)).astype(BF)
    node_in = jnp.concatenate([h_ref[...], total], axis=1)
    hidden = jnp.maximum(dot(node_in, w1_ref[...]) + b1_ref[...], 0.0).astype(BF)
    update = dot(hidden, w2_ref[...])
    upd_ref[...] = update
    stat_ref[0:1, :] += jnp.sum(update, axis=0, keepdims=True)
    stat_ref[1:2, :] += jnp.sum(update * update, axis=0, keepdims=True)
    if send:
        ut = update.astype(BF).T
        for k in range(FACES):
            acc_ref[k] = acc_ref[k] + dot(ut, hots[k])

        @pl.when(step == NODES // NB - 1)
        def _():
            for k in range(FACES):
                sent[k][...] = acc_ref[k].astype(BF)


def node_layer(send, h, own, returned, sidx, weights):
    rows = pl.BlockSpec((NB, C), lambda i: (i, 0))
    outs = [jax.ShapeDtypeStruct((NODES, C), F32), jax.ShapeDtypeStruct((2, C), F32)]
    out_specs = [rows, full((2, C))]
    scratch = []
    if send:
        outs += [jax.ShapeDtypeStruct((C, HALO), BF)] * FACES
        out_specs += [full((C, HALO))] * FACES
        scratch = [pltpu.VMEM((FACES, C, HALO), F32)]
    return pl.pallas_call(
        functools.partial(node_kernel, send),
        grid=(NODES // NB,),
        in_specs=[rows, rows]
        + [full((HALO, C))] * FACES
        + [full(sidx.shape)]
        + [full(w.shape) for w in weights],
        out_specs=out_specs,
        out_shape=outs,
        scratch_shapes=scratch,
        name="nodes",
    )(h, own, *returned, sidx, *weights)


def pass_along(block, distance):
    n = lax.axis_size("blk")
    return lax.ppermute(block, "blk", [((i - distance) % n, i) for i in range(n)])


def total_over(stats):
    n = lax.axis_size("blk")
    parts = lax.all_to_all(jnp.broadcast_to(stats[None], (n,) + stats.shape), "blk", 0, 0)
    return jnp.sum(parts, axis=0)


def per_device(
    node_latent,
    edge_latent,
    edge_ends,
    edge_owned,
    send_index,
    edge_w1,
    edge_b1,
    edge_w2,
    edge_gain,
    edge_shift,
    node_w1,
    node_b1,
    node_w2,
    node_gain,
    node_shift,
):
    total_nodes = NODES * lax.axis_size("blk")
    faces = send_index[0]
    tile = jnp.arange(EDGES, dtype=jnp.int32) // TILE
    own_base = tile // FACES * TILE
    halo_base = NODES + tile % FACES * HALO
    owned = edge_owned > 0
    far = jnp.full((), FAR, F32)
    idx = jnp.stack(
        [
            (edge_ends[0] - own_base).astype(F32),
            jnp.where(owned, (edge_ends[1] - own_base).astype(F32), far),
            (edge_ends[0] - halo_base).astype(F32),
            jnp.where(owned, (edge_ends[1] - halo_base).astype(F32), far),
            edge_owned.astype(F32),
        ]
        + [jnp.zeros((EDGES,), F32)] * 3
    )
    sidx = faces.astype(F32)
    h = node_latent
    e = edge_latent
    rows = node_latent[faces.reshape(-1)].T
    halos = [
        pass_along(rows[:, k * HALO : (k + 1) * HALO], OFFSETS[k]) for k in range(FACES)
    ]
    extra = None
    halo_upds = None
    for layer in range(LAYERS):
        w1 = edge_w1[layer]
        w2 = edge_w2[layer].astype(F32)
        w2 = (w2 - jnp.mean(w2, axis=1, keepdims=True)).astype(BF).T
        wsr = jnp.concatenate([w1[C : 2 * C], w1[2 * C : 3 * C]], axis=1).T
        lanes = lambda v: jnp.broadcast_to(v[:, None], (C, C))
        weights = [
            wsr,
            lanes(edge_b1[layer]),
            w1[0:C].T,
            w2,
            lanes(edge_gain[layer]),
            lanes(edge_shift[layer]),
        ]
        moved = layer > 0
        outs = edge_layer(moved, h, extra, halos, halo_upds, e, idx, weights)
        if moved:
            h, outs = outs[0], outs[1:]
        e, own = outs[0], outs[1]
        returned = [pass_along(outs[2 + k], -OFFSETS[k]) for k in range(FACES)]
        node_weights = [node_w1[layer], node_b1[layer][None], node_w2[layer]]
        last = layer == LAYERS - 1
        outs = node_layer(not last, h, own, returned, sidx, node_weights)
        update, stats = outs[0], outs[1]
        if not last:
            halo_upds = [pass_along(outs[2 + k], OFFSETS[k]) for k in range(FACES)]
        totals = total_over(stats) / total_nodes
        mu = totals[0]
        var = jnp.maximum(totals[1] - mu * mu, 0.0)
        a = node_gain[layer] * lax.rsqrt(var + 1e-05)
        b = node_shift[layer] - a * mu
        if not last:
            extra = (update, jnp.stack([a, b]), jnp.stack([lanes(a), lanes(b)]))
    out = (h.astype(F32) + update * a + b).astype(BF)
    return (out, e)


def solution(mesh):
    shared = P()
    return jax.shard_map(
        per_device,
        mesh=mesh,
        in_specs=(
            P("blk", None),
            P("blk", None),
            P(None, "blk"),
            P("blk"),
            P("blk", None, None),
        )
        + (shared,) * 10,
        out_specs=(P("blk", None), P("blk", None)),
        check_vma=False,
    )
```

time: 381 us -> 260 us (0.68); the launches traced: 375 us -> 259 us
  Pallas kernels: 0 us -> 122 us
  matrix products: 106 us -> 0 us
  other arithmetic: 97.5 us -> 9.01 us
  blocking collectives: 67.3 us -> 17.1 us
  starting transfers between devices: 61 us -> 74.1 us
  waiting for transfers between devices: 29.5 us -> 18 us
  local copies, waits for them, and re-layouts: 12.4 us -> 18.1 us
    pallas_call x0 -> x4, Pallas kernels: none -> 122 us  [the longest x2 89.8 us: edge_layer(): pl.pallas_call(functools.partial(edge_kernel, moved), grid=(STEPS,), in_s...]
    dot_general x16 -> x0, matrix products: 106 us -> none  [the longest x4 34.1 us: select_rows(): jnp.einsum('bkeh,khc->bkec', halo_hot, halo_view, preferred_element_type=...]
    psum x8 -> x0, blocking collectives: 67.3 us -> none  [over_axes(): return functools.reduce(lax.psum, axes, shard)]
    convert_element_type x7 -> x4, other arithmetic: 53.8 us -> 4.05 us  [the longest x1 2.9 us: per_device(): out = (h.astype(F32) + update * a + b).astype(BF)]
    scatter-add x2 -> x0, other arithmetic: 21.7 us -> none  [per_device(): node_sums = own_sums.at[flat_faces].add(jnp.concatenate(returned, axis=0))]
    reduce_sum x2 -> x4, other arithmetic: 21 us -> 0.36 us  [the longest x2 0.29 us: total_over(): return jnp.sum(parts, axis=0)]
    all_to_all x0 -> x1, blocking collectives: none -> 17.1 us  [total_over(): lax.all_to_all(jnp.broadcast_to(stats[None], (n,) + stats.shape), 'blk',...]
    all_to_all x0 -> x1, starting transfers between devices: none -> 12.4 us  [total_over(): lax.all_to_all(jnp.broadcast_to(stats[None], (n,) + stats.shape), 'blk',...]
  transfers between devices with their start and end apart: 24 -> 25, of which waited for: 5 -> 7; matrix products, arithmetic and copies ran while one was open for 10% -> 4% of each run, Pallas kernels for 0% -> 0%
where the time goes in v1:
time: 260 us; the launch traced here: 259 us
  Pallas kernels  122 us (47%)
  starting transfers between devices  74.1 us (28%)
  local copies, waits for them, and re-layouts  18.1 us (7%)
  waiting for transfers between devices  18 us (7%)
  blocking collectives  17.1 us (7%)
  other arithmetic  9.01 us (3%)
    pallas_call x2, Pallas kernels, edge_layer(): pl.pallas_call(functools.partial(edge_kernel, moved), grid=(STEPS,), in_s...  89.8 us
    ppermute x24, starting transfers between devices, pass_along(): lax.ppermute(block, 'blk', [((i - distance) % n, i) for i in range(n)])  61.7 us
    pallas_call x2, Pallas kernels, node_layer(): pl.pallas_call(functools.partial(node_kernel, send), grid=(NODES // NB,),...  32.2 us
    ppermute x24, waiting for transfers between devices, pass_along(): lax.ppermute(block, 'blk', [((i - distance) % n, i) for i in range(n)])  18 us
    all_to_all x1, blocking collectives, total_over(): lax.all_to_all(jnp.broadcast_to(stats[None], (n,) + stats.shape), 'blk',...  17.1 us
    all_to_all x1, starting transfers between devices, total_over(): lax.all_to_all(jnp.broadcast_to(stats[None], (n,) + stats.shape), 'blk',...  12.4 us
  transfers between devices with their start and end apart: 25, of which 7 were waited for; matrix products, arithmetic and copies ran while one was open for 4% of the time, Pallas kernels for 0%

profile of v1, /device:TPU:1, one launch (start us, length us, event | category | flops | bytes accessed | tf_op | source)
XLA Modules:
  0.0 259.4 jit_solution(7678504027510636288)
XLA Ops:
  0.6 0.7 fusion.31
  1.5 4.1 %gather_fusion = bf16[1536,128]{1,0:T(8,128)(2,1)S(1)} fusion(bf16[4096,128]{1,0:T(8,128)(2,1)} %refs_0_.5, s32[2048]{0:T(1024)S(1)} %pad_clamp_fusion), kind=kCustom, calls=%fused_computation | custom fusion | bytes 792576 | tf_op jit(solution)/shard_map/gather | solution.py:294
  5.6 0.2 copy.37
  5.8 6.1 %collective-permute-start.5 = (bf16[128,256]{1,0:T(8,128)(2,1)S(1)}, bf16[128,256]{1,0:T(8,128)(2,1)S(1)}, u32[]{:S(2)}, u32[]{:S(2)}) collective-permute-start(bf16[128,256]{1,0:T(8,128)(2,1)S(1)} %get-tuple-element.64), channel_id=1, source_target_pairs={{16,0},{17,1},{18,2},{19,3},{20,4},{21,5},{22,6},{23,7},{24,8},{25... | collective-permute-start | bytes 196616 | tf_op jit(solution)/shard_map/ppermute | solution.py:248
  11.9 8.1 %collective-permute-start.3 = (bf16[128,256]{1,0:T(8,128)(2,1)S(1)}, bf16[128,256]{1,0:T(8,128)(2,1)S(1)}, u32[]{:S(2)}, u32[]{:S(2)}) collective-permute-start(bf16[128,256]{1,0:T(8,128)(2,1)S(1)} %get-tuple-element.66), channel_id=1, source_target_pairs={{4,0},{5,1},{6,2},{7,3},{8,4},{9,5},{10,6},{11,7},{12,8},{13,9},{1... | collective-permute-start | bytes 196616 | tf_op jit(solution)/shard_map/ppermute | solution.py:248
  20.0 1.5 collective-permute-start.1
  21.5 0.6 fusion.30.refs_8_
  22.2 0.1 copy.54
  22.4 0.6 fusion.29.refs_12_
  23.0 0.6 slice_bitcast_fusion.2
  23.6 0.7 slice_bitcast_fusion
  24.3 0.5 fusion.20
  25.0 0.5 fusion.37
  25.6 0.1 copy.58
  25.7 0.7 copy.53
  26.5 0.1 copy.51
  26.8 2.1 stack.29.refs_8_.refs_17_
  28.8 0.6 collective-permute-start
  29.5 0.6 maximum_bitcast_fusion.refs_9_
  30.2 5.6 %collective-permute-done.refs_1_.refs_4_ = bf16[128,256]{1,0:T(8,128)(2,1)S(1)} collective-permute-done((bf16[128,256]{1,0:T(8,128)(2,1)S(1)}, bf16[128,256]{1,0:T(8,128)(2,1)S(1)}, u32[]{:S(2)}, u32[]{:S(2)}) %collective-permute-start) | collective-permute-done | bytes 65568 | tf_op jit(solution)/shard_map/ppermute | solution.py:248
  35.8 0.7 broadcast_in_dim.72.refs_14_
  36.5 0.7 broadcast_in_dim.70.refs_13_
  37.2 0.7 broadcast_in_dim.68.refs_10_
  37.9 44.5 %edges.2 = (bf16[128,24576]{1,0:T(8,128)(2,1)}, f32[4096,128]{1,0:T(8,128)}, bf16[256,128]{1,0:T(8,128)(2,1)}, bf16[256,128]{1,0:T(8,128)(2,1)}, bf16[256,128]{1...) custom-call(bf16[4096,128]{1,0:T(8,128)(2,1)} %refs_0_.5, ...), custom_call_target="tpu_custom_call" | custom-call | tf_op jit(solution)/shard_map/edges/pallas_call | solution.py:171
  82.4 8.4 %collective-permute-start.6 = (bf16[256,128]{1,0:T(8,128)(2,1)}, bf16[256,128]{1,0:T(8,128)(2,1)S(1)}, u32[]{:S(2)}, u32[]{:S(2)}) collective-permute-start(bf16[256,128]{1,0:T(8,128)(2,1)} %get-tuple-element.30), channel_id=1, source_target_pairs={{1,0},{2,1},{3,2},{4,3},{5,4},{6,5},{7,6},{8,7},{9,8},{10,9},{11,1... | collective-permute-start | bytes 196616 | tf_op jit(solution)/shard_map/ppermute | solution.py:248
  91.1 3.0 %collective-permute-start.9 = (bf16[256,128]{1,0:T(8,128)(2,1)}, bf16[256,128]{1,0:T(8,128)(2,1)S(1)}, u32[]{:S(2)}, u32[]{:S(2)}) collective-permute-start(bf16[256,128]{1,0:T(8,128)(2,1)} %get-tuple-element.33), channel_id=1, source_target_pairs={{124,0},{125,1},{126,2},{127,3},{0,4},{1,5},{2,6},{3,7},{4,8},{5,9... | collective-permute-start | bytes 196616 | tf_op jit(solution)/shard_map/ppermute | solution.py:248
  94.0 3.0 %collective-permute-start.11 = (bf16[256,128]{1,0:T(8,128)(2,1)}, bf16[256,128]{1,0:T(8,128)(2,1)S(1)}, u32[]{:S(2)}, u32[]{:S(2)}) collective-permute-start(bf16[256,128]{1,0:T(8,128)(2,1)} %get-tuple-element.35), channel_id=1, source_target_pairs={{112,0},{113,1},{114,2},{115,3},{116,4},{117,5},{118,6},{119,7},{1... | collective-permute-start | bytes 196616 | tf_op jit(solution)/shard_map/ppermute | solution.py:248
  97.0 4.2 %collective-permute-done.9.refs_5_ = bf16[256,128]{1,0:T(8,128)(2,1)S(1)} collective-permute-done((bf16[256,128]{1,0:T(8,128)(2,1)}, bf16[256,128]{1,0:T(8,128)(2,1)S(1)}, u32[]{:S(2)}, u32[]{:S(2)}) %collective-permute-start.9) | collective-permute-done | bytes 65568 | tf_op jit(solution)/shard_map/ppermute | solution.py:248
  101.2 0.1 collective-permute-done.11.refs_7_
  101.3 0.5 copy-done.22
  101.8 0.1 copy-done.27
  101.9 17.6 %nodes.2 = (f32[4096,128]{1,0:T(8,128)}, f32[2,128]{1,0:T(2,128)}, bf16[128,256]{1,0:T(8,128)(2,1)}, bf16[128,256]{1,0:T(8,128)(2,1)}, bf16[128,256]{1,0:T(8,128...) custom-call(bf16[4096,128]{1,0:T(8,128)(2,1)} %refs_0_.5, ...), custom_call_target="tpu_custom_call" | custom-call | tf_op jit(solution)/shard_map/nodes/pallas_call | solution.py:232
  119.6 1.3 broadcast_in_dim.73
  120.9 12.4 %all-to-all-start = ((f32[128,2,128]{2,1,0:T(2,128)}), f32[128,2,128]{2,1,0:T(2,128)S(1)}, u32[]{:S(2)}, u32[]{:S(2)}) async-start(f32[128,2,128]{2,1,0:T(2,128)} %broadcast_in_dim.73), calls=%async_computation | async-start | bytes 262144 | tf_op jit(solution)/shard_map/all_to_all | solution.py:253
  133.3 0.6 fusion.28.refs_21_
  133.9 0.7 copy.57
  134.6 0.1 copy.56
  134.7 0.1 copy.55
  134.8 0.6 maximum_bitcast_fusion.1.refs_18_
  135.5 1.8 collective-permute-start.12
  137.2 2.9 %collective-permute-start.14 = (bf16[128,256]{1,0:T(8,128)(2,1)}, bf16[128,256]{1,0:T(8,128)(2,1)S(1)}, u32[]{:S(2)}, u32[]{:S(2)}) collective-permute-start(bf16[128,256]{1,0:T(8,128)(2,1)} %get-tuple-element.40), channel_id=1, source_target_pairs={{124,0},{125,1},{126,2},{127,3},{0,4},{1,5},{2,6},{3,7},{4,8},{5,9... | collective-permute-start | bytes 196616 | tf_op jit(solution)/shard_map/ppermute | solution.py:248
  140.2 4.5 %collective-permute-start.15 = (bf16[128,256]{1,0:T(8,128)(2,1)}, bf16[128,256]{1,0:T(8,128)(2,1)S(1)}, u32[]{:S(2)}, u32[]{:S(2)}) collective-permute-start(bf16[128,256]{1,0:T(8,128)(2,1)} %get-tuple-element.41), channel_id=1, source_target_pairs={{4,0},{5,1},{6,2},{7,3},{8,4},{9,5},{10,6},{11,7},{12,8},{13,9},{1... | collective-permute-start | bytes 196616 | tf_op jit(solution)/shard_map/ppermute | solution.py:248
  144.6 0.1 reduce_sum.37
  145.0 0.7 pad_maximum_fusion.refs_3_
  145.7 5.1 %collective-permute-start.17 = (bf16[128,256]{1,0:T(8,128)(2,1)}, bf16[128,256]{1,0:T(8,128)(2,1)S(1)}, u32[]{:S(2)}, u32[]{:S(2)}) collective-permute-start(bf16[128,256]{1,0:T(8,128)(2,1)} %get-tuple-element.43), channel_id=1, source_target_pairs={{16,0},{17,1},{18,2},{19,3},{20,4},{21,5},{22,6},{23,7},{24,8},{25... | collective-permute-start | bytes 196616 | tf_op jit(solution)/shard_map/ppermute | solution.py:248
  150.8 0.5 pad_maximum_fusion.1.refs_2_
  151.3 0.3 collective-permute-done.16.refs_14_
  151.6 0.8 collective-permute-done.17.refs_15_
  152.4 0.7 broadcast_in_dim.79.refs_23_
  153.1 0.7 broadcast_in_dim.77.refs_22_
  153.8 0.7 broadcast_in_dim.75.refs_19_
  154.5 45.3 %edges.3 = (bf16[4096,128]{1,0:T(8,128)(2,1)}, bf16[24576,128]{1,0:T(8,128)(2,1)}, f32[4096,128]{1,0:T(8,128)}, bf16[256,128]{1,0:T(8,128)(2,1)}, bf16[256,128]{...) custom-call(bf16[4096,128]{1,0:T(8,128)(2,1)} %refs_0_.5, ...), custom_call_target="tpu_custom_call" | custom-call | tf_op jit(solution)/shard_map/edges/pallas_call | solution.py:171
  199.8 8.0 %collective-permute-start.18 = (bf16[256,128]{1,0:T(8,128)(2,1)}, bf16[256,128]{1,0:T(8,128)(2,1)S(1)}, u32[]{:S(2)}, u32[]{:S(2)}) collective-permute-start(bf16[256,128]{1,0:T(8,128)(2,1)} %get-tuple-element.47), channel_id=1, source_target_pairs={{1,0},{2,1},{3,2},{4,3},{5,4},{6,5},{7,6},{8,7},{9,8},{10,9},{11,1... | collective-permute-start | bytes 196616 | tf_op jit(solution)/shard_map/ppermute | solution.py:248
  207.9 1.7 collective-permute-start.20
  209.6 1.2 collective-permute-start.21
  210.9 5.6 %collective-permute-start.22 = (bf16[256,128]{1,0:T(8,128)(2,1)}, bf16[256,128]{1,0:T(8,128)(2,1)S(1)}, u32[]{:S(2)}, u32[]{:S(2)}) collective-permute-start(bf16[256,128]{1,0:T(8,128)(2,1)} %get-tuple-element.51), channel_id=1, source_target_pairs={{16,0},{17,1},{18,2},{19,3},{20,4},{21,5},{22,6},{23,7},{24,8},{25... | collective-permute-start | bytes 196616 | tf_op jit(solution)/shard_map/ppermute | solution.py:248
  216.5 4.0 %collective-permute-done.21.refs_5_ = bf16[256,128]{1,0:T(8,128)(2,1)S(1)} collective-permute-done((bf16[256,128]{1,0:T(8,128)(2,1)}, bf16[256,128]{1,0:T(8,128)(2,1)S(1)}, u32[]{:S(2)}, u32[]{:S(2)}) %collective-permute-start.21) | collective-permute-done | bytes 65568 | tf_op jit(solution)/shard_map/ppermute | solution.py:248
  220.5 2.8 %collective-permute-done.23.refs_7_ = bf16[256,128]{1,0:T(8,128)(2,1)S(1)} collective-permute-done((bf16[256,128]{1,0:T(8,128)(2,1)}, bf16[256,128]{1,0:T(8,128)(2,1)S(1)}, u32[]{:S(2)}, u32[]{:S(2)}) %collective-permute-start.23) | collective-permute-done | bytes 65568 | tf_op jit(solution)/shard_map/ppermute | solution.py:248
  223.4 0.6 copy-done.28
  224.0 14.6 %nodes.3 = (f32[4096,128]{1,0:T(8,128)}, f32[2,128]{1,0:T(2,128)}) custom-call(bf16[4096,128]{1,0:T(8,128)(2,1)} %get-tuple-element.45.refs_0_, f32[4096,128]{1,0:T(8,128)} %get-tuple-element.46.refs_1_, bf16[256,128]{1,0:T(8,128)(2,1)} %copy-done.19, bf16[256,128]{1,0:T(8,128)(2,1)} %copy-done.21, bf16[256,128]{1,0:T(8,128)(2,1)} %copy-done.23, ...), custom_call_target="tpu_custom_call" | custom-call | tf_op jit(solution)/shard_map/nodes/pallas_call | solution.py:232
  238.6 0.7 broadcast_in_dim.80
  239.2 17.1 %all_to_all.10 = f32[128,2,128]{2,1,0:T(2,128)S(1)} all-to-all(f32[128,2,128]{2,1,0:T(2,128)S(1)} %broadcast_in_dim.80), channel_id=1, replica_groups=mesh['blk'=128] {'blk'}, dimensions={0} | all-to-all | bytes 262144 | tf_op jit(solution)/shard_map/all_to_all | solution.py:253
  256.4 0.1 reduce_sum.39
  256.5 2.9 %add_convert_fusion = bf16[4096,128]{1,0:T(8,128)(2,1)} fusion(f32[4096,128]{1,0:T(8,128)} %get-tuple-element.53, bf16[4096,128]{1,0:T(8,128)(2,1)S(1)} %copy-done, f32[128]{0:T(128)S(1)} %get-tuple-element.56, f32[128]{0:T(128)S(1)} %bitcast.100), kind=kLoop, calls=%fused_computation.1 | loop fusion | flops 2621440 | bytes 4195328 | tf_op jit(solution)/shard_map/convert_element_type | solution.py:333
  (124 shorter events, 1.1 us)
Async XLA Ops:
  1.4 20.2 %copy-start.31 = (s32[1,6,256]{2,0,1:T(1,128)S(1)}, s32[1,6,256]{2,0,1:T(1,128)}, u32[]{:S(2)}) copy-start(s32[1,6,256]{2,0,1:T(1,128)} %param.19) | copy-start | bytes 18436
  1.4 20.8 %copy-start.34 = (f32[2,128]{1,0:T(2,128)S(1)}, f32[2,128]{1,0:T(2,128)}, u32[]{:S(2)}) copy-start(f32[2,128]{1,0:T(2,128)} %param.21) | copy-start | bytes 3076
  1.4 20.8 %copy-start.35 = (f32[2,128]{1,0:T(2,128)S(1)}, f32[2,128]{1,0:T(2,128)}, u32[]{:S(2)}) copy-start(f32[2,128]{1,0:T(2,128)} %param.23) | copy-start | bytes 3076
  1.4 20.8 %copy-start.36 = (f32[2,128]{1,0:T(2,128)S(1)}, f32[2,128]{1,0:T(2,128)}, u32[]{:S(2)}) copy-start(f32[2,128]{1,0:T(2,128)} %param.24) | copy-start | bytes 3076
  1.4 20.8 %copy-start.29 = (bf16[2,128,128]{2,1,0:T(8,128)(2,1)S(1)}, bf16[2,128,128]{2,1,0:T(8,128)(2,1)}, u32[]{:S(2)}) copy-start(bf16[2,128,128]{2,1,0:T(8,128)(2,1)} %param.22) | copy-start | bytes 196612
  1.4 21.6 %copy-start.30 = (bf16[2,128,128]{2,1,0:T(8,128)(2,1)S(1)}, bf16[2,128,128]{2,1,0:T(8,128)(2,1)}, u32[]{:S(2)}) copy-start(bf16[2,128,128]{2,1,0:T(8,128)(2,1)} %param.27) | copy-start | bytes 196612
  1.4 22.2 %copy-start.10 = (bf16[2,256,128]{2,1,0:T(8,128)(2,1)S(1)}, bf16[2,256,128]{2,1,0:T(8,128)(2,1)}, u32[]{:S(2)}) copy-start(bf16[2,256,128]{2,1,0:T(8,128)(2,1)} %param.25) | copy-start | bytes 393220
  1.4 22.8 %copy-start.8 = (bf16[2,384,128]{2,1,0:T(8,128)(2,1)S(1)}, bf16[2,384,128]{2,1,0:T(8,128)(2,1)}, u32[]{:S(2)}) copy-start(bf16[2,384,128]{2,1,0:T(8,128)(2,1)} %param.20) | copy-start | bytes 589828
  5.5 18.7 %copy-start.9 = (s32[2,24576]{1,0:T(2,128)S(1)}, s32[2,24576]{1,0:T(2,128)}, u32[]{:S(2)}) copy-start(s32[2,24576]{1,0:T(2,128)} %param.17) | copy-start | bytes 589828
  5.6 19.3 %copy-start.1 = (s32[24576]{0:T(1024)S(1)}, s32[24576]{0:T(1024)}, u32[]{:S(2)}) copy-start(s32[24576]{0:T(1024)} %param.18) | copy-start | bytes 294916
  5.6 19.4 %copy-start.37 = (f32[2,128]{1,0:T(2,128)S(1)}, f32[2,128]{1,0:T(2,128)}, u32[]{:S(2)}) copy-start(f32[2,128]{1,0:T(2,128)} %param.26) | copy-start | bytes 3076
  5.8 23.0 %collective-permute-start.5 = (bf16[128,256]{1,0:T(8,128)(2,1)S(1)}, bf16[128,256]{1,0:T(8,128)(2,1)S(1)}, u32[]{:S(2)}, u32[]{:S(2)}) collective-permute-start(bf16[128,256]{1,0:T(8,128)(2,1)S(1)} %get-tuple-element.64), channel_id=1, source_target_pairs={{16,0},{17,1},{18,2},{19,3},{20,4},{21,5},{22,6},{23,7},{24,8},{25... | collective-permute-start | bytes 196616 | tf_op jit(solution)/shard_map/ppermute | solution.py:248
  11.9 18.2 %collective-permute-start.4 = (bf16[128,256]{1,0:T(8,128)(2,1)S(1)}, bf16[128,256]{1,0:T(8,128)(2,1)S(1)}, u32[]{:S(2)}, u32[]{:S(2)}) collective-permute-start(bf16[128,256]{1,0:T(8,128)(2,1)S(1)} %get-tuple-element.65), channel_id=1, source_target_pairs={{112,0},{113,1},{114,2},{115,3},{116,4},{117,5},{118,6},{119,7},{1... | collective-permute-start | bytes 196616 | tf_op jit(solution)/shard_map/ppermute | solution.py:248
  11.9 18.2 %collective-permute-start.3 = (bf16[128,256]{1,0:T(8,128)(2,1)S(1)}, bf16[128,256]{1,0:T(8,128)(2,1)S(1)}, u32[]{:S(2)}, u32[]{:S(2)}) collective-permute-start(bf16[128,256]{1,0:T(8,128)(2,1)S(1)} %get-tuple-element.66), channel_id=1, source_target_pairs={{4,0},{5,1},{6,2},{7,3},{8,4},{9,5},{10,6},{11,7},{12,8},{13,9},{1... | collective-permute-start | bytes 196616 | tf_op jit(solution)/shard_map/ppermute | solution.py:248
  20.0 10.1 %collective-permute-start.2 = (bf16[128,256]{1,0:T(8,128)(2,1)S(1)}, bf16[128,256]{1,0:T(8,128)(2,1)S(1)}, u32[]{:S(2)}, u32[]{:S(2)}) collective-permute-start(bf16[128,256]{1,0:T(8,128)(2,1)S(1)} %get-tuple-element.67), channel_id=1, source_target_pairs={{124,0},{125,1},{126,2},{127,3},{0,4},{1,5},{2,6},{3,7},{4,8},{5,9... | collective-permute-start | bytes 196616 | tf_op jit(solution)/shard_map/ppermute | solution.py:248
  20.0 10.1 %collective-permute-start.1 = (bf16[128,256]{1,0:T(8,128)(2,1)S(1)}, bf16[128,256]{1,0:T(8,128)(2,1)S(1)}, u32[]{:S(2)}, u32[]{:S(2)}) collective-permute-start(bf16[128,256]{1,0:T(8,128)(2,1)S(1)} %get-tuple-element.68), channel_id=1, source_target_pairs={{1,0},{2,1},{3,2},{4,3},{5,4},{6,5},{7,6},{8,7},{9,8},{10,9},{11,1... | collective-permute-start | bytes 196616 | tf_op jit(solution)/shard_map/ppermute | solution.py:248
  28.8 9.1 %copy-start.2 = (bf16[128,256]{1,0:T(8,128)(2,1)}, bf16[128,256]{1,0:T(8,128)(2,1)S(1)}, u32[]{:S(2)}) copy-start(bf16[128,256]{1,0:T(8,128)(2,1)S(1)} %collective-permute-done.5.refs_6_.refs_9_) | copy-start | bytes 196612
  28.8 7.0 %collective-permute-start = (bf16[128,256]{1,0:T(8,128)(2,1)S(1)}, bf16[128,256]{1,0:T(8,128)(2,1)S(1)}, u32[]{:S(2)}, u32[]{:S(2)}) collective-permute-start(bf16[128,256]{1,0:T(8,128)(2,1)S(1)} %get-tuple-element.69), channel_id=1, source_target_pairs={{127,0},{0,1},{1,2},{2,3},{3,4},{4,5},{5,6},{6,7},{7,8},{8,9},{9,1... | collective-permute-start | bytes 196616 | tf_op jit(solution)/shard_map/ppermute | solution.py:248
  30.1 7.8 %copy-start.3 = (bf16[128,256]{1,0:T(8,128)(2,1)}, bf16[128,256]{1,0:T(8,128)(2,1)S(1)}, u32[]{:S(2)}) copy-start(bf16[128,256]{1,0:T(8,128)(2,1)S(1)} %collective-permute-done.4.refs_5_.refs_8_) | copy-start | bytes 196612
  30.1 7.8 %copy-start.4 = (bf16[128,256]{1,0:T(8,128)(2,1)}, bf16[128,256]{1,0:T(8,128)(2,1)S(1)}, u32[]{:S(2)}) copy-start(bf16[128,256]{1,0:T(8,128)(2,1)S(1)} %collective-permute-done.3.refs_4_.refs_7_) | copy-start | bytes 196612
  30.1 7.8 %copy-start.5 = (bf16[128,256]{1,0:T(8,128)(2,1)}, bf16[128,256]{1,0:T(8,128)(2,1)S(1)}, u32[]{:S(2)}) copy-start(bf16[128,256]{1,0:T(8,128)(2,1)S(1)} %collective-permute-done.2.refs_3_.refs_6_) | copy-start | bytes 196612
  30.1 7.8 %copy-start.6 = (bf16[128,256]{1,0:T(8,128)(2,1)}, bf16[128,256]{1,0:T(8,128)(2,1)S(1)}, u32[]{:S(2)}) copy-start(bf16[128,256]{1,0:T(8,128)(2,1)S(1)} %collective-permute-done.1.refs_2_.refs_5_) | copy-start | bytes 196612
  35.8 2.1 copy-start.7
  82.4 11.6 %collective-permute-start.6 = (bf16[256,128]{1,0:T(8,128)(2,1)}, bf16[256,128]{1,0:T(8,128)(2,1)S(1)}, u32[]{:S(2)}, u32[]{:S(2)}) collective-permute-start(bf16[256,128]{1,0:T(8,128)(2,1)} %get-tuple-element.30), channel_id=1, source_target_pairs={{1,0},{2,1},{3,2},{4,3},{5,4},{6,5},{7,6},{8,7},{9,8},{10,9},{11,1... | collective-permute-start | bytes 196616 | tf_op jit(solution)/shard_map/ppermute | solution.py:248
  90.9 6.1 %collective-permute-start.7 = (bf16[256,128]{1,0:T(8,128)(2,1)}, bf16[256,128]{1,0:T(8,128)(2,1)S(1)}, u32[]{:S(2)}, u32[]{:S(2)}) collective-permute-start(bf16[256,128]{1,0:T(8,128)(2,1)} %get-tuple-element.31), channel_id=1, source_target_pairs={{127,0},{0,1},{1,2},{2,3},{3,4},{4,5},{5,6},{6,7},{7,8},{8,9},{9,1... | collective-permute-start | bytes 196616 | tf_op jit(solution)/shard_map/ppermute | solution.py:248
  91.0 6.0 %collective-permute-start.8 = (bf16[256,128]{1,0:T(8,128)(2,1)}, bf16[256,128]{1,0:T(8,128)(2,1)S(1)}, u32[]{:S(2)}, u32[]{:S(2)}) collective-permute-start(bf16[256,128]{1,0:T(8,128)(2,1)} %get-tuple-element.32), channel_id=1, source_target_pairs={{4,0},{5,1},{6,2},{7,3},{8,4},{9,5},{10,6},{11,7},{12,8},{13,9},{1... | collective-permute-start | bytes 196616 | tf_op jit(solution)/shard_map/ppermute | solution.py:248
  91.1 10.1 %collective-permute-start.9 = (bf16[256,128]{1,0:T(8,128)(2,1)}, bf16[256,128]{1,0:T(8,128)(2,1)S(1)}, u32[]{:S(2)}, u32[]{:S(2)}) collective-permute-start(bf16[256,128]{1,0:T(8,128)(2,1)} %get-tuple-element.33), channel_id=1, source_target_pairs={{124,0},{125,1},{126,2},{127,3},{0,4},{1,5},{2,6},{3,7},{4,8},{5,9... | collective-permute-start | bytes 196616 | tf_op jit(solution)/shard_map/ppermute | solution.py:248
  94.0 7.2 %collective-permute-start.10 = (bf16[256,128]{1,0:T(8,128)(2,1)}, bf16[256,128]{1,0:T(8,128)(2,1)S(1)}, u32[]{:S(2)}, u32[]{:S(2)}) collective-permute-start(bf16[256,128]{1,0:T(8,128)(2,1)} %get-tuple-element.34), channel_id=1, source_target_pairs={{16,0},{17,1},{18,2},{19,3},{20,4},{21,5},{22,6},{23,7},{24,8},{25... | collective-permute-start | bytes 196616 | tf_op jit(solution)/shard_map/ppermute | solution.py:248
  94.0 7.3 %copy-start.17 = (bf16[256,128]{1,0:T(8,128)(2,1)}, bf16[256,128]{1,0:T(8,128)(2,1)S(1)}, u32[]{:S(2)}) copy-start(bf16[256,128]{1,0:T(8,128)(2,1)S(1)} %collective-permute-done.6.refs_2_) | copy-start | bytes 196612
  94.0 7.3 %collective-permute-start.11 = (bf16[256,128]{1,0:T(8,128)(2,1)}, bf16[256,128]{1,0:T(8,128)(2,1)S(1)}, u32[]{:S(2)}, u32[]{:S(2)}) collective-permute-start(bf16[256,128]{1,0:T(8,128)(2,1)} %get-tuple-element.35), channel_id=1, source_target_pairs={{112,0},{113,1},{114,2},{115,3},{116,4},{117,5},{118,6},{119,7},{1... | collective-permute-start | bytes 196616 | tf_op jit(solution)/shard_map/ppermute | solution.py:248
  97.0 4.3 %copy-start.18 = (bf16[256,128]{1,0:T(8,128)(2,1)}, bf16[256,128]{1,0:T(8,128)(2,1)S(1)}, u32[]{:S(2)}) copy-start(bf16[256,128]{1,0:T(8,128)(2,1)S(1)} %collective-permute-done.7.refs_3_) | copy-start | bytes 196612
  97.0 4.3 %copy-start.20 = (bf16[256,128]{1,0:T(8,128)(2,1)}, bf16[256,128]{1,0:T(8,128)(2,1)S(1)}, u32[]{:S(2)}) copy-start(bf16[256,128]{1,0:T(8,128)(2,1)S(1)} %collective-permute-done.8.refs_4_) | copy-start | bytes 196612
  101.2 0.6 copy-start.22
  101.2 0.6 copy-start.24
  101.3 0.6 copy-start.27
  101.9 42.9 %copy-start.32 = (f32[2,128]{1,0:T(2,128)S(1)}, f32[2,128]{1,0:T(2,128)}, u32[]{:S(2)}) copy-start(f32[2,128]{1,0:T(2,128)} %param.29) | copy-start | bytes 3076
  101.9 42.9 %copy-start.33 = (f32[2,128]{1,0:T(2,128)S(1)}, f32[2,128]{1,0:T(2,128)}, u32[]{:S(2)}) copy-start(f32[2,128]{1,0:T(2,128)} %param.28) | copy-start | bytes 3076
  120.9 23.8 %all-to-all-start = ((f32[128,2,128]{2,1,0:T(2,128)}), f32[128,2,128]{2,1,0:T(2,128)S(1)}, u32[]{:S(2)}, u32[]{:S(2)}) async-start(f32[128,2,128]{2,1,0:T(2,128)} %broadcast_in_dim.73), calls=%async_computation | async-start | bytes 262144 | tf_op jit(solution)/shard_map/all_to_all | solution.py:253
  135.5 10.2 %collective-permute-start.12 = (bf16[128,256]{1,0:T(8,128)(2,1)}, bf16[128,256]{1,0:T(8,128)(2,1)S(1)}, u32[]{:S(2)}, u32[]{:S(2)}) collective-permute-start(bf16[128,256]{1,0:T(8,128)(2,1)} %get-tuple-element.38), channel_id=1, source_target_pairs={{127,0},{0,1},{1,2},{2,3},{3,4},{4,5},{5,6},{6,7},{7,8},{8,9},{9,1... | collective-permute-start | bytes 196616 | tf_op jit(solution)/shard_map/ppermute | solution.py:248
  137.2 14.1 %collective-permute-start.13 = (bf16[128,256]{1,0:T(8,128)(2,1)}, bf16[128,256]{1,0:T(8,128)(2,1)S(1)}, u32[]{:S(2)}, u32[]{:S(2)}) collective-permute-start(bf16[128,256]{1,0:T(8,128)(2,1)} %get-tuple-element.39), channel_id=1, source_target_pairs={{1,0},{2,1},{3,2},{4,3},{5,4},{6,5},{7,6},{8,7},{9,8},{10,9},{11,1... | collective-permute-start | bytes 196616 | tf_op jit(solution)/shard_map/ppermute | solution.py:248
  137.2 14.1 %collective-permute-start.14 = (bf16[128,256]{1,0:T(8,128)(2,1)}, bf16[128,256]{1,0:T(8,128)(2,1)S(1)}, u32[]{:S(2)}, u32[]{:S(2)}) collective-permute-start(bf16[128,256]{1,0:T(8,128)(2,1)} %get-tuple-element.40), channel_id=1, source_target_pairs={{124,0},{125,1},{126,2},{127,3},{0,4},{1,5},{2,6},{3,7},{4,8},{5,9... | collective-permute-start | bytes 196616 | tf_op jit(solution)/shard_map/ppermute | solution.py:248
  140.2 11.1 %collective-permute-start.15 = (bf16[128,256]{1,0:T(8,128)(2,1)}, bf16[128,256]{1,0:T(8,128)(2,1)S(1)}, u32[]{:S(2)}, u32[]{:S(2)}) collective-permute-start(bf16[128,256]{1,0:T(8,128)(2,1)} %get-tuple-element.41), channel_id=1, source_target_pairs={{4,0},{5,1},{6,2},{7,3},{8,4},{9,5},{10,6},{11,7},{12,8},{13,9},{1... | collective-permute-start | bytes 196616 | tf_op jit(solution)/shard_map/ppermute | solution.py:248
  144.6 6.9 %collective-permute-start.16 = (bf16[128,256]{1,0:T(8,128)(2,1)}, bf16[128,256]{1,0:T(8,128)(2,1)S(1)}, u32[]{:S(2)}, u32[]{:S(2)}) collective-permute-start(bf16[128,256]{1,0:T(8,128)(2,1)} %get-tuple-element.42), channel_id=1, source_target_pairs={{112,0},{113,1},{114,2},{115,3},{116,4},{117,5},{118,6},{119,7},{1... | collective-permute-start | bytes 196616 | tf_op jit(solution)/shard_map/ppermute | solution.py:248
  145.7 8.8 %copy-start.11 = (bf16[128,256]{1,0:T(8,128)(2,1)}, bf16[128,256]{1,0:T(8,128)(2,1)S(1)}, u32[]{:S(2)}) copy-start(bf16[128,256]{1,0:T(8,128)(2,1)S(1)} %collective-permute-done.12.refs_10_) | copy-start | bytes 196612
  145.7 6.7 %collective-permute-start.17 = (bf16[128,256]{1,0:T(8,128)(2,1)}, bf16[128,256]{1,0:T(8,128)(2,1)S(1)}, u32[]{:S(2)}, u32[]{:S(2)}) collective-permute-start(bf16[128,256]{1,0:T(8,128)(2,1)} %get-tuple-element.43), channel_id=1, source_target_pairs={{16,0},{17,1},{18,2},{19,3},{20,4},{21,5},{22,6},{23,7},{24,8},{25... | collective-permute-start | bytes 196616 | tf_op jit(solution)/shard_map/ppermute | solution.py:248
  151.3 3.2 %copy-start.12 = (bf16[128,256]{1,0:T(8,128)(2,1)}, bf16[128,256]{1,0:T(8,128)(2,1)S(1)}, u32[]{:S(2)}) copy-start(bf16[128,256]{1,0:T(8,128)(2,1)S(1)} %collective-permute-done.13.refs_11_) | copy-start | bytes 196612
  151.3 3.2 %copy-start.13 = (bf16[128,256]{1,0:T(8,128)(2,1)}, bf16[128,256]{1,0:T(8,128)(2,1)S(1)}, u32[]{:S(2)}) copy-start(bf16[128,256]{1,0:T(8,128)(2,1)S(1)} %collective-permute-done.14.refs_12_) | copy-start | bytes 196612
  151.3 3.2 %copy-start.14 = (bf16[128,256]{1,0:T(8,128)(2,1)}, bf16[128,256]{1,0:T(8,128)(2,1)S(1)}, u32[]{:S(2)}) copy-start(bf16[128,256]{1,0:T(8,128)(2,1)S(1)} %collective-permute-done.15.refs_13_) | copy-start | bytes 196612
  151.6 2.9 %copy-start.15 = (bf16[128,256]{1,0:T(8,128)(2,1)}, bf16[128,256]{1,0:T(8,128)(2,1)S(1)}, u32[]{:S(2)}) copy-start(bf16[128,256]{1,0:T(8,128)(2,1)S(1)} %collective-permute-done.16.refs_14_) | copy-start | bytes 196612
  152.4 2.1 copy-start.16
  199.8 16.6 %collective-permute-start.18 = (bf16[256,128]{1,0:T(8,128)(2,1)}, bf16[256,128]{1,0:T(8,128)(2,1)S(1)}, u32[]{:S(2)}, u32[]{:S(2)}) collective-permute-start(bf16[256,128]{1,0:T(8,128)(2,1)} %get-tuple-element.47), channel_id=1, source_target_pairs={{1,0},{2,1},{3,2},{4,3},{5,4},{6,5},{7,6},{8,7},{9,8},{10,9},{11,1... | collective-permute-start | bytes 196616 | tf_op jit(solution)/shard_map/ppermute | solution.py:248
  207.9 8.6 %collective-permute-start.19 = (bf16[256,128]{1,0:T(8,128)(2,1)}, bf16[256,128]{1,0:T(8,128)(2,1)S(1)}, u32[]{:S(2)}, u32[]{:S(2)}) collective-permute-start(bf16[256,128]{1,0:T(8,128)(2,1)} %get-tuple-element.48), channel_id=1, source_target_pairs={{127,0},{0,1},{1,2},{2,3},{3,4},{4,5},{5,6},{6,7},{7,8},{8,9},{9,1... | collective-permute-start | bytes 196616 | tf_op jit(solution)/shard_map/ppermute | solution.py:248
  207.9 8.6 %collective-permute-start.20 = (bf16[256,128]{1,0:T(8,128)(2,1)}, bf16[256,128]{1,0:T(8,128)(2,1)S(1)}, u32[]{:S(2)}, u32[]{:S(2)}) collective-permute-start(bf16[256,128]{1,0:T(8,128)(2,1)} %get-tuple-element.49), channel_id=1, source_target_pairs={{4,0},{5,1},{6,2},{7,3},{8,4},{9,5},{10,6},{11,7},{12,8},{13,9},{1... | collective-permute-start | bytes 196616 | tf_op jit(solution)/shard_map/ppermute | solution.py:248
  209.6 10.9 %collective-permute-start.21 = (bf16[256,128]{1,0:T(8,128)(2,1)}, bf16[256,128]{1,0:T(8,128)(2,1)S(1)}, u32[]{:S(2)}, u32[]{:S(2)}) collective-permute-start(bf16[256,128]{1,0:T(8,128)(2,1)} %get-tuple-element.50), channel_id=1, source_target_pairs={{124,0},{125,1},{126,2},{127,3},{0,4},{1,5},{2,6},{3,7},{4,8},{5,9... | collective-permute-start | bytes 196616 | tf_op jit(solution)/shard_map/ppermute | solution.py:248
  210.9 9.7 %collective-permute-start.22 = (bf16[256,128]{1,0:T(8,128)(2,1)}, bf16[256,128]{1,0:T(8,128)(2,1)S(1)}, u32[]{:S(2)}, u32[]{:S(2)}) collective-permute-start(bf16[256,128]{1,0:T(8,128)(2,1)} %get-tuple-element.51), channel_id=1, source_target_pairs={{16,0},{17,1},{18,2},{19,3},{20,4},{21,5},{22,6},{23,7},{24,8},{25... | collective-permute-start | bytes 196616 | tf_op jit(solution)/shard_map/ppermute | solution.py:248
  216.4 7.0 %copy-start.19 = (bf16[256,128]{1,0:T(8,128)(2,1)}, bf16[256,128]{1,0:T(8,128)(2,1)S(1)}, u32[]{:S(2)}) copy-start(bf16[256,128]{1,0:T(8,128)(2,1)S(1)} %collective-permute-done.18.refs_2_) | copy-start | bytes 196612
  216.4 6.9 %collective-permute-start.23 = (bf16[256,128]{1,0:T(8,128)(2,1)}, bf16[256,128]{1,0:T(8,128)(2,1)S(1)}, u32[]{:S(2)}, u32[]{:S(2)}) collective-permute-start(bf16[256,128]{1,0:T(8,128)(2,1)} %get-tuple-element.52), channel_id=1, source_target_pairs={{112,0},{113,1},{114,2},{115,3},{116,4},{117,5},{118,6},{119,7},{1... | collective-permute-start | bytes 196616 | tf_op jit(solution)/shard_map/ppermute | solution.py:248
  216.5 6.9 %copy-start.21 = (bf16[256,128]{1,0:T(8,128)(2,1)}, bf16[256,128]{1,0:T(8,128)(2,1)S(1)}, u32[]{:S(2)}) copy-start(bf16[256,128]{1,0:T(8,128)(2,1)S(1)} %collective-permute-done.19.refs_3_) | copy-start | bytes 196612
  216.5 6.9 %copy-start.23 = (bf16[256,128]{1,0:T(8,128)(2,1)}, bf16[256,128]{1,0:T(8,128)(2,1)S(1)}, u32[]{:S(2)}) copy-start(bf16[256,128]{1,0:T(8,128)(2,1)S(1)} %collective-permute-done.20.refs_4_) | copy-start | bytes 196612
  220.5 2.9 %copy-start.25 = (bf16[256,128]{1,0:T(8,128)(2,1)}, bf16[256,128]{1,0:T(8,128)(2,1)S(1)}, u32[]{:S(2)}) copy-start(bf16[256,128]{1,0:T(8,128)(2,1)S(1)} %collective-permute-done.21.refs_5_) | copy-start | bytes 196612
  220.5 2.9 %copy-start.26 = (bf16[256,128]{1,0:T(8,128)(2,1)}, bf16[256,128]{1,0:T(8,128)(2,1)S(1)}, u32[]{:S(2)}) copy-start(bf16[256,128]{1,0:T(8,128)(2,1)S(1)} %collective-permute-done.22.refs_6_) | copy-start | bytes 196612
  223.4 0.6 copy-start.28
  223.4 33.1 %copy-start = (bf16[4096,128]{1,0:T(8,128)(2,1)S(1)}, bf16[4096,128]{1,0:T(8,128)(2,1)}, u32[]{:S(2)}) copy-start(bf16[4096,128]{1,0:T(8,128)(2,1)} %get-tuple-element.45.refs_0_) | copy-start | bytes 3145732

commit v2 on v1

v2 whole, which is shorter than its diff:
```python
import functools

import jax
import jax.numpy as jnp
from jax import lax
from jax.experimental import pallas as pl
from jax.experimental.pallas import tpu as pltpu
from jax.sharding import PartitionSpec as P

LAYERS = 2
FACES = 6
C = 128
NODES = 4096
HALO = 256
TILE = 128
EDGES = 24576
GROUPS = NODES // TILE
GSTEP = 8
LAG1 = 3
LAG2 = 6
GE = FACES * TILE
SE = GSTEP * GE
STEPS = GROUPS // GSTEP
NB = 256
NSTEP = 8
NLAG = 1
BF = jnp.bfloat16
F32 = jnp.float32
FAR = -1000.0


def hot_rows(row, rows):
    n = row.shape[1]
    index = jnp.broadcast_to(row, (16, n)).astype(BF)[None]
    counter = lax.broadcasted_iota(jnp.int32, (rows, n), 0).astype(F32).astype(BF)
    counter = counter.reshape(rows // 16, 16, n)
    hot = jnp.where(counter == index, jnp.ones((), BF), jnp.zeros((), BF))
    return hot.reshape(rows, n)


def dot(a, b):
    return jnp.dot(a, b, preferred_element_type=F32)


def dot_nt(a, b):
    return lax.dot_general(a, b, (((1,), (1,)), ((), ())), preferred_element_type=F32)


def receiver(ends_ref, owned_ref, lanes, base):
    local = (ends_ref[1:2, lanes] - base).astype(F32)
    return jnp.where(owned_ref[0:1, lanes] > 0, local, FAR)


def scale_shift(layer, total_ref, gain_ref, shift_ref):
    mu = total_ref[0:1, :]
    var = jnp.maximum(total_ref[1:2, :] - mu * mu, 0.0)
    a = gain_ref[layer : layer + 1, :] * lax.rsqrt(var + 1e-05)
    return a, shift_ref[layer : layer + 1, :] - a * mu


def edge_kernel(layer, moved, face_ref, *refs):
    refs = list(refs)
    h_ref = refs.pop(0)
    if moved:
        upd_ref, total_ref, ngain_ref, nshift_ref = [refs.pop(0) for _ in range(4)]
    halo = [refs.pop(0) for _ in range(FACES)]
    if moved:
        halo_upd = [refs.pop(0) for _ in range(FACES)]
    e_ref, ends_ref, owned_ref, w1_ref, b1_ref, w2_in, egain_ref, eshift_ref = refs[:8]
    refs = refs[8:]
    if moved:
        h_out = refs.pop(0)
    e_out, own_out = refs.pop(0), refs.pop(0)
    halo_out = [refs.pop(0) for _ in range(FACES)]
    tab_ref, acc_ref, wsr_ref, we_ref, w2_ref, col_ref, row_ref = refs
    step = pl.program_id(0)

    def column(row):
        return jnp.broadcast_to(row, (C, C)).T

    @pl.when(step == 0)
    def _():
        acc_ref[...] = jnp.zeros_like(acc_ref)
        w1 = w1_ref[0]
        wsr_ref[0:C] = w1[C : 2 * C].T
        wsr_ref[C : 2 * C] = w1[2 * C : 3 * C].T
        we_ref[...] = w1[0:C].T
        w2 = w2_in[0].astype(F32)
        w2 = w2 - jnp.sum(w2, axis=1, keepdims=True) * (1.0 / C)
        w2_ref[...] = w2.T.astype(BF)
        bias = column(b1_ref[layer : layer + 1, :])
        col_ref[0] = bias
        col_ref[1] = column(egain_ref[layer : layer + 1, :])
        col_ref[2] = column(eshift_ref[layer : layer + 1, :])
        bias2 = jnp.concatenate([bias, bias], axis=1)
        if moved:
            a, b = scale_shift(layer - 1, total_ref, ngain_ref, nshift_ref)
            row_ref[0:1, :] = a
            row_ref[1:2, :] = b
            a2 = jnp.concatenate([column(a)] * 2, axis=1)
            b2 = jnp.concatenate([column(b)] * 2, axis=1)
        for m in range(FACES):
            ht = halo[m][...].T
            if moved:
                ht = (ht.astype(F32) + halo_upd[m][...].astype(F32) * a2 + b2).astype(BF)
            t = dot(wsr_ref[...], ht)
            k = face_ref[m]
            tab_ref[k, :, 0:HALO] = (t[0:C] + bias2).astype(BF)
            tab_ref[k, :, HALO : 2 * HALO] = t[C : 2 * C].astype(BF)

    tables = []
    for g in range(GSTEP):
        hg = h_ref[g * TILE : (g + 1) * TILE, :]
        if moved:
            up = upd_ref[g * TILE : (g + 1) * TILE, :]
            hg = (hg.astype(F32) + up * row_ref[0:1, :] + row_ref[1:2, :]).astype(BF)
            h_out[g * TILE : (g + 1) * TILE, :] = hg
        t = dot_nt(wsr_ref[...], hg)
        ps = (t[0:C] + col_ref[0]).astype(BF)
        pr = t[C : 2 * C].astype(BF)
        tables.append(jnp.concatenate([ps, pr, we_ref[...]], axis=1))
    gain = jnp.concatenate([col_ref[1]] * 2, axis=1)
    shift = jnp.concatenate([col_ref[2]] * 2, axis=1)
    pre_own, old, r_own, fresh, hidden, r_halo = {}, {}, {}, {}, {}, {}

    def own_part(g, j):
        lanes = slice(g * GE + j * 2 * TILE, g * GE + (j + 1) * 2 * TILE)
        et = e_ref[:, lanes] if moved else e_ref[lanes, :].T
        base = (step * GSTEP + g) * TILE
        s_hot = hot_rows((ends_ref[0:1, lanes] - base).astype(F32), TILE)
        r_hot = hot_rows(receiver(ends_ref, owned_ref, lanes, base), TILE)
        r_own[g, j] = r_hot
        pre = dot(tables[g], jnp.concatenate([s_hot, r_hot, et], axis=0))
        for i in range(2):
            pre_own[g, 2 * j + i] = pre[:, i * TILE : (i + 1) * TILE]
            old[g, 2 * j + i] = et[:, i * TILE : (i + 1) * TILE]

    def two(row_of, p, k):
        cut = [slice(g * GE + k * TILE, g * GE + (k + 1) * TILE) for g in (2 * p, 2 * p + 1)]
        return jnp.concatenate([row_of(c) for c in cut], axis=1)

    def first(p, k):
        base = NODES + k * HALO
        s_hot = hot_rows(two(lambda c: (ends_ref[0:1, c] - base).astype(F32), p, k), HALO)
        r_hot = hot_rows(two(lambda c: receiver(ends_ref, owned_ref, c, base), p, k), HALO)
        r_halo[p, k] = r_hot
        pre = dot(tab_ref[k], jnp.concatenate([s_hot, r_hot], axis=0))
        pre = pre + jnp.concatenate([pre_own[2 * p, k], pre_own[2 * p + 1, k]], axis=1)
        hidden[p, k] = jnp.maximum(pre, 0.0).astype(BF)

    def second(p, k):
        z = dot(w2_ref[...], hidden[p, k])
        spread = jnp.sum(z * z, axis=0, keepdims=True) * (1.0 / C)
        own_row = two(lambda c: owned_ref[0:1, c].astype(F32), p, k)
        rs = lax.rsqrt(spread + 1e-05) * own_row
        before = jnp.concatenate([old[2 * p, k], old[2 * p + 1, k]], axis=1).astype(F32)
        value = (before + (z * gain) * rs + shift * own_row).astype(BF)
        fresh[p, k] = value
        for i in range(2):
            g = 2 * p + i
            lanes = slice(g * GE + k * TILE, g * GE + (k + 1) * TILE)
            if moved:
                e_out[lanes, :] = value[:, i * TILE : (i + 1) * TILE].T
            else:
                e_out[:, lanes] = value[:, i * TILE : (i + 1) * TILE]

    def third(p, k):
        acc_ref[k] = acc_ref[k] + dot_nt(r_halo[p, k], fresh[p, k])
        if k == FACES - 1:
            for i in range(2):
                g = 2 * p + i
                hot = jnp.concatenate([r_own[g, j] for j in range(3)], axis=1)
                new = jnp.concatenate(
                    [fresh[p, q][:, i * TILE : (i + 1) * TILE] for q in range(FACES)], axis=1
                )
                own_out[g * TILE : (g + 1) * TILE, :] = dot_nt(hot, new)

    units = [(p, k) for p in range(GSTEP // 2) for k in range(FACES)]
    parts = [(2 * p + i, j) for p in range(GSTEP // 2) for j in range(3) for i in range(2)]
    own_part(*parts[0])
    own_part(*parts[1])
    for t in range(len(units) + LAG2):
        if t < len(units):
            first(*units[t])
        if 0 <= t - LAG1 < len(units):
            second(*units[t - LAG1])
        if 0 <= t - LAG2:
            third(*units[t - LAG2])
        if t + 2 < len(parts):
            own_part(*parts[t + 2])

    @pl.when(step == STEPS - 1)
    def _():
        for k in range(FACES):
            halo_out[k][...] = acc_ref[face_ref[k]].astype(BF)


def full(shape):
    zeros = (0,) * len(shape)
    return pl.BlockSpec(shape, lambda i, *_: zeros)


def of_layer(shape, layer):
    return pl.BlockSpec((1,) + shape[1:], lambda i, *_: (layer, 0, 0))


def edge_layer(layer, faces, h, extra, halos, halo_upds, e, ends, owned, weights):
    moved = layer > 0
    rows = pl.BlockSpec((GSTEP * TILE, C), lambda i, *_: (i, 0))
    by_edge = pl.BlockSpec((SE, C), lambda i, *_: (i, 0))
    by_lane = pl.BlockSpec((C, SE), lambda i, *_: (0, i))
    args, specs = [h], [rows]
    if moved:
        args += list(extra)
        specs += [rows] + [full(x.shape) for x in extra[1:]]
    args += list(halos)
    specs += [full((HALO, C))] * FACES
    if moved:
        args += list(halo_upds)
        specs += [full((C, HALO))] * FACES
    args += [e, ends, owned] + list(weights)
    specs += [by_lane if moved else by_edge]
    specs += [pl.BlockSpec((n, SE), lambda i, *_: (0, i)) for n in (2, 1)]
    specs += [of_layer(w.shape, layer) if w.ndim == 3 else full(w.shape) for w in weights]
    outs, out_specs = [], []
    if moved:
        outs.append(jax.ShapeDtypeStruct((NODES, C), BF))
        out_specs.append(rows)
    outs.append(jax.ShapeDtypeStruct((EDGES, C) if moved else (C, EDGES), BF))
    out_specs.append(by_edge if moved else by_lane)
    outs.append(jax.ShapeDtypeStruct((NODES, C), F32))
    out_specs.append(rows)
    outs += [jax.ShapeDtypeStruct((HALO, C), BF)] * FACES
    out_specs += [full((HALO, C))] * FACES
    return pl.pallas_call(
        functools.partial(edge_kernel, layer, moved),
        grid_spec=pltpu.PrefetchScalarGridSpec(
            num_scalar_prefetch=1,
            grid=(STEPS,),
            in_specs=specs,
            out_specs=out_specs,
            scratch_shapes=[
                pltpu.VMEM((FACES, C, 2 * HALO), BF),
                pltpu.VMEM((FACES, HALO, C), F32),
                pltpu.VMEM((2 * C, C), BF),
                pltpu.VMEM((C, C), BF),
                pltpu.VMEM((C, C), BF),
                pltpu.VMEM((3, C, C), F32),
                pltpu.VMEM((8, C), F32),
            ],
        ),
        out_shape=outs,
        name="edges",
    )(faces, *args)


def rows_of(u):
    return slice(u * NB, (u + 1) * NB)


def node_kernel(layer, send, *refs):
    refs = list(refs)
    h_ref, own_ref = refs.pop(0), refs.pop(0)
    ret = [refs.pop(0) for _ in range(FACES)]
    sidx_ref, w1_ref, b1_ref, w2_ref = refs[:4]
    upd_ref, stat_ref = refs[4], refs[5]
    sent = refs[6 : 6 + FACES] if send else None
    acc_ref = refs[6 + FACES] if send else None
    sum_ref = refs[-1]
    step = pl.program_id(0)

    @pl.when(step == 0)
    def _():
        sum_ref[...] = jnp.zeros_like(sum_ref)
        if send:
            acc_ref[...] = jnp.zeros_like(acc_ref)

    arrived = jnp.concatenate([r[...] for r in ret], axis=0)
    hots, node_in, hidden, update = {}, {}, {}, {}
    sums = [jnp.zeros((8, C), F32), jnp.zeros((8, C), F32)]

    def gather(u):
        base = step * NSTEP * NB + u * NB
        hots[u] = [hot_rows((sidx_ref[k : k + 1, :] - base).astype(F32), NB) for k in range(FACES)]
        total = own_ref[rows_of(u), :] + dot(jnp.concatenate(hots[u], axis=1), arrived)
        node_in[u] = jnp.concatenate([h_ref[rows_of(u), :], total.astype(BF)], axis=1)

    def first(u):
        pre = dot(node_in[u], w1_ref[0]) + b1_ref[layer : layer + 1, :]
        hidden[u] = jnp.maximum(pre, 0.0).astype(BF)

    def second(u):
        value = dot(hidden[u], w2_ref[0])
        upd_ref[rows_of(u), :] = value
        sums[0] = sums[0] + jnp.sum(value.reshape(NB // 8, 8, C), axis=0)
        sums[1] = sums[1] + jnp.sum((value * value).reshape(NB // 8, 8, C), axis=0)
        update[u] = value.astype(BF)

    def third(u):
        if send:
            ut = update[u].T
            for k in range(FACES):
                acc_ref[k] = acc_ref[k] + dot(ut, hots[u][k])

    stages = (gather, first, second, third)
    for t in range(NSTEP + NLAG * 3):
        for i, stage in enumerate(stages):
            if 0 <= t - NLAG * i < NSTEP:
                stage(t - NLAG * i)
    sum_ref[0:1, :] += jnp.sum(sums[0], axis=0, keepdims=True)
    sum_ref[1:2, :] += jnp.sum(sums[1], axis=0, keepdims=True)

    @pl.when(step == NODES // NB // NSTEP - 1)
    def _():
        stat_ref[...] = jnp.broadcast_to(sum_ref[0:2, :][None], stat_ref.shape)
        if send:
            for k in range(FACES):
                sent[k][...] = acc_ref[k].astype(BF)


def node_layer(layer, send, devices, h, own, returned, sidx, weights):
    rows = pl.BlockSpec((NSTEP * NB, C), lambda i: (i, 0))
    stats = (devices, 2, C)
    outs = [jax.ShapeDtypeStruct((NODES, C), F32), jax.ShapeDtypeStruct(stats, F32)]
    out_specs = [rows, full(stats)]
    scratch = []
    if send:
        outs += [jax.ShapeDtypeStruct((C, HALO), BF)] * FACES
        out_specs += [full((C, HALO))] * FACES
        scratch = [pltpu.VMEM((FACES, C, HALO), F32)]
    return pl.pallas_call(
        functools.partial(node_kernel, layer, send),
        grid=(NODES // NB // NSTEP,),
        in_specs=[rows, rows]
        + [full((HALO, C))] * FACES
        + [full(sidx.shape)]
        + [of_layer(w.shape, layer) if w.ndim == 3 else full(w.shape) for w in weights],
        out_specs=out_specs,
        out_shape=outs,
        scratch_shapes=scratch + [pltpu.VMEM((8, C), F32)],
        name="nodes",
    )(h, own, *returned, sidx, *weights)


SLOTS = tuple((bit, side) for bit in (0, 2, 4) for side in (0, 1))


def swap(blocks):
    n = lax.axis_size("blk")
    out = []
    for block, (bit, side) in zip(blocks, SLOTS):
        step = 1 << bit
        pairs = [(i, (i + (step if (i >> bit) & 1 == side else -step)) % n) for i in range(n)]
        out.append(lax.ppermute(block, "blk", pairs))
    return out


def total_over(stats):
    return jnp.sum(lax.all_to_all(stats, "blk", 0, 0), axis=0)


def per_device(
    node_latent,
    edge_latent,
    edge_ends,
    edge_owned,
    send_index,
    edge_w1,
    edge_b1,
    edge_w2,
    edge_gain,
    edge_shift,
    node_w1,
    node_b1,
    node_w2,
    node_gain,
    node_shift,
):
    devices = lax.axis_size("blk")
    total_nodes = NODES * devices
    here = lax.axis_index("blk")
    odd = [(here >> bit) & 1 for bit in (0, 2, 4)]
    faces = jnp.stack([2 * j + 1 - (odd[j] ^ side) for j in range(3) for side in (0, 1)])
    index = send_index[0]
    sidx = jnp.concatenate(
        [
            jnp.where(odd[j] == side, index[2 * j : 2 * j + 1], index[2 * j + 1 : 2 * j + 2])
            for j in range(3)
            for side in (0, 1)
        ]
    )
    owned = edge_owned[None]
    h = node_latent
    e = edge_latent
    rows = node_latent[sidx.reshape(-1)]
    halos = swap([rows[k * HALO : (k + 1) * HALO] for k in range(FACES)])
    extra = None
    halo_upds = None
    edge_weights = (edge_w1, edge_b1, edge_w2, edge_gain, edge_shift)
    node_weights = (node_w1, node_b1, node_w2)
    for layer in range(LAYERS):
        outs = edge_layer(
            layer, faces, h, extra, halos, halo_upds, e, edge_ends, owned, edge_weights
        )
        if layer > 0:
            h, outs = outs[0], outs[1:]
        e, own = outs[0], outs[1]
        returned = swap(outs[2:])
        send = layer < LAYERS - 1
        outs = node_layer(layer, send, devices, h, own, returned, sidx, node_weights)
        update, stats = outs[0], outs[1]
        if send:
            halo_upds = swap(outs[2:])
        totals = total_over(stats) / total_nodes
        extra = (update, totals, node_gain, node_shift)
    a, b = scale_shift(LAYERS - 1, totals, node_gain, node_shift)
    out = (h.astype(F32) + update * a + b).astype(BF)
    return (out, e)


def solution(mesh):
    shared = P()
    return jax.shard_map(
        per_device,
        mesh=mesh,
        in_specs=(
            P("blk", None),
            P("blk", None),
            P(None, "blk"),
            P("blk"),
            P("blk", None, None),
        )
        + (shared,) * 10,
        out_specs=(P("blk", None), P("blk", None)),
        check_vma=False,
    )
```

time: 260 us -> 163 us (0.63)
  Pallas kernels: 122 us -> 57.2 us
  starting transfers between devices: 74.1 us -> 60 us
  local copies, waits for them, and re-layouts: 18.1 us -> 7.23 us
  other arithmetic: 9.01 us -> 4.61 us
  waiting for transfers between devices: 18 us -> 15.1 us
    pallas_call x4, Pallas kernels: 122 us -> 57.2 us  [the longest x2 41 us: edge_layer(): pl.pallas_call(functools.partial(edge_kernel, layer, moved), grid_spec=pl...]
    ppermute x24, starting transfers between devices: 61.7 us -> 51.3 us  [swap(): out.append(lax.ppermute(block, 'blk', pairs))]
    broadcast_in_dim x11 -> x0, local copies, waits for them, and re-layouts: 6.17 us -> none  [the longest x9 4.21 us: per_device(): lanes = lambda v: jnp.broadcast_to(v[:, None], (C, C))]
    all_to_all x1, starting transfers between devices: 12.4 us -> 8.68 us  [total_over(): return jnp.sum(lax.all_to_all(stats, 'blk', 0, 0), axis=0)]
    ppermute x24, waiting for transfers between devices: 18 us -> 14.7 us  [swap(): out.append(lax.ppermute(block, 'blk', pairs))]
  transfers between devices with their start and end apart: 25 -> 25, of which waited for: 7 -> 10; matrix products, arithmetic and copies ran while one was open for 4% -> 1% of each run, Pallas kernels for 0% -> 0%
where the time goes in v2:
time: 163 us; the launch traced here: 162 us
  starting transfers between devices  60 us (37%)
  Pallas kernels  57.2 us (35%)
  blocking collectives  17.1 us (10%)
  waiting for transfers between devices  15.1 us (9%)
  local copies, waits for them, and re-layouts  7.23 us (4%)
  other arithmetic  4.61 us (3%)
    ppermute x24, starting transfers between devices, swap(): out.append(lax.ppermute(block, 'blk', pairs))  51.3 us
    pallas_call x2, Pallas kernels, edge_layer(): pl.pallas_call(functools.partial(edge_kernel, layer, moved), grid_spec=pl...  41 us
    all_to_all x1, blocking collectives, total_over(): return jnp.sum(lax.all_to_all(stats, 'blk', 0, 0), axis=0)  17.1 us
    pallas_call x2, Pallas kernels, node_layer(): pl.pallas_call(functools.partial(node_kernel, layer, send), grid=(NODES /...  16.3 us
    ppermute x24, waiting for transfers between devices, swap(): out.append(lax.ppermute(block, 'blk', pairs))  14.7 us
    all_to_all x1, starting transfers between devices, total_over(): return jnp.sum(lax.all_to_all(stats, 'blk', 0, 0), axis=0)  8.68 us
    gather x1, local copies, waits for them, and re-layouts, per_device(): rows = node_latent[sidx.reshape(-1)]  4 us
  transfers between devices with their start and end apart: 25, of which 10 were waited for; matrix products, arithmetic and copies ran while one was open for 1% of the time, Pallas kernels for 0%

profile of v2, /device:TPU:1, one launch (start us, length us, event | category | flops | bytes accessed | tf_op | source)
XLA Modules:
  0.0 162.3 jit_solution(9796501243435617845)
XLA Ops:
  0.6 0.8 fusion.6
  1.5 4.0 %gather_fusion = bf16[1536,128]{1,0:T(8,128)(2,1)S(1)} fusion(bf16[4096,128]{1,0:T(8,128)(2,1)} %refs_0_.5, s32[2048]{0:T(1024)S(1)} %pad_clamp_fusion), kind=kCustom, calls=%fused_computation | custom fusion | bytes 792576 | tf_op jit(solution)/shard_map/gather | solution.py:395
  5.6 6.1 %collective-permute-start.5 = (bf16[256,128]{1,0:T(8,128)(2,1)S(1)}, bf16[256,128]{1,0:T(8,128)(2,1)S(1)}, u32[]{:S(2)}, u32[]{:S(2)}) collective-permute-start(bf16[256,128]{1,0:T(8,128)(2,1)S(1)} %get-tuple-element.58), channel_id=1, source_target_pairs={{0,112},{1,113},{2,114},{3,115},{4,116},{5,117},{6,118},{7,119},{8... | collective-permute-start | bytes 196616 | tf_op jit(solution)/shard_map/ppermute | solution.py:354
  11.7 0.0 collective-permute-start.4
  11.7 6.2 %collective-permute-start.3 = (bf16[256,128]{1,0:T(8,128)(2,1)S(1)}, bf16[256,128]{1,0:T(8,128)(2,1)S(1)}, u32[]{:S(2)}, u32[]{:S(2)}) collective-permute-start(bf16[256,128]{1,0:T(8,128)(2,1)S(1)} %get-tuple-element.60), channel_id=1, source_target_pairs={{0,124},{1,125},{2,126},{3,127},{4,8},{5,9},{6,10},{7,11},{8,4},{9... | collective-permute-start | bytes 196616 | tf_op jit(solution)/shard_map/ppermute | solution.py:354
  17.8 0.0 collective-permute-start.2
  17.9 2.1 %collective-permute-start.1 = (bf16[256,128]{1,0:T(8,128)(2,1)S(1)}, bf16[256,128]{1,0:T(8,128)(2,1)S(1)}, u32[]{:S(2)}, u32[]{:S(2)}) collective-permute-start(bf16[256,128]{1,0:T(8,128)(2,1)S(1)} %get-tuple-element.62), channel_id=1, source_target_pairs={{0,127},{1,2},{2,1},{3,4},{4,3},{5,6},{6,5},{7,8},{8,7},{9,10},{10... | collective-permute-start | bytes 196616 | tf_op jit(solution)/shard_map/ppermute | solution.py:354
  20.0 0.0 collective-permute-done.5.refs_6_.refs_10_
  20.0 1.6 %collective-permute-start = (bf16[256,128]{1,0:T(8,128)(2,1)S(1)}, bf16[256,128]{1,0:T(8,128)(2,1)S(1)}, u32[]{:S(2)}, u32[]{:S(2)}) collective-permute-start(bf16[256,128]{1,0:T(8,128)(2,1)S(1)} %get-tuple-element.63), channel_id=1, source_target_pairs={{0,1},{1,0},{2,3},{3,2},{4,5},{5,4},{6,7},{7,6},{8,9},{9,8},{10,11... | collective-permute-start | bytes 196616 | tf_op jit(solution)/shard_map/ppermute | solution.py:354
  21.6 0.7 stack.27.face_ref
  22.3 0.0 collective-permute-done.4.refs_5_.refs_9_
  22.3 0.0 collective-permute-done.3.refs_4_.refs_8_
  22.3 0.3 collective-permute-done.2.refs_3_.refs_7_
  22.6 0.0 collective-permute-done.1.refs_2_.refs_6_
  22.7 0.3 copy-done.2
  22.9 0.0 copy-done.3
  23.0 0.3 copy-done.4
  23.2 0.0 copy-done.5
  23.3 0.0 copy-done.6
  23.3 20.1 %edges.2 = (bf16[128,24576]{1,0:T(8,128)(2,1)}, f32[4096,128]{1,0:T(8,128)}, bf16[256,128]{1,0:T(8,128)(2,1)}, bf16[256,128]{1,0:T(8,128)(2,1)}, bf16[256,128]{1...) custom-call(s32[6]{0:T(128)} %stack.27.face_ref, ...), custom_call_target="tpu_custom_call" | custom-call | tf_op jit(solution)/shard_map/edges/pallas_call | solution.py:235
  43.4 5.9 %collective-permute-start.6 = (bf16[256,128]{1,0:T(8,128)(2,1)}, bf16[256,128]{1,0:T(8,128)(2,1)S(1)}, u32[]{:S(2)}, u32[]{:S(2)}) collective-permute-start(bf16[256,128]{1,0:T(8,128)(2,1)} %get-tuple-element.30), channel_id=1, source_target_pairs={{0,1},{1,0},{2,3},{3,2},{4,5},{5,4},{6,7},{7,6},{8,9},{9,8},{10,11... | collective-permute-start | bytes 196616 | tf_op jit(solution)/shard_map/ppermute | solution.py:354
  49.3 0.0 collective-permute-start.8
  49.3 3.5 %collective-permute-start.9 = (bf16[256,128]{1,0:T(8,128)(2,1)}, bf16[256,128]{1,0:T(8,128)(2,1)S(1)}, u32[]{:S(2)}, u32[]{:S(2)}) collective-permute-start(bf16[256,128]{1,0:T(8,128)(2,1)} %get-tuple-element.33), channel_id=1, source_target_pairs={{0,124},{1,125},{2,126},{3,127},{4,8},{5,9},{6,10},{7,11},{8,4},{9... | collective-permute-start | bytes 196616 | tf_op jit(solution)/shard_map/ppermute | solution.py:354
  52.7 0.0 collective-permute-done.6.refs_2_
  52.8 1.6 %collective-permute-start.11 = (bf16[256,128]{1,0:T(8,128)(2,1)}, bf16[256,128]{1,0:T(8,128)(2,1)S(1)}, u32[]{:S(2)}, u32[]{:S(2)}) collective-permute-start(bf16[256,128]{1,0:T(8,128)(2,1)} %get-tuple-element.35), channel_id=1, source_target_pairs={{0,112},{1,113},{2,114},{3,115},{4,116},{5,117},{6,118},{7,119},{8... | collective-permute-start | bytes 196616 | tf_op jit(solution)/shard_map/ppermute | solution.py:354
  54.4 0.0 collective-permute-done.7.refs_3_
  54.4 0.0 collective-permute-done.8.refs_4_
  54.4 4.4 %collective-permute-done.9.refs_5_ = bf16[256,128]{1,0:T(8,128)(2,1)S(1)} collective-permute-done((bf16[256,128]{1,0:T(8,128)(2,1)}, bf16[256,128]{1,0:T(8,128)(2,1)S(1)}, u32[]{:S(2)}, u32[]{:S(2)}) %collective-permute-start.9) | collective-permute-done | bytes 65568 | tf_op jit(solution)/shard_map/ppermute | solution.py:354
  58.8 1.0 collective-permute-done.11.refs_7_
  59.8 0.6 copy-done.24
  60.4 9.0 %nodes.2 = (f32[4096,128]{1,0:T(8,128)}, f32[128,2,128]{2,1,0:T(2,128)}, bf16[128,256]{1,0:T(8,128)(2,1)}, bf16[128,256]{1,0:T(8,128)(2,1)}, bf16[128,256]{1,0:T...) custom-call(bf16[4096,128]{1,0:T(8,128)(2,1)} %refs_0_.5, ...), custom_call_target="tpu_custom_call" | custom-call | tf_op jit(solution)/shard_map/nodes/pallas_call | solution.py:331
  69.4 8.7 %all-to-all-start = ((f32[128,2,128]{2,1,0:T(2,128)}), f32[128,2,128]{2,1,0:T(2,128)S(1)}, u32[]{:S(2)}, u32[]{:S(2)}) async-start(f32[128,2,128]{2,1,0:T(2,128)} %get-tuple-element.37), calls=%async_computation | async-start | bytes 262144 | tf_op jit(solution)/shard_map/all_to_all | solution.py:359
  78.1 1.1 collective-permute-start.12
  79.3 0.8 collective-permute-start.13
  80.1 2.9 %collective-permute-start.14 = (bf16[128,256]{1,0:T(8,128)(2,1)}, bf16[128,256]{1,0:T(8,128)(2,1)S(1)}, u32[]{:S(2)}, u32[]{:S(2)}) collective-permute-start(bf16[128,256]{1,0:T(8,128)(2,1)} %get-tuple-element.40), channel_id=1, source_target_pairs={{0,4},{1,5},{2,6},{3,7},{4,0},{5,1},{6,2},{7,3},{8,12},{9,13},{10,... | collective-permute-start | bytes 196616 | tf_op jit(solution)/shard_map/ppermute | solution.py:354
  83.0 4.5 %collective-permute-start.15 = (bf16[128,256]{1,0:T(8,128)(2,1)}, bf16[128,256]{1,0:T(8,128)(2,1)S(1)}, u32[]{:S(2)}, u32[]{:S(2)}) collective-permute-start(bf16[128,256]{1,0:T(8,128)(2,1)} %get-tuple-element.41), channel_id=1, source_target_pairs={{0,124},{1,125},{2,126},{3,127},{4,8},{5,9},{6,10},{7,11},{8,4},{9... | collective-permute-start | bytes 196616 | tf_op jit(solution)/shard_map/ppermute | solution.py:354
  87.5 0.4 all-to-all-done
  87.9 0.1 reduce_sum.18
  88.1 0.0 collective-permute-done.12.refs_11_
  88.1 2.9 %collective-permute-start.17 = (bf16[128,256]{1,0:T(8,128)(2,1)}, bf16[128,256]{1,0:T(8,128)(2,1)S(1)}, u32[]{:S(2)}, u32[]{:S(2)}) collective-permute-start(bf16[128,256]{1,0:T(8,128)(2,1)} %get-tuple-element.43), channel_id=1, source_target_pairs={{0,112},{1,113},{2,114},{3,115},{4,116},{5,117},{6,118},{7,119},{8... | collective-permute-start | bytes 196616 | tf_op jit(solution)/shard_map/ppermute | solution.py:354
  90.9 0.6 broadcast_multiply_fusion.1.refs_2_
  91.5 0.0 collective-permute-done.13.refs_12_
  91.5 0.0 collective-permute-done.14.refs_13_
  91.6 0.6 collective-permute-done.15.refs_14_
  92.1 0.5 collective-permute-done.16.refs_15_
  92.6 2.5 %collective-permute-done.17.refs_16_ = bf16[128,256]{1,0:T(8,128)(2,1)S(1)} collective-permute-done((bf16[128,256]{1,0:T(8,128)(2,1)}, bf16[128,256]{1,0:T(8,128)(2,1)S(1)}, u32[]{:S(2)}, u32[]{:S(2)}) %collective-permute-start.17) | collective-permute-done | bytes 65568 | tf_op jit(solution)/shard_map/ppermute | solution.py:354
  95.1 0.6 copy-done.17
  95.7 20.9 %edges.3 = (bf16[4096,128]{1,0:T(8,128)(2,1)}, bf16[24576,128]{1,0:T(8,128)(2,1)}, f32[4096,128]{1,0:T(8,128)}, bf16[256,128]{1,0:T(8,128)(2,1)}, bf16[256,128]{...) custom-call(s32[6]{0:T(128)} %stack.27.face_ref, ...), custom_call_target="tpu_custom_call" | custom-call | tf_op jit(solution)/shard_map/edges/pallas_call | solution.py:235
  116.6 0.0 copy-start.26
  116.6 0.0 copy-start.27
  116.6 0.0 copy-start
  116.7 3.8 %collective-permute-start.18 = (bf16[256,128]{1,0:T(8,128)(2,1)}, bf16[256,128]{1,0:T(8,128)(2,1)S(1)}, u32[]{:S(2)}, u32[]{:S(2)}) collective-permute-start(bf16[256,128]{1,0:T(8,128)(2,1)} %get-tuple-element.47), channel_id=1, source_target_pairs={{0,1},{1,0},{2,3},{3,2},{4,5},{5,4},{6,7},{7,6},{8,9},{9,8},{10,11... | collective-permute-start | bytes 196616 | tf_op jit(solution)/shard_map/ppermute | solution.py:354
  120.5 0.0 collective-permute-start.19
  120.5 0.3 collective-permute-start.20
  120.8 6.2 %collective-permute-start.21 = (bf16[256,128]{1,0:T(8,128)(2,1)}, bf16[256,128]{1,0:T(8,128)(2,1)S(1)}, u32[]{:S(2)}, u32[]{:S(2)}) collective-permute-start(bf16[256,128]{1,0:T(8,128)(2,1)} %get-tuple-element.50), channel_id=1, source_target_pairs={{0,124},{1,125},{2,126},{3,127},{4,8},{5,9},{6,10},{7,11},{8,4},{9... | collective-permute-start | bytes 196616 | tf_op jit(solution)/shard_map/ppermute | solution.py:354
  127.0 1.7 %collective-permute-start.23 = (bf16[256,128]{1,0:T(8,128)(2,1)}, bf16[256,128]{1,0:T(8,128)(2,1)S(1)}, u32[]{:S(2)}, u32[]{:S(2)}) collective-permute-start(bf16[256,128]{1,0:T(8,128)(2,1)} %get-tuple-element.52), channel_id=1, source_target_pairs={{0,112},{1,113},{2,114},{3,115},{4,116},{5,117},{6,118},{7,119},{8... | collective-permute-start | bytes 196616 | tf_op jit(solution)/shard_map/ppermute | solution.py:354
  128.7 1.2 collective-permute-done.21.refs_5_
  129.9 1.9 %collective-permute-done.22.refs_6_ = bf16[256,128]{1,0:T(8,128)(2,1)S(1)} collective-permute-done((bf16[256,128]{1,0:T(8,128)(2,1)}, bf16[256,128]{1,0:T(8,128)(2,1)S(1)}, u32[]{:S(2)}, u32[]{:S(2)}) %collective-permute-start.22) | collective-permute-done | bytes 65568 | tf_op jit(solution)/shard_map/ppermute | solution.py:354
  131.8 2.4 %collective-permute-done.23.refs_7_ = bf16[256,128]{1,0:T(8,128)(2,1)S(1)} collective-permute-done((bf16[256,128]{1,0:T(8,128)(2,1)}, bf16[256,128]{1,0:T(8,128)(2,1)S(1)}, u32[]{:S(2)}, u32[]{:S(2)}) %collective-permute-start.23) | collective-permute-done | bytes 65568 | tf_op jit(solution)/shard_map/ppermute | solution.py:354
  134.2 0.6 copy-done.25
  134.8 7.3 %nodes.3 = (f32[4096,128]{1,0:T(8,128)}, f32[128,2,128]{2,1,0:T(2,128)}) custom-call(bf16[4096,128]{1,0:T(8,128)(2,1)} %get-tuple-element.45.refs_0_, f32[4096,128]{1,0:T(8,128)} %get-tuple-element.46.refs_1_, bf16[256,128]{1,0:T(8,128)(2,1)} %copy-done.15, bf16[256,128]{1,0:T(8,128)(2,1)} %copy-done.18, bf16[256,128]{1,0:T(8,128)(2,1)} %copy-done.20, ...), custom_call_target="tpu_custom_call" | custom-call | tf_op jit(solution)/shard_map/nodes/pallas_call | solution.py:331
  142.1 17.1 %all_to_all.10 = f32[128,2,128]{2,1,0:T(2,128)S(1)} all-to-all(f32[128,2,128]{2,1,0:T(2,128)} %get-tuple-element.54), channel_id=1, replica_groups=mesh['blk'=128] {'blk'}, dimensions={0} | all-to-all | bytes 262144 | tf_op jit(solution)/shard_map/all_to_all | solution.py:359
  159.2 0.1 reduce_sum.19
  159.4 2.9 %add_convert_fusion = bf16[4096,128]{1,0:T(8,128)(2,1)} fusion(f32[4096,128]{1,0:T(8,128)} %get-tuple-element.53, bf16[4096,128]{1,0:T(8,128)(2,1)S(1)} %copy-done, f32[128]{0:T(128)S(1)} %get-tuple-element.56, f32[128]{0:T(128)S(1)} %bitcast.30), kind=kLoop, calls=%fused_computation.1 | loop fusion | flops 2621440 | bytes 4195328 | tf_op jit(solution)/shard_map/convert_element_type | solution.py:417
  (61 shorter events, 0.2 us)
Async XLA Ops:
  1.4 4.1 %copy-start.7 = (s32[6,256]{1,0:T(8,128)}, s32[6,256]{1,0:T(8,128)S(1)}, u32[]{:S(2)}) copy-start(s32[6,256]{1,0:T(8,128)S(1)} %concatenate.3.refs_8_) | copy-start | bytes 18436
  5.6 14.4 %collective-permute-start.5 = (bf16[256,128]{1,0:T(8,128)(2,1)S(1)}, bf16[256,128]{1,0:T(8,128)(2,1)S(1)}, u32[]{:S(2)}, u32[]{:S(2)}) collective-permute-start(bf16[256,128]{1,0:T(8,128)(2,1)S(1)} %get-tuple-element.58), channel_id=1, source_target_pairs={{0,112},{1,113},{2,114},{3,115},{4,116},{5,117},{6,118},{7,119},{8... | collective-permute-start | bytes 196616 | tf_op jit(solution)/shard_map/ppermute | solution.py:354
  11.7 10.7 %collective-permute-start.4 = (bf16[256,128]{1,0:T(8,128)(2,1)S(1)}, bf16[256,128]{1,0:T(8,128)(2,1)S(1)}, u32[]{:S(2)}, u32[]{:S(2)}) collective-permute-start(bf16[256,128]{1,0:T(8,128)(2,1)S(1)} %get-tuple-element.59), channel_id=1, source_target_pairs={{0,16},{1,17},{2,18},{3,19},{4,20},{5,21},{6,22},{7,23},{8,24},{9,... | collective-permute-start | bytes 196616 | tf_op jit(solution)/shard_map/ppermute | solution.py:354
  11.7 10.7 %collective-permute-start.3 = (bf16[256,128]{1,0:T(8,128)(2,1)S(1)}, bf16[256,128]{1,0:T(8,128)(2,1)S(1)}, u32[]{:S(2)}, u32[]{:S(2)}) collective-permute-start(bf16[256,128]{1,0:T(8,128)(2,1)S(1)} %get-tuple-element.60), channel_id=1, source_target_pairs={{0,124},{1,125},{2,126},{3,127},{4,8},{5,9},{6,10},{7,11},{8,4},{9... | collective-permute-start | bytes 196616 | tf_op jit(solution)/shard_map/ppermute | solution.py:354
  17.8 4.8 %collective-permute-start.2 = (bf16[256,128]{1,0:T(8,128)(2,1)S(1)}, bf16[256,128]{1,0:T(8,128)(2,1)S(1)}, u32[]{:S(2)}, u32[]{:S(2)}) collective-permute-start(bf16[256,128]{1,0:T(8,128)(2,1)S(1)} %get-tuple-element.61), channel_id=1, source_target_pairs={{0,4},{1,5},{2,6},{3,7},{4,0},{5,1},{6,2},{7,3},{8,12},{9,13},{10,... | collective-permute-start | bytes 196616 | tf_op jit(solution)/shard_map/ppermute | solution.py:354
  17.9 4.8 %collective-permute-start.1 = (bf16[256,128]{1,0:T(8,128)(2,1)S(1)}, bf16[256,128]{1,0:T(8,128)(2,1)S(1)}, u32[]{:S(2)}, u32[]{:S(2)}) collective-permute-start(bf16[256,128]{1,0:T(8,128)(2,1)S(1)} %get-tuple-element.62), channel_id=1, source_target_pairs={{0,127},{1,2},{2,1},{3,4},{4,3},{5,6},{6,5},{7,8},{8,7},{9,10},{10... | collective-permute-start | bytes 196616 | tf_op jit(solution)/shard_map/ppermute | solution.py:354
  20.0 2.7 %copy-start.1 = (bf16[256,128]{1,0:T(8,128)(2,1)}, bf16[256,128]{1,0:T(8,128)(2,1)S(1)}, u32[]{:S(2)}) copy-start(bf16[256,128]{1,0:T(8,128)(2,1)S(1)} %collective-permute-done.5.refs_6_.refs_10_) | copy-start | bytes 196612
  20.0 2.6 %collective-permute-start = (bf16[256,128]{1,0:T(8,128)(2,1)S(1)}, bf16[256,128]{1,0:T(8,128)(2,1)S(1)}, u32[]{:S(2)}, u32[]{:S(2)}) collective-permute-start(bf16[256,128]{1,0:T(8,128)(2,1)S(1)} %get-tuple-element.63), channel_id=1, source_target_pairs={{0,1},{1,0},{2,3},{3,2},{4,5},{5,4},{6,7},{7,6},{8,9},{9,8},{10,11... | collective-permute-start | bytes 196616 | tf_op jit(solution)/shard_map/ppermute | solution.py:354
  22.3 0.6 copy-start.2
  22.3 0.7 copy-start.3
  22.6 0.6 copy-start.4
  22.6 0.6 copy-start.5
  22.6 0.7 copy-start.6
  43.4 9.4 %collective-permute-start.6 = (bf16[256,128]{1,0:T(8,128)(2,1)}, bf16[256,128]{1,0:T(8,128)(2,1)S(1)}, u32[]{:S(2)}, u32[]{:S(2)}) collective-permute-start(bf16[256,128]{1,0:T(8,128)(2,1)} %get-tuple-element.30), channel_id=1, source_target_pairs={{0,1},{1,0},{2,3},{3,2},{4,5},{5,4},{6,7},{7,6},{8,9},{9,8},{10,11... | collective-permute-start | bytes 196616 | tf_op jit(solution)/shard_map/ppermute | solution.py:354
  49.3 5.1 %collective-permute-start.7 = (bf16[256,128]{1,0:T(8,128)(2,1)}, bf16[256,128]{1,0:T(8,128)(2,1)S(1)}, u32[]{:S(2)}, u32[]{:S(2)}) collective-permute-start(bf16[256,128]{1,0:T(8,128)(2,1)} %get-tuple-element.31), channel_id=1, source_target_pairs={{0,127},{1,2},{2,1},{3,4},{4,3},{5,6},{6,5},{7,8},{8,7},{9,10},{10... | collective-permute-start | bytes 196616 | tf_op jit(solution)/shard_map/ppermute | solution.py:354
  49.3 5.1 %collective-permute-start.8 = (bf16[256,128]{1,0:T(8,128)(2,1)}, bf16[256,128]{1,0:T(8,128)(2,1)S(1)}, u32[]{:S(2)}, u32[]{:S(2)}) collective-permute-start(bf16[256,128]{1,0:T(8,128)(2,1)} %get-tuple-element.32), channel_id=1, source_target_pairs={{0,4},{1,5},{2,6},{3,7},{4,0},{5,1},{6,2},{7,3},{8,12},{9,13},{10,... | collective-permute-start | bytes 196616 | tf_op jit(solution)/shard_map/ppermute | solution.py:354
  49.3 9.5 %collective-permute-start.9 = (bf16[256,128]{1,0:T(8,128)(2,1)}, bf16[256,128]{1,0:T(8,128)(2,1)S(1)}, u32[]{:S(2)}, u32[]{:S(2)}) collective-permute-start(bf16[256,128]{1,0:T(8,128)(2,1)} %get-tuple-element.33), channel_id=1, source_target_pairs={{0,124},{1,125},{2,126},{3,127},{4,8},{5,9},{6,10},{7,11},{8,4},{9... | collective-permute-start | bytes 196616 | tf_op jit(solution)/shard_map/ppermute | solution.py:354
  52.7 6.1 %collective-permute-start.10 = (bf16[256,128]{1,0:T(8,128)(2,1)}, bf16[256,128]{1,0:T(8,128)(2,1)S(1)}, u32[]{:S(2)}, u32[]{:S(2)}) collective-permute-start(bf16[256,128]{1,0:T(8,128)(2,1)} %get-tuple-element.34), channel_id=1, source_target_pairs={{0,16},{1,17},{2,18},{3,19},{4,20},{5,21},{6,22},{7,23},{8,24},{9,... | collective-permute-start | bytes 196616 | tf_op jit(solution)/shard_map/ppermute | solution.py:354
  52.7 7.0 %copy-start.13 = (bf16[256,128]{1,0:T(8,128)(2,1)}, bf16[256,128]{1,0:T(8,128)(2,1)S(1)}, u32[]{:S(2)}) copy-start(bf16[256,128]{1,0:T(8,128)(2,1)S(1)} %collective-permute-done.6.refs_2_) | copy-start | bytes 196612
  52.8 7.0 %collective-permute-start.11 = (bf16[256,128]{1,0:T(8,128)(2,1)}, bf16[256,128]{1,0:T(8,128)(2,1)S(1)}, u32[]{:S(2)}, u32[]{:S(2)}) collective-permute-start(bf16[256,128]{1,0:T(8,128)(2,1)} %get-tuple-element.35), channel_id=1, source_target_pairs={{0,112},{1,113},{2,114},{3,115},{4,116},{5,117},{6,118},{7,119},{8... | collective-permute-start | bytes 196616 | tf_op jit(solution)/shard_map/ppermute | solution.py:354
  54.4 5.4 %copy-start.14 = (bf16[256,128]{1,0:T(8,128)(2,1)}, bf16[256,128]{1,0:T(8,128)(2,1)S(1)}, u32[]{:S(2)}) copy-start(bf16[256,128]{1,0:T(8,128)(2,1)S(1)} %collective-permute-done.7.refs_3_) | copy-start | bytes 196612
  54.4 5.4 %copy-start.16 = (bf16[256,128]{1,0:T(8,128)(2,1)}, bf16[256,128]{1,0:T(8,128)(2,1)S(1)}, u32[]{:S(2)}) copy-start(bf16[256,128]{1,0:T(8,128)(2,1)S(1)} %collective-permute-done.8.refs_4_) | copy-start | bytes 196612
  58.8 1.0 copy-start.19
  58.8 1.0 copy-start.21
  59.8 0.6 copy-start.24
  69.4 18.5 %all-to-all-start = ((f32[128,2,128]{2,1,0:T(2,128)}), f32[128,2,128]{2,1,0:T(2,128)S(1)}, u32[]{:S(2)}, u32[]{:S(2)}) async-start(f32[128,2,128]{2,1,0:T(2,128)} %get-tuple-element.37), calls=%async_computation | async-start | bytes 262144 | tf_op jit(solution)/shard_map/all_to_all | solution.py:359
  78.1 10.0 %collective-permute-start.12 = (bf16[128,256]{1,0:T(8,128)(2,1)}, bf16[128,256]{1,0:T(8,128)(2,1)S(1)}, u32[]{:S(2)}, u32[]{:S(2)}) collective-permute-start(bf16[128,256]{1,0:T(8,128)(2,1)} %get-tuple-element.38), channel_id=1, source_target_pairs={{0,1},{1,0},{2,3},{3,2},{4,5},{5,4},{6,7},{7,6},{8,9},{9,8},{10,11... | collective-permute-start | bytes 196616 | tf_op jit(solution)/shard_map/ppermute | solution.py:354
  79.3 12.3 %collective-permute-start.13 = (bf16[128,256]{1,0:T(8,128)(2,1)}, bf16[128,256]{1,0:T(8,128)(2,1)S(1)}, u32[]{:S(2)}, u32[]{:S(2)}) collective-permute-start(bf16[128,256]{1,0:T(8,128)(2,1)} %get-tuple-element.39), channel_id=1, source_target_pairs={{0,127},{1,2},{2,1},{3,4},{4,3},{5,6},{6,5},{7,8},{8,7},{9,10},{10... | collective-permute-start | bytes 196616 | tf_op jit(solution)/shard_map/ppermute | solution.py:354
  80.1 11.5 %collective-permute-start.14 = (bf16[128,256]{1,0:T(8,128)(2,1)}, bf16[128,256]{1,0:T(8,128)(2,1)S(1)}, u32[]{:S(2)}, u32[]{:S(2)}) collective-permute-start(bf16[128,256]{1,0:T(8,128)(2,1)} %get-tuple-element.40), channel_id=1, source_target_pairs={{0,4},{1,5},{2,6},{3,7},{4,0},{5,1},{6,2},{7,3},{8,12},{9,13},{10,... | collective-permute-start | bytes 196616 | tf_op jit(solution)/shard_map/ppermute | solution.py:354
  83.0 9.2 %collective-permute-start.15 = (bf16[128,256]{1,0:T(8,128)(2,1)}, bf16[128,256]{1,0:T(8,128)(2,1)S(1)}, u32[]{:S(2)}, u32[]{:S(2)}) collective-permute-start(bf16[128,256]{1,0:T(8,128)(2,1)} %get-tuple-element.41), channel_id=1, source_target_pairs={{0,124},{1,125},{2,126},{3,127},{4,8},{5,9},{6,10},{7,11},{8,4},{9... | collective-permute-start | bytes 196616 | tf_op jit(solution)/shard_map/ppermute | solution.py:354
  87.5 5.1 %collective-permute-start.16 = (bf16[128,256]{1,0:T(8,128)(2,1)}, bf16[128,256]{1,0:T(8,128)(2,1)S(1)}, u32[]{:S(2)}, u32[]{:S(2)}) collective-permute-start(bf16[128,256]{1,0:T(8,128)(2,1)} %get-tuple-element.42), channel_id=1, source_target_pairs={{0,16},{1,17},{2,18},{3,19},{4,20},{5,21},{6,22},{7,23},{8,24},{9,... | collective-permute-start | bytes 196616 | tf_op jit(solution)/shard_map/ppermute | solution.py:354
  88.1 7.0 %copy-start.8 = (bf16[128,256]{1,0:T(8,128)(2,1)}, bf16[128,256]{1,0:T(8,128)(2,1)S(1)}, u32[]{:S(2)}) copy-start(bf16[128,256]{1,0:T(8,128)(2,1)S(1)} %collective-permute-done.12.refs_11_) | copy-start | bytes 196612
  88.1 7.0 %collective-permute-start.17 = (bf16[128,256]{1,0:T(8,128)(2,1)}, bf16[128,256]{1,0:T(8,128)(2,1)S(1)}, u32[]{:S(2)}, u32[]{:S(2)}) collective-permute-start(bf16[128,256]{1,0:T(8,128)(2,1)} %get-tuple-element.43), channel_id=1, source_target_pairs={{0,112},{1,113},{2,114},{3,115},{4,116},{5,117},{6,118},{7,119},{8... | collective-permute-start | bytes 196616 | tf_op jit(solution)/shard_map/ppermute | solution.py:354
  91.5 3.6 %copy-start.9 = (bf16[128,256]{1,0:T(8,128)(2,1)}, bf16[128,256]{1,0:T(8,128)(2,1)S(1)}, u32[]{:S(2)}) copy-start(bf16[128,256]{1,0:T(8,128)(2,1)S(1)} %collective-permute-done.13.refs_12_) | copy-start | bytes 196612
  91.5 3.6 %copy-start.10 = (bf16[128,256]{1,0:T(8,128)(2,1)}, bf16[128,256]{1,0:T(8,128)(2,1)S(1)}, u32[]{:S(2)}) copy-start(bf16[128,256]{1,0:T(8,128)(2,1)S(1)} %collective-permute-done.14.refs_13_) | copy-start | bytes 196612
  92.1 3.0 %copy-start.11 = (bf16[128,256]{1,0:T(8,128)(2,1)}, bf16[128,256]{1,0:T(8,128)(2,1)S(1)}, u32[]{:S(2)}) copy-start(bf16[128,256]{1,0:T(8,128)(2,1)S(1)} %collective-permute-done.15.refs_14_) | copy-start | bytes 196612
  92.6 2.5 %copy-start.12 = (bf16[128,256]{1,0:T(8,128)(2,1)}, bf16[128,256]{1,0:T(8,128)(2,1)S(1)}, u32[]{:S(2)}) copy-start(bf16[128,256]{1,0:T(8,128)(2,1)S(1)} %collective-permute-done.16.refs_15_) | copy-start | bytes 196612
  95.1 0.6 copy-start.17
  116.6 42.7 %copy-start.26 = (f32[2,128]{1,0:T(2,128)S(1)}, f32[2,128]{1,0:T(2,128)}, u32[]{:S(2)}) copy-start(f32[2,128]{1,0:T(2,128)} %refs_3_.1) | copy-start | bytes 3076
  116.6 42.7 %copy-start.27 = (f32[2,128]{1,0:T(2,128)S(1)}, f32[2,128]{1,0:T(2,128)}, u32[]{:S(2)}) copy-start(f32[2,128]{1,0:T(2,128)} %refs_4_.1) | copy-start | bytes 3076
  116.6 42.7 %copy-start = (bf16[4096,128]{1,0:T(8,128)(2,1)S(1)}, bf16[4096,128]{1,0:T(8,128)(2,1)}, u32[]{:S(2)}) copy-start(bf16[4096,128]{1,0:T(8,128)(2,1)} %get-tuple-element.45.refs_0_) | copy-start | bytes 3145732
  116.7 10.3 %collective-permute-start.18 = (bf16[256,128]{1,0:T(8,128)(2,1)}, bf16[256,128]{1,0:T(8,128)(2,1)S(1)}, u32[]{:S(2)}, u32[]{:S(2)}) collective-permute-start(bf16[256,128]{1,0:T(8,128)(2,1)} %get-tuple-element.47), channel_id=1, source_target_pairs={{0,1},{1,0},{2,3},{3,2},{4,5},{5,4},{6,7},{7,6},{8,9},{9,8},{10,11... | collective-permute-start | bytes 196616 | tf_op jit(solution)/shard_map/ppermute | solution.py:354
  120.5 8.2 %collective-permute-start.19 = (bf16[256,128]{1,0:T(8,128)(2,1)}, bf16[256,128]{1,0:T(8,128)(2,1)S(1)}, u32[]{:S(2)}, u32[]{:S(2)}) collective-permute-start(bf16[256,128]{1,0:T(8,128)(2,1)} %get-tuple-element.48), channel_id=1, source_target_pairs={{0,127},{1,2},{2,1},{3,4},{4,3},{5,6},{6,5},{7,8},{8,7},{9,10},{10... | collective-permute-start | bytes 196616 | tf_op jit(solution)/shard_map/ppermute | solution.py:354
  120.5 8.2 %collective-permute-start.20 = (bf16[256,128]{1,0:T(8,128)(2,1)}, bf16[256,128]{1,0:T(8,128)(2,1)S(1)}, u32[]{:S(2)}, u32[]{:S(2)}) collective-permute-start(bf16[256,128]{1,0:T(8,128)(2,1)} %get-tuple-element.49), channel_id=1, source_target_pairs={{0,4},{1,5},{2,6},{3,7},{4,0},{5,1},{6,2},{7,3},{8,12},{9,13},{10,... | collective-permute-start | bytes 196616 | tf_op jit(solution)/shard_map/ppermute | solution.py:354
  120.8 9.1 %collective-permute-start.21 = (bf16[256,128]{1,0:T(8,128)(2,1)}, bf16[256,128]{1,0:T(8,128)(2,1)S(1)}, u32[]{:S(2)}, u32[]{:S(2)}) collective-permute-start(bf16[256,128]{1,0:T(8,128)(2,1)} %get-tuple-element.50), channel_id=1, source_target_pairs={{0,124},{1,125},{2,126},{3,127},{4,8},{5,9},{6,10},{7,11},{8,4},{9... | collective-permute-start | bytes 196616 | tf_op jit(solution)/shard_map/ppermute | solution.py:354
  126.9 4.8 %collective-permute-start.22 = (bf16[256,128]{1,0:T(8,128)(2,1)}, bf16[256,128]{1,0:T(8,128)(2,1)S(1)}, u32[]{:S(2)}, u32[]{:S(2)}) collective-permute-start(bf16[256,128]{1,0:T(8,128)(2,1)} %get-tuple-element.51), channel_id=1, source_target_pairs={{0,16},{1,17},{2,18},{3,19},{4,20},{5,21},{6,22},{7,23},{8,24},{9,... | collective-permute-start | bytes 196616 | tf_op jit(solution)/shard_map/ppermute | solution.py:354
  127.0 7.2 %copy-start.15 = (bf16[256,128]{1,0:T(8,128)(2,1)}, bf16[256,128]{1,0:T(8,128)(2,1)S(1)}, u32[]{:S(2)}) copy-start(bf16[256,128]{1,0:T(8,128)(2,1)S(1)} %collective-permute-done.18.refs_2_) | copy-start | bytes 196612
  127.0 7.2 %collective-permute-start.23 = (bf16[256,128]{1,0:T(8,128)(2,1)}, bf16[256,128]{1,0:T(8,128)(2,1)S(1)}, u32[]{:S(2)}, u32[]{:S(2)}) collective-permute-start(bf16[256,128]{1,0:T(8,128)(2,1)} %get-tuple-element.52), channel_id=1, source_target_pairs={{0,112},{1,113},{2,114},{3,115},{4,116},{5,117},{6,118},{7,119},{8... | collective-permute-start | bytes 196616 | tf_op jit(solution)/shard_map/ppermute | solution.py:354
  128.6 5.5 %copy-start.18 = (bf16[256,128]{1,0:T(8,128)(2,1)}, bf16[256,128]{1,0:T(8,128)(2,1)S(1)}, u32[]{:S(2)}) copy-start(bf16[256,128]{1,0:T(8,128)(2,1)S(1)} %collective-permute-done.19.refs_3_) | copy-start | bytes 196612
  128.7 5.5 %copy-start.20 = (bf16[256,128]{1,0:T(8,128)(2,1)}, bf16[256,128]{1,0:T(8,128)(2,1)S(1)}, u32[]{:S(2)}) copy-start(bf16[256,128]{1,0:T(8,128)(2,1)S(1)} %collective-permute-done.20.refs_4_) | copy-start | bytes 196612
  129.9 4.3 %copy-start.22 = (bf16[256,128]{1,0:T(8,128)(2,1)}, bf16[256,128]{1,0:T(8,128)(2,1)S(1)}, u32[]{:S(2)}) copy-start(bf16[256,128]{1,0:T(8,128)(2,1)S(1)} %collective-permute-done.21.refs_5_) | copy-start | bytes 196612
  131.8 2.4 %copy-start.23 = (bf16[256,128]{1,0:T(8,128)(2,1)}, bf16[256,128]{1,0:T(8,128)(2,1)S(1)}, u32[]{:S(2)}) copy-start(bf16[256,128]{1,0:T(8,128)(2,1)S(1)} %collective-permute-done.22.refs_6_) | copy-start | bytes 196612
  134.2 0.6 copy-start.25

commit v3 on v2

--- a/solution.py
+++ b/solution.py
@@ -6,6 +6,7 @@
 from jax.experimental import pallas as pl
 from jax.experimental.pallas import tpu as pltpu
 from jax.sharding import PartitionSpec as P
+
 
 LAYERS = 2
 FACES = 6
@@ -112,7 +113,7 @@
     for g in range(GSTEP):
         hg = h_ref[g * TILE : (g + 1) * TILE, :]
         if moved:
-            up = upd_ref[g * TILE : (g + 1) * TILE, :]
+            up = upd_ref[g * TILE : (g + 1) * TILE, :].astype(F32)
             hg = (hg.astype(F32) + up * row_ref[0:1, :] + row_ref[1:2, :]).astype(BF)
             h_out[g * TILE : (g + 1) * TILE, :] = hg
         t = dot_nt(wsr_ref[...], hg)
@@ -173,7 +174,7 @@
                 new = jnp.concatenate(
                     [fresh[p, q][:, i * TILE : (i + 1) * TILE] for q in range(FACES)], axis=1
                 )
-                own_out[g * TILE : (g + 1) * TILE, :] = dot_nt(hot, new)
+                own_out[g * TILE : (g + 1) * TILE, :] = dot_nt(hot, new).astype(BF)
 
     units = [(p, k) for p in range(GSTEP // 2) for k in range(FACES)]
     parts = [(2 * p + i, j) for p in range(GSTEP // 2) for j in range(3) for i in range(2)]
@@ -228,7 +229,7 @@
         out_specs.append(rows)
     outs.append(jax.ShapeDtypeStruct((EDGES, C) if moved else (C, EDGES), BF))
     out_specs.append(by_edge if moved else by_lane)
-    outs.append(jax.ShapeDtypeStruct((NODES, C), F32))
+    outs.append(jax.ShapeDtypeStruct((NODES, C), BF))
     out_specs.append(rows)
     outs += [jax.ShapeDtypeStruct((HALO, C), BF)] * FACES
     out_specs += [full((HALO, C))] * FACES
@@ -282,7 +283,7 @@
     def gather(u):
         base = step * NSTEP * NB + u * NB
         hots[u] = [hot_rows((sidx_ref[k : k + 1, :] - base).astype(F32), NB) for k in range(FACES)]
-        total = own_ref[rows_of(u), :] + dot(jnp.concatenate(hots[u], axis=1), arrived)
+        total = own_ref[rows_of(u), :].astype(F32) + dot(jnp.concatenate(hots[u], axis=1), arrived)
         node_in[u] = jnp.concatenate([h_ref[rows_of(u), :], total.astype(BF)], axis=1)
 
     def first(u):
@@ -291,7 +292,7 @@
 
     def second(u):
         value = dot(hidden[u], w2_ref[0])
-        upd_ref[rows_of(u), :] = value
+        upd_ref[rows_of(u), :] = value.astype(BF)
         sums[0] = sums[0] + jnp.sum(value.reshape(NB // 8, 8, C), axis=0)
         sums[1] = sums[1] + jnp.sum((value * value).reshape(NB // 8, 8, C), axis=0)
         update[u] = value.astype(BF)
@@ -321,7 +322,7 @@
 def node_layer(layer, send, devices, h, own, returned, sidx, weights):
     rows = pl.BlockSpec((NSTEP * NB, C), lambda i: (i, 0))
     stats = (devices, 2, C)
-    outs = [jax.ShapeDtypeStruct((NODES, C), F32), jax.ShapeDtypeStruct(stats, F32)]
+    outs = [jax.ShapeDtypeStruct((NODES, C), BF), jax.ShapeDtypeStruct(stats, F32)]
     out_specs = [rows, full(stats)]
     scratch = []
     if send:
@@ -356,7 +357,8 @@
 
 
 def total_over(stats):
-    return jnp.sum(lax.all_to_all(stats, "blk", 0, 0), axis=0)
+    parts = lax.all_to_all(stats, "blk", 0, 0)
+    return jnp.sum(parts, axis=0)
 
 
 def per_device(
@@ -414,7 +416,7 @@
         totals = total_over(stats) / total_nodes
         extra = (update, totals, node_gain, node_shift)
     a, b = scale_shift(LAYERS - 1, totals, node_gain, node_shift)
-    out = (h.astype(F32) + update * a + b).astype(BF)
+    out = (h.astype(F32) + update.astype(F32) * a + b).astype(BF)
     return (out, e)
 
 

time: 163 us -> 161 us (0.988)
  no operation moved by 1% of the time
where the time goes in v3:
time: 161 us
  starting transfers between devices  60 us (37%)
  Pallas kernels  56.3 us (35%)
  blocking collectives  17.1 us (11%)
  waiting for transfers between devices  15.1 us (9%)
  local copies, waits for them, and re-layouts  7.25 us (5%)
  other arithmetic  4.31 us (3%)
    ppermute x24, starting transfers between devices, swap(): out.append(lax.ppermute(block, 'blk', pairs))  51.3 us
    pallas_call x2, Pallas kernels, edge_layer(): pl.pallas_call(functools.partial(edge_kernel, layer, moved), grid_spec=pl...  40.7 us
    all_to_all x1, blocking collectives, total_over(): parts = lax.all_to_all(stats, 'blk', 0, 0)  17.1 us
    pallas_call x2, Pallas kernels, node_layer(): pl.pallas_call(functools.partial(node_kernel, layer, send), grid=(NODES /...  15.6 us
    ppermute x24, waiting for transfers between devices, swap(): out.append(lax.ppermute(block, 'blk', pairs))  14.7 us
    all_to_all x1, starting transfers between devices, total_over(): parts = lax.all_to_all(stats, 'blk', 0, 0)  8.67 us
    gather x1, local copies, waits for them, and re-layouts, per_device(): rows = node_latent[sidx.reshape(-1)]  4 us
  transfers between devices with their start and end apart: 25, of which 10 were waited for; matrix products, arithmetic and copies ran while one was open for 1% of the time, Pallas kernels for 0%

profile of v3, /device:TPU:1, one launch (start us, length us, event | category | flops | bytes accessed | tf_op | source)
XLA Modules:
  0.0 161.1 jit_solution(16033490061579409306)
XLA Ops:
  0.6 0.8 fusion.6
  1.5 4.0 %gather_fusion = bf16[1536,128]{1,0:T(8,128)(2,1)S(1)} fusion(bf16[4096,128]{1,0:T(8,128)(2,1)} %refs_0_.5, s32[2048]{0:T(1024)S(1)} %pad_clamp_fusion), kind=kCustom, calls=%fused_computation | custom fusion | bytes 792576 | tf_op jit(solution)/shard_map/gather | solution.py:397
  5.6 6.1 %collective-permute-start.5 = (bf16[256,128]{1,0:T(8,128)(2,1)S(1)}, bf16[256,128]{1,0:T(8,128)(2,1)S(1)}, u32[]{:S(2)}, u32[]{:S(2)}) collective-permute-start(bf16[256,128]{1,0:T(8,128)(2,1)S(1)} %get-tuple-element.58), channel_id=1, source_target_pairs={{0,112},{1,113},{2,114},{3,115},{4,116},{5,117},{6,118},{7,119},{8... | collective-permute-start | bytes 196616 | tf_op jit(solution)/shard_map/ppermute | solution.py:355
  11.7 0.0 collective-permute-start.4
  11.7 6.2 %collective-permute-start.3 = (bf16[256,128]{1,0:T(8,128)(2,1)S(1)}, bf16[256,128]{1,0:T(8,128)(2,1)S(1)}, u32[]{:S(2)}, u32[]{:S(2)}) collective-permute-start(bf16[256,128]{1,0:T(8,128)(2,1)S(1)} %get-tuple-element.60), channel_id=1, source_target_pairs={{0,124},{1,125},{2,126},{3,127},{4,8},{5,9},{6,10},{7,11},{8,4},{9... | collective-permute-start | bytes 196616 | tf_op jit(solution)/shard_map/ppermute | solution.py:355
  17.9 0.0 collective-permute-start.2
  17.9 2.1 %collective-permute-start.1 = (bf16[256,128]{1,0:T(8,128)(2,1)S(1)}, bf16[256,128]{1,0:T(8,128)(2,1)S(1)}, u32[]{:S(2)}, u32[]{:S(2)}) collective-permute-start(bf16[256,128]{1,0:T(8,128)(2,1)S(1)} %get-tuple-element.62), channel_id=1, source_target_pairs={{0,127},{1,2},{2,1},{3,4},{4,3},{5,6},{6,5},{7,8},{8,7},{9,10},{10... | collective-permute-start | bytes 196616 | tf_op jit(solution)/shard_map/ppermute | solution.py:355
  20.0 0.0 collective-permute-done.5.refs_6_.refs_10_
  20.0 1.6 %collective-permute-start = (bf16[256,128]{1,0:T(8,128)(2,1)S(1)}, bf16[256,128]{1,0:T(8,128)(2,1)S(1)}, u32[]{:S(2)}, u32[]{:S(2)}) collective-permute-start(bf16[256,128]{1,0:T(8,128)(2,1)S(1)} %get-tuple-element.63), channel_id=1, source_target_pairs={{0,1},{1,0},{2,3},{3,2},{4,5},{5,4},{6,7},{7,6},{8,9},{9,8},{10,11... | collective-permute-start | bytes 196616 | tf_op jit(solution)/shard_map/ppermute | solution.py:355
  21.6 0.7 stack.27.face_ref
  22.3 0.0 collective-permute-done.4.refs_5_.refs_9_
  22.3 0.3 collective-permute-done.2.refs_3_.refs_7_
  22.6 0.0 collective-permute-done.1.refs_2_.refs_6_
  22.6 0.0 collective-permute-done.refs_1_.refs_5_
  22.7 0.3 copy-done.2
  22.9 0.0 copy-done.3
  23.0 0.3 copy-done.4
  23.2 0.0 copy-done.5
  23.3 0.0 copy-done.6
  23.3 20.0 %edges.2 = (bf16[128,24576]{1,0:T(8,128)(2,1)}, bf16[4096,128]{1,0:T(8,128)(2,1)}, bf16[256,128]{1,0:T(8,128)(2,1)}, bf16[256,128]{1,0:T(8,128)(2,1)}, bf16[256,...) custom-call(s32[6]{0:T(128)} %stack.27.face_ref, ...), custom_call_target="tpu_custom_call" | custom-call | tf_op jit(solution)/shard_map/edges/pallas_call | solution.py:236
  43.3 5.9 %collective-permute-start.6 = (bf16[256,128]{1,0:T(8,128)(2,1)}, bf16[256,128]{1,0:T(8,128)(2,1)S(1)}, u32[]{:S(2)}, u32[]{:S(2)}) collective-permute-start(bf16[256,128]{1,0:T(8,128)(2,1)} %get-tuple-element.30), channel_id=1, source_target_pairs={{0,1},{1,0},{2,3},{3,2},{4,5},{5,4},{6,7},{7,6},{8,9},{9,8},{10,11... | collective-permute-start | bytes 196616 | tf_op jit(solution)/shard_map/ppermute | solution.py:355
  49.2 0.0 collective-permute-start.8
  49.2 3.4 %collective-permute-start.9 = (bf16[256,128]{1,0:T(8,128)(2,1)}, bf16[256,128]{1,0:T(8,128)(2,1)S(1)}, u32[]{:S(2)}, u32[]{:S(2)}) collective-permute-start(bf16[256,128]{1,0:T(8,128)(2,1)} %get-tuple-element.33), channel_id=1, source_target_pairs={{0,124},{1,125},{2,126},{3,127},{4,8},{5,9},{6,10},{7,11},{8,4},{9... | collective-permute-start | bytes 196616 | tf_op jit(solution)/shard_map/ppermute | solution.py:355
  52.7 0.0 collective-permute-start.10
  52.7 0.0 collective-permute-done.6.refs_2_
  52.7 1.6 %collective-permute-start.11 = (bf16[256,128]{1,0:T(8,128)(2,1)}, bf16[256,128]{1,0:T(8,128)(2,1)S(1)}, u32[]{:S(2)}, u32[]{:S(2)}) collective-permute-start(bf16[256,128]{1,0:T(8,128)(2,1)} %get-tuple-element.35), channel_id=1, source_target_pairs={{0,112},{1,113},{2,114},{3,115},{4,116},{5,117},{6,118},{7,119},{8... | collective-permute-start | bytes 196616 | tf_op jit(solution)/shard_map/ppermute | solution.py:355
  54.3 4.4 %collective-permute-done.9.refs_5_ = bf16[256,128]{1,0:T(8,128)(2,1)S(1)} collective-permute-done((bf16[256,128]{1,0:T(8,128)(2,1)}, bf16[256,128]{1,0:T(8,128)(2,1)S(1)}, u32[]{:S(2)}, u32[]{:S(2)}) %collective-permute-start.9) | collective-permute-done | bytes 65568 | tf_op jit(solution)/shard_map/ppermute | solution.py:355
  58.8 0.0 collective-permute-done.10.refs_6_
  58.8 0.9 collective-permute-done.11.refs_7_
  59.7 0.6 copy-done.24
  60.3 8.7 %nodes.2 = (bf16[4096,128]{1,0:T(8,128)(2,1)}, f32[128,2,128]{2,1,0:T(2,128)}, bf16[128,256]{1,0:T(8,128)(2,1)}, bf16[128,256]{1,0:T(8,128)(2,1)}, bf16[128,256]...) custom-call(bf16[4096,128]{1,0:T(8,128)(2,1)} %refs_0_.5, ...), custom_call_target="tpu_custom_call" | custom-call | tf_op jit(solution)/shard_map/nodes/pallas_call | solution.py:332
  69.1 8.7 %all-to-all-start = ((f32[128,2,128]{2,1,0:T(2,128)}), f32[128,2,128]{2,1,0:T(2,128)S(1)}, u32[]{:S(2)}, u32[]{:S(2)}) async-start(f32[128,2,128]{2,1,0:T(2,128)} %get-tuple-element.37), calls=%async_computation | async-start | bytes 262144 | tf_op jit(solution)/shard_map/all_to_all | solution.py:360
  77.7 1.1 collective-permute-start.12
  78.9 0.8 collective-permute-start.13
  79.7 2.9 %collective-permute-start.14 = (bf16[128,256]{1,0:T(8,128)(2,1)}, bf16[128,256]{1,0:T(8,128)(2,1)S(1)}, u32[]{:S(2)}, u32[]{:S(2)}) collective-permute-start(bf16[128,256]{1,0:T(8,128)(2,1)} %get-tuple-element.40), channel_id=1, source_target_pairs={{0,4},{1,5},{2,6},{3,7},{4,0},{5,1},{6,2},{7,3},{8,12},{9,13},{10,... | collective-permute-start | bytes 196616 | tf_op jit(solution)/shard_map/ppermute | solution.py:355
  82.6 4.5 %collective-permute-start.15 = (bf16[128,256]{1,0:T(8,128)(2,1)}, bf16[128,256]{1,0:T(8,128)(2,1)S(1)}, u32[]{:S(2)}, u32[]{:S(2)}) collective-permute-start(bf16[128,256]{1,0:T(8,128)(2,1)} %get-tuple-element.41), channel_id=1, source_target_pairs={{0,124},{1,125},{2,126},{3,127},{4,8},{5,9},{6,10},{7,11},{8,4},{9... | collective-permute-start | bytes 196616 | tf_op jit(solution)/shard_map/ppermute | solution.py:355
  87.1 0.4 all-to-all-done
  87.5 0.1 reduce_sum.18
  87.7 0.0 collective-permute-done.12.refs_11_
  87.7 2.9 %collective-permute-start.17 = (bf16[128,256]{1,0:T(8,128)(2,1)}, bf16[128,256]{1,0:T(8,128)(2,1)S(1)}, u32[]{:S(2)}, u32[]{:S(2)}) collective-permute-start(bf16[128,256]{1,0:T(8,128)(2,1)} %get-tuple-element.43), channel_id=1, source_target_pairs={{0,112},{1,113},{2,114},{3,115},{4,116},{5,117},{6,118},{7,119},{8... | collective-permute-start | bytes 196616 | tf_op jit(solution)/shard_map/ppermute | solution.py:355
  90.6 0.6 broadcast_multiply_fusion.1.refs_2_
  91.2 0.0 collective-permute-done.13.refs_12_
  91.2 0.6 collective-permute-done.15.refs_14_
  91.8 0.5 collective-permute-done.16.refs_15_
  92.3 2.5 %collective-permute-done.17.refs_16_ = bf16[128,256]{1,0:T(8,128)(2,1)S(1)} collective-permute-done((bf16[128,256]{1,0:T(8,128)(2,1)}, bf16[128,256]{1,0:T(8,128)(2,1)S(1)}, u32[]{:S(2)}, u32[]{:S(2)}) %collective-permute-start.17) | collective-permute-done | bytes 65568 | tf_op jit(solution)/shard_map/ppermute | solution.py:355
  94.8 0.6 copy-done.13
  95.4 20.7 %edges.3 = (bf16[4096,128]{1,0:T(8,128)(2,1)}, bf16[24576,128]{1,0:T(8,128)(2,1)}, bf16[4096,128]{1,0:T(8,128)(2,1)}, bf16[256,128]{1,0:T(8,128)(2,1)}, bf16[256...) custom-call(s32[6]{0:T(128)} %stack.27.face_ref, ...), custom_call_target="tpu_custom_call" | custom-call | tf_op jit(solution)/shard_map/edges/pallas_call | solution.py:236
  116.1 0.0 copy-start.26
  116.1 0.0 copy-start.27
  116.1 0.0 copy-start
  116.1 3.8 %collective-permute-start.18 = (bf16[256,128]{1,0:T(8,128)(2,1)}, bf16[256,128]{1,0:T(8,128)(2,1)S(1)}, u32[]{:S(2)}, u32[]{:S(2)}) collective-permute-start(bf16[256,128]{1,0:T(8,128)(2,1)} %get-tuple-element.47), channel_id=1, source_target_pairs={{0,1},{1,0},{2,3},{3,2},{4,5},{5,4},{6,7},{7,6},{8,9},{9,8},{10,11... | collective-permute-start | bytes 196616 | tf_op jit(solution)/shard_map/ppermute | solution.py:355
  119.9 0.0 collective-permute-start.19
  119.9 0.3 collective-permute-start.20
  120.2 6.2 %collective-permute-start.21 = (bf16[256,128]{1,0:T(8,128)(2,1)}, bf16[256,128]{1,0:T(8,128)(2,1)S(1)}, u32[]{:S(2)}, u32[]{:S(2)}) collective-permute-start(bf16[256,128]{1,0:T(8,128)(2,1)} %get-tuple-element.50), channel_id=1, source_target_pairs={{0,124},{1,125},{2,126},{3,127},{4,8},{5,9},{6,10},{7,11},{8,4},{9... | collective-permute-start | bytes 196616 | tf_op jit(solution)/shard_map/ppermute | solution.py:355
  126.4 1.7 %collective-permute-start.23 = (bf16[256,128]{1,0:T(8,128)(2,1)}, bf16[256,128]{1,0:T(8,128)(2,1)S(1)}, u32[]{:S(2)}, u32[]{:S(2)}) collective-permute-start(bf16[256,128]{1,0:T(8,128)(2,1)} %get-tuple-element.52), channel_id=1, source_target_pairs={{0,112},{1,113},{2,114},{3,115},{4,116},{5,117},{6,118},{7,119},{8... | collective-permute-start | bytes 196616 | tf_op jit(solution)/shard_map/ppermute | solution.py:355
  128.1 0.0 collective-permute-done.20.refs_4_
  128.1 1.3 collective-permute-done.21.refs_5_
  129.4 2.2 %collective-permute-done.22.refs_6_ = bf16[256,128]{1,0:T(8,128)(2,1)S(1)} collective-permute-done((bf16[256,128]{1,0:T(8,128)(2,1)}, bf16[256,128]{1,0:T(8,128)(2,1)S(1)}, u32[]{:S(2)}, u32[]{:S(2)}) %collective-permute-start.22) | collective-permute-done | bytes 65568 | tf_op jit(solution)/shard_map/ppermute | solution.py:355
  131.5 2.1 %collective-permute-done.23.refs_7_ = bf16[256,128]{1,0:T(8,128)(2,1)S(1)} collective-permute-done((bf16[256,128]{1,0:T(8,128)(2,1)}, bf16[256,128]{1,0:T(8,128)(2,1)S(1)}, u32[]{:S(2)}, u32[]{:S(2)}) %collective-permute-start.23) | collective-permute-done | bytes 65568 | tf_op jit(solution)/shard_map/ppermute | solution.py:355
  133.7 0.6 copy-done.25
  134.2 6.9 %nodes.3 = (bf16[4096,128]{1,0:T(8,128)(2,1)}, f32[128,2,128]{2,1,0:T(2,128)}) custom-call(bf16[4096,128]{1,0:T(8,128)(2,1)} %get-tuple-element.45.refs_0_, bf16[4096,128]{1,0:T(8,128)(2,1)} %get-tuple-element.46.refs_1_, bf16[256,128]{1,0:T(8,128)(2,1)} %copy-done.16, bf16[256,128]{1,0:T(8,128)(2,1)} %copy-done.18, bf16[256,128]{1,0:T(8,128)(2,1)} %copy-done.20, ...), custom_call_target="tpu_custom_call" | custom-call | tf_op jit(solution)/shard_map/nodes/pallas_call | solution.py:332
  141.2 17.1 %all_to_all.10 = f32[128,2,128]{2,1,0:T(2,128)S(1)} all-to-all(f32[128,2,128]{2,1,0:T(2,128)} %get-tuple-element.54), channel_id=1, replica_groups=mesh['blk'=128] {'blk'}, dimensions={0} | all-to-all | bytes 262144 | tf_op jit(solution)/shard_map/all_to_all | solution.py:360
  158.3 0.1 reduce_sum.19
  158.5 2.6 %add_convert_fusion = bf16[4096,128]{1,0:T(8,128)(2,1)} fusion(bf16[4096,128]{1,0:T(8,128)(2,1)} %get-tuple-element.53, bf16[4096,128]{1,0:T(8,128)(2,1)S(1)} %copy-done, f32[128]{0:T(128)S(1)} %get-tuple-element.56, f32[128]{0:T(128)S(1)} %bitcast.30), kind=kLoop, calls=%fused_computation.1 | loop fusion | flops 3145728 | bytes 3146752 | tf_op jit(solution)/shard_map/convert_element_type | solution.py:419
  (61 shorter events, 0.2 us)
Async XLA Ops:
  1.4 4.1 %copy-start.7 = (s32[6,256]{1,0:T(8,128)}, s32[6,256]{1,0:T(8,128)S(1)}, u32[]{:S(2)}) copy-start(s32[6,256]{1,0:T(8,128)S(1)} %concatenate.3.refs_8_) | copy-start | bytes 18436
  5.6 14.4 %collective-permute-start.5 = (bf16[256,128]{1,0:T(8,128)(2,1)S(1)}, bf16[256,128]{1,0:T(8,128)(2,1)S(1)}, u32[]{:S(2)}, u32[]{:S(2)}) collective-permute-start(bf16[256,128]{1,0:T(8,128)(2,1)S(1)} %get-tuple-element.58), channel_id=1, source_target_pairs={{0,112},{1,113},{2,114},{3,115},{4,116},{5,117},{6,118},{7,119},{8... | collective-permute-start | bytes 196616 | tf_op jit(solution)/shard_map/ppermute | solution.py:355
  11.7 10.7 %collective-permute-start.4 = (bf16[256,128]{1,0:T(8,128)(2,1)S(1)}, bf16[256,128]{1,0:T(8,128)(2,1)S(1)}, u32[]{:S(2)}, u32[]{:S(2)}) collective-permute-start(bf16[256,128]{1,0:T(8,128)(2,1)S(1)} %get-tuple-element.59), channel_id=1, source_target_pairs={{0,16},{1,17},{2,18},{3,19},{4,20},{5,21},{6,22},{7,23},{8,24},{9,... | collective-permute-start | bytes 196616 | tf_op jit(solution)/shard_map/ppermute | solution.py:355
  11.7 10.7 %collective-permute-start.3 = (bf16[256,128]{1,0:T(8,128)(2,1)S(1)}, bf16[256,128]{1,0:T(8,128)(2,1)S(1)}, u32[]{:S(2)}, u32[]{:S(2)}) collective-permute-start(bf16[256,128]{1,0:T(8,128)(2,1)S(1)} %get-tuple-element.60), channel_id=1, source_target_pairs={{0,124},{1,125},{2,126},{3,127},{4,8},{5,9},{6,10},{7,11},{8,4},{9... | collective-permute-start | bytes 196616 | tf_op jit(solution)/shard_map/ppermute | solution.py:355
  17.9 4.8 %collective-permute-start.2 = (bf16[256,128]{1,0:T(8,128)(2,1)S(1)}, bf16[256,128]{1,0:T(8,128)(2,1)S(1)}, u32[]{:S(2)}, u32[]{:S(2)}) collective-permute-start(bf16[256,128]{1,0:T(8,128)(2,1)S(1)} %get-tuple-element.61), channel_id=1, source_target_pairs={{0,4},{1,5},{2,6},{3,7},{4,0},{5,1},{6,2},{7,3},{8,12},{9,13},{10,... | collective-permute-start | bytes 196616 | tf_op jit(solution)/shard_map/ppermute | solution.py:355
  17.9 4.8 %collective-permute-start.1 = (bf16[256,128]{1,0:T(8,128)(2,1)S(1)}, bf16[256,128]{1,0:T(8,128)(2,1)S(1)}, u32[]{:S(2)}, u32[]{:S(2)}) collective-permute-start(bf16[256,128]{1,0:T(8,128)(2,1)S(1)} %get-tuple-element.62), channel_id=1, source_target_pairs={{0,127},{1,2},{2,1},{3,4},{4,3},{5,6},{6,5},{7,8},{8,7},{9,10},{10... | collective-permute-start | bytes 196616 | tf_op jit(solution)/shard_map/ppermute | solution.py:355
  20.0 2.7 %copy-start.1 = (bf16[256,128]{1,0:T(8,128)(2,1)}, bf16[256,128]{1,0:T(8,128)(2,1)S(1)}, u32[]{:S(2)}) copy-start(bf16[256,128]{1,0:T(8,128)(2,1)S(1)} %collective-permute-done.5.refs_6_.refs_10_) | copy-start | bytes 196612
  20.0 2.6 %collective-permute-start = (bf16[256,128]{1,0:T(8,128)(2,1)S(1)}, bf16[256,128]{1,0:T(8,128)(2,1)S(1)}, u32[]{:S(2)}, u32[]{:S(2)}) collective-permute-start(bf16[256,128]{1,0:T(8,128)(2,1)S(1)} %get-tuple-element.63), channel_id=1, source_target_pairs={{0,1},{1,0},{2,3},{3,2},{4,5},{5,4},{6,7},{7,6},{8,9},{9,8},{10,11... | collective-permute-start | bytes 196616 | tf_op jit(solution)/shard_map/ppermute | solution.py:355
  22.3 0.6 copy-start.2
  22.3 0.7 copy-start.3
  22.6 0.6 copy-start.4
  22.6 0.6 copy-start.5
  22.6 0.7 copy-start.6
  43.3 9.4 %collective-permute-start.6 = (bf16[256,128]{1,0:T(8,128)(2,1)}, bf16[256,128]{1,0:T(8,128)(2,1)S(1)}, u32[]{:S(2)}, u32[]{:S(2)}) collective-permute-start(bf16[256,128]{1,0:T(8,128)(2,1)} %get-tuple-element.30), channel_id=1, source_target_pairs={{0,1},{1,0},{2,3},{3,2},{4,5},{5,4},{6,7},{7,6},{8,9},{9,8},{10,11... | collective-permute-start | bytes 196616 | tf_op jit(solution)/shard_map/ppermute | solution.py:355
  49.2 5.1 %collective-permute-start.7 = (bf16[256,128]{1,0:T(8,128)(2,1)}, bf16[256,128]{1,0:T(8,128)(2,1)S(1)}, u32[]{:S(2)}, u32[]{:S(2)}) collective-permute-start(bf16[256,128]{1,0:T(8,128)(2,1)} %get-tuple-element.31), channel_id=1, source_target_pairs={{0,127},{1,2},{2,1},{3,4},{4,3},{5,6},{6,5},{7,8},{8,7},{9,10},{10... | collective-permute-start | bytes 196616 | tf_op jit(solution)/shard_map/ppermute | solution.py:355
  49.2 5.1 %collective-permute-start.8 = (bf16[256,128]{1,0:T(8,128)(2,1)}, bf16[256,128]{1,0:T(8,128)(2,1)S(1)}, u32[]{:S(2)}, u32[]{:S(2)}) collective-permute-start(bf16[256,128]{1,0:T(8,128)(2,1)} %get-tuple-element.32), channel_id=1, source_target_pairs={{0,4},{1,5},{2,6},{3,7},{4,0},{5,1},{6,2},{7,3},{8,12},{9,13},{10,... | collective-permute-start | bytes 196616 | tf_op jit(solution)/shard_map/ppermute | solution.py:355
  49.2 9.5 %collective-permute-start.9 = (bf16[256,128]{1,0:T(8,128)(2,1)}, bf16[256,128]{1,0:T(8,128)(2,1)S(1)}, u32[]{:S(2)}, u32[]{:S(2)}) collective-permute-start(bf16[256,128]{1,0:T(8,128)(2,1)} %get-tuple-element.33), channel_id=1, source_target_pairs={{0,124},{1,125},{2,126},{3,127},{4,8},{5,9},{6,10},{7,11},{8,4},{9... | collective-permute-start | bytes 196616 | tf_op jit(solution)/shard_map/ppermute | solution.py:355
  52.7 6.1 %collective-permute-start.10 = (bf16[256,128]{1,0:T(8,128)(2,1)}, bf16[256,128]{1,0:T(8,128)(2,1)S(1)}, u32[]{:S(2)}, u32[]{:S(2)}) collective-permute-start(bf16[256,128]{1,0:T(8,128)(2,1)} %get-tuple-element.34), channel_id=1, source_target_pairs={{0,16},{1,17},{2,18},{3,19},{4,20},{5,21},{6,22},{7,23},{8,24},{9,... | collective-permute-start | bytes 196616 | tf_op jit(solution)/shard_map/ppermute | solution.py:355
  52.7 7.0 %copy-start.14 = (bf16[256,128]{1,0:T(8,128)(2,1)}, bf16[256,128]{1,0:T(8,128)(2,1)S(1)}, u32[]{:S(2)}) copy-start(bf16[256,128]{1,0:T(8,128)(2,1)S(1)} %collective-permute-done.6.refs_2_) | copy-start | bytes 196612
  52.7 7.0 %collective-permute-start.11 = (bf16[256,128]{1,0:T(8,128)(2,1)}, bf16[256,128]{1,0:T(8,128)(2,1)S(1)}, u32[]{:S(2)}, u32[]{:S(2)}) collective-permute-start(bf16[256,128]{1,0:T(8,128)(2,1)} %get-tuple-element.35), channel_id=1, source_target_pairs={{0,112},{1,113},{2,114},{3,115},{4,116},{5,117},{6,118},{7,119},{8... | collective-permute-start | bytes 196616 | tf_op jit(solution)/shard_map/ppermute | solution.py:355
  54.3 5.4 %copy-start.15 = (bf16[256,128]{1,0:T(8,128)(2,1)}, bf16[256,128]{1,0:T(8,128)(2,1)S(1)}, u32[]{:S(2)}) copy-start(bf16[256,128]{1,0:T(8,128)(2,1)S(1)} %collective-permute-done.7.refs_3_) | copy-start | bytes 196612
  54.3 5.4 %copy-start.17 = (bf16[256,128]{1,0:T(8,128)(2,1)}, bf16[256,128]{1,0:T(8,128)(2,1)S(1)}, u32[]{:S(2)}) copy-start(bf16[256,128]{1,0:T(8,128)(2,1)S(1)} %collective-permute-done.8.refs_4_) | copy-start | bytes 196612
  58.8 1.0 copy-start.19
  58.8 1.0 copy-start.21
  59.7 0.6 copy-start.24
  69.1 18.5 %all-to-all-start = ((f32[128,2,128]{2,1,0:T(2,128)}), f32[128,2,128]{2,1,0:T(2,128)S(1)}, u32[]{:S(2)}, u32[]{:S(2)}) async-start(f32[128,2,128]{2,1,0:T(2,128)} %get-tuple-element.37), calls=%async_computation | async-start | bytes 262144 | tf_op jit(solution)/shard_map/all_to_all | solution.py:360
  77.7 10.0 %collective-permute-start.12 = (bf16[128,256]{1,0:T(8,128)(2,1)}, bf16[128,256]{1,0:T(8,128)(2,1)S(1)}, u32[]{:S(2)}, u32[]{:S(2)}) collective-permute-start(bf16[128,256]{1,0:T(8,128)(2,1)} %get-tuple-element.38), channel_id=1, source_target_pairs={{0,1},{1,0},{2,3},{3,2},{4,5},{5,4},{6,7},{7,6},{8,9},{9,8},{10,11... | collective-permute-start | bytes 196616 | tf_op jit(solution)/shard_map/ppermute | solution.py:355
  78.9 12.3 %collective-permute-start.13 = (bf16[128,256]{1,0:T(8,128)(2,1)}, bf16[128,256]{1,0:T(8,128)(2,1)S(1)}, u32[]{:S(2)}, u32[]{:S(2)}) collective-permute-start(bf16[128,256]{1,0:T(8,128)(2,1)} %get-tuple-element.39), channel_id=1, source_target_pairs={{0,127},{1,2},{2,1},{3,4},{4,3},{5,6},{6,5},{7,8},{8,7},{9,10},{10... | collective-permute-start | bytes 196616 | tf_op jit(solution)/shard_map/ppermute | solution.py:355
  79.7 11.5 %collective-permute-start.14 = (bf16[128,256]{1,0:T(8,128)(2,1)}, bf16[128,256]{1,0:T(8,128)(2,1)S(1)}, u32[]{:S(2)}, u32[]{:S(2)}) collective-permute-start(bf16[128,256]{1,0:T(8,128)(2,1)} %get-tuple-element.40), channel_id=1, source_target_pairs={{0,4},{1,5},{2,6},{3,7},{4,0},{5,1},{6,2},{7,3},{8,12},{9,13},{10,... | collective-permute-start | bytes 196616 | tf_op jit(solution)/shard_map/ppermute | solution.py:355
  82.6 9.2 %collective-permute-start.15 = (bf16[128,256]{1,0:T(8,128)(2,1)}, bf16[128,256]{1,0:T(8,128)(2,1)S(1)}, u32[]{:S(2)}, u32[]{:S(2)}) collective-permute-start(bf16[128,256]{1,0:T(8,128)(2,1)} %get-tuple-element.41), channel_id=1, source_target_pairs={{0,124},{1,125},{2,126},{3,127},{4,8},{5,9},{6,10},{7,11},{8,4},{9... | collective-permute-start | bytes 196616 | tf_op jit(solution)/shard_map/ppermute | solution.py:355
  87.1 5.1 %collective-permute-start.16 = (bf16[128,256]{1,0:T(8,128)(2,1)}, bf16[128,256]{1,0:T(8,128)(2,1)S(1)}, u32[]{:S(2)}, u32[]{:S(2)}) collective-permute-start(bf16[128,256]{1,0:T(8,128)(2,1)} %get-tuple-element.42), channel_id=1, source_target_pairs={{0,16},{1,17},{2,18},{3,19},{4,20},{5,21},{6,22},{7,23},{8,24},{9,... | collective-permute-start | bytes 196616 | tf_op jit(solution)/shard_map/ppermute | solution.py:355
  87.7 7.0 %copy-start.8 = (bf16[128,256]{1,0:T(8,128)(2,1)}, bf16[128,256]{1,0:T(8,128)(2,1)S(1)}, u32[]{:S(2)}) copy-start(bf16[128,256]{1,0:T(8,128)(2,1)S(1)} %collective-permute-done.12.refs_11_) | copy-start | bytes 196612
  87.7 7.0 %collective-permute-start.17 = (bf16[128,256]{1,0:T(8,128)(2,1)}, bf16[128,256]{1,0:T(8,128)(2,1)S(1)}, u32[]{:S(2)}, u32[]{:S(2)}) collective-permute-start(bf16[128,256]{1,0:T(8,128)(2,1)} %get-tuple-element.43), channel_id=1, source_target_pairs={{0,112},{1,113},{2,114},{3,115},{4,116},{5,117},{6,118},{7,119},{8... | collective-permute-start | bytes 196616 | tf_op jit(solution)/shard_map/ppermute | solution.py:355
  91.2 3.6 %copy-start.9 = (bf16[128,256]{1,0:T(8,128)(2,1)}, bf16[128,256]{1,0:T(8,128)(2,1)S(1)}, u32[]{:S(2)}) copy-start(bf16[128,256]{1,0:T(8,128)(2,1)S(1)} %collective-permute-done.13.refs_12_) | copy-start | bytes 196612
  91.2 3.6 %copy-start.10 = (bf16[128,256]{1,0:T(8,128)(2,1)}, bf16[128,256]{1,0:T(8,128)(2,1)S(1)}, u32[]{:S(2)}) copy-start(bf16[128,256]{1,0:T(8,128)(2,1)S(1)} %collective-permute-done.14.refs_13_) | copy-start | bytes 196612
  91.8 3.0 %copy-start.11 = (bf16[128,256]{1,0:T(8,128)(2,1)}, bf16[128,256]{1,0:T(8,128)(2,1)S(1)}, u32[]{:S(2)}) copy-start(bf16[128,256]{1,0:T(8,128)(2,1)S(1)} %collective-permute-done.15.refs_14_) | copy-start | bytes 196612
  92.3 2.5 %copy-start.12 = (bf16[128,256]{1,0:T(8,128)(2,1)}, bf16[128,256]{1,0:T(8,128)(2,1)S(1)}, u32[]{:S(2)}) copy-start(bf16[128,256]{1,0:T(8,128)(2,1)S(1)} %collective-permute-done.16.refs_15_) | copy-start | bytes 196612
  94.7 0.6 copy-start.13
  116.1 42.4 %copy-start.26 = (f32[2,128]{1,0:T(2,128)S(1)}, f32[2,128]{1,0:T(2,128)}, u32[]{:S(2)}) copy-start(f32[2,128]{1,0:T(2,128)} %refs_3_.1) | copy-start | bytes 3076
  116.1 42.4 %copy-start.27 = (f32[2,128]{1,0:T(2,128)S(1)}, f32[2,128]{1,0:T(2,128)}, u32[]{:S(2)}) copy-start(f32[2,128]{1,0:T(2,128)} %refs_4_.1) | copy-start | bytes 3076
  116.1 42.4 %copy-start = (bf16[4096,128]{1,0:T(8,128)(2,1)S(1)}, bf16[4096,128]{1,0:T(8,128)(2,1)}, u32[]{:S(2)}) copy-start(bf16[4096,128]{1,0:T(8,128)(2,1)} %get-tuple-element.45.refs_0_) | copy-start | bytes 3145732
  116.1 10.3 %collective-permute-start.18 = (bf16[256,128]{1,0:T(8,128)(2,1)}, bf16[256,128]{1,0:T(8,128)(2,1)S(1)}, u32[]{:S(2)}, u32[]{:S(2)}) collective-permute-start(bf16[256,128]{1,0:T(8,128)(2,1)} %get-tuple-element.47), channel_id=1, source_target_pairs={{0,1},{1,0},{2,3},{3,2},{4,5},{5,4},{6,7},{7,6},{8,9},{9,8},{10,11... | collective-permute-start | bytes 196616 | tf_op jit(solution)/shard_map/ppermute | solution.py:355
  119.9 8.2 %collective-permute-start.19 = (bf16[256,128]{1,0:T(8,128)(2,1)}, bf16[256,128]{1,0:T(8,128)(2,1)S(1)}, u32[]{:S(2)}, u32[]{:S(2)}) collective-permute-start(bf16[256,128]{1,0:T(8,128)(2,1)} %get-tuple-element.48), channel_id=1, source_target_pairs={{0,127},{1,2},{2,1},{3,4},{4,3},{5,6},{6,5},{7,8},{8,7},{9,10},{10... | collective-permute-start | bytes 196616 | tf_op jit(solution)/shard_map/ppermute | solution.py:355
  119.9 8.2 %collective-permute-start.20 = (bf16[256,128]{1,0:T(8,128)(2,1)}, bf16[256,128]{1,0:T(8,128)(2,1)S(1)}, u32[]{:S(2)}, u32[]{:S(2)}) collective-permute-start(bf16[256,128]{1,0:T(8,128)(2,1)} %get-tuple-element.49), channel_id=1, source_target_pairs={{0,4},{1,5},{2,6},{3,7},{4,0},{5,1},{6,2},{7,3},{8,12},{9,13},{10,... | collective-permute-start | bytes 196616 | tf_op jit(solution)/shard_map/ppermute | solution.py:355
  120.2 9.1 %collective-permute-start.21 = (bf16[256,128]{1,0:T(8,128)(2,1)}, bf16[256,128]{1,0:T(8,128)(2,1)S(1)}, u32[]{:S(2)}, u32[]{:S(2)}) collective-permute-start(bf16[256,128]{1,0:T(8,128)(2,1)} %get-tuple-element.50), channel_id=1, source_target_pairs={{0,124},{1,125},{2,126},{3,127},{4,8},{5,9},{6,10},{7,11},{8,4},{9... | collective-permute-start | bytes 196616 | tf_op jit(solution)/shard_map/ppermute | solution.py:355
  126.4 5.1 %collective-permute-start.22 = (bf16[256,128]{1,0:T(8,128)(2,1)}, bf16[256,128]{1,0:T(8,128)(2,1)S(1)}, u32[]{:S(2)}, u32[]{:S(2)}) collective-permute-start(bf16[256,128]{1,0:T(8,128)(2,1)} %get-tuple-element.51), channel_id=1, source_target_pairs={{0,16},{1,17},{2,18},{3,19},{4,20},{5,21},{6,22},{7,23},{8,24},{9,... | collective-permute-start | bytes 196616 | tf_op jit(solution)/shard_map/ppermute | solution.py:355
  126.4 7.2 %copy-start.16 = (bf16[256,128]{1,0:T(8,128)(2,1)}, bf16[256,128]{1,0:T(8,128)(2,1)S(1)}, u32[]{:S(2)}) copy-start(bf16[256,128]{1,0:T(8,128)(2,1)S(1)} %collective-permute-done.18.refs_2_) | copy-start | bytes 196612
  126.4 7.2 %collective-permute-start.23 = (bf16[256,128]{1,0:T(8,128)(2,1)}, bf16[256,128]{1,0:T(8,128)(2,1)S(1)}, u32[]{:S(2)}, u32[]{:S(2)}) collective-permute-start(bf16[256,128]{1,0:T(8,128)(2,1)} %get-tuple-element.52), channel_id=1, source_target_pairs={{0,112},{1,113},{2,114},{3,115},{4,116},{5,117},{6,118},{7,119},{8... | collective-permute-start | bytes 196616 | tf_op jit(solution)/shard_map/ppermute | solution.py:355
  128.1 5.5 %copy-start.18 = (bf16[256,128]{1,0:T(8,128)(2,1)}, bf16[256,128]{1,0:T(8,128)(2,1)S(1)}, u32[]{:S(2)}) copy-start(bf16[256,128]{1,0:T(8,128)(2,1)S(1)} %collective-permute-done.19.refs_3_) | copy-start | bytes 196612
  128.1 5.5 %copy-start.20 = (bf16[256,128]{1,0:T(8,128)(2,1)}, bf16[256,128]{1,0:T(8,128)(2,1)S(1)}, u32[]{:S(2)}) copy-start(bf16[256,128]{1,0:T(8,128)(2,1)S(1)} %collective-permute-done.20.refs_4_) | copy-start | bytes 196612
  129.4 4.3 %copy-start.22 = (bf16[256,128]{1,0:T(8,128)(2,1)}, bf16[256,128]{1,0:T(8,128)(2,1)S(1)}, u32[]{:S(2)}) copy-start(bf16[256,128]{1,0:T(8,128)(2,1)S(1)} %collective-permute-done.21.refs_5_) | copy-start | bytes 196612
  131.5 2.1 %copy-start.23 = (bf16[256,128]{1,0:T(8,128)(2,1)}, bf16[256,128]{1,0:T(8,128)(2,1)S(1)}, u32[]{:S(2)}) copy-start(bf16[256,128]{1,0:T(8,128)(2,1)S(1)} %collective-permute-done.22.refs_6_) | copy-start | bytes 196612
  133.6 0.6 copy-start.25

commit v4 on v3

--- a/solution.py
+++ b/solution.py
@@ -53,8 +53,9 @@
 
 
 def scale_shift(layer, total_ref, gain_ref, shift_ref):
-    mu = total_ref[0:1, :]
-    var = jnp.maximum(total_ref[1:2, :] - mu * mu, 0.0)
+    count = 1.0 / (NODES * lax.axis_size("blk"))
+    mu = total_ref[0:1, :] * count
+    var = jnp.maximum(total_ref[1:2, :] * count - mu * mu, 0.0)
     a = gain_ref[layer : layer + 1, :] * lax.rsqrt(var + 1e-05)
     return a, shift_ref[layer : layer + 1, :] - a * mu
 
@@ -379,7 +380,6 @@
     node_shift,
 ):
     devices = lax.axis_size("blk")
-    total_nodes = NODES * devices
     here = lax.axis_index("blk")
     odd = [(here >> bit) & 1 for bit in (0, 2, 4)]
     faces = jnp.stack([2 * j + 1 - (odd[j] ^ side) for j in range(3) for side in (0, 1)])
@@ -413,7 +413,7 @@
         update, stats = outs[0], outs[1]
         if send:
             halo_upds = swap(outs[2:])
-        totals = total_over(stats) / total_nodes
+        totals = total_over(stats)
         extra = (update, totals, node_gain, node_shift)
     a, b = scale_shift(LAYERS - 1, totals, node_gain, node_shift)
     out = (h.astype(F32) + update.astype(F32) * a + b).astype(BF)

time: 161 us -> 161 us (level)
    ppermute x24, starting transfers between devices: 51.3 us -> 54.6 us  [swap(): out.append(lax.ppermute(block, 'blk', pairs))]
    all_to_all x1, starting transfers between devices: 8.67 us -> 6.09 us  [total_over(): parts = lax.all_to_all(stats, 'blk', 0, 0)]
  transfers between devices with their start and end apart: 25 -> 25, of which waited for: 10 -> 9; matrix products, arithmetic and copies ran while one was open for 1% -> 1% of each run, Pallas kernels for 0% -> 0%
where the time goes in v4:
time: 161 us
  starting transfers between devices  60.7 us (38%)
  Pallas kernels  56.3 us (35%)
  blocking collectives  17.1 us (11%)
  waiting for transfers between devices  14.3 us (9%)
  local copies, waits for them, and re-layouts  7.25 us (5%)
  other arithmetic  4.3 us (3%)
    ppermute x24, starting transfers between devices, swap(): out.append(lax.ppermute(block, 'blk', pairs))  54.6 us
    pallas_call x2, Pallas kernels, edge_layer(): pl.pallas_call(functools.partial(edge_kernel, layer, moved), grid_spec=pl...  40.7 us
    all_to_all x1, blocking collectives, total_over(): parts = lax.all_to_all(stats, 'blk', 0, 0)  17.1 us
    pallas_call x2, Pallas kernels, node_layer(): pl.pallas_call(functools.partial(node_kernel, layer, send), grid=(NODES /...  15.6 us
    ppermute x24, waiting for transfers between devices, swap(): out.append(lax.ppermute(block, 'blk', pairs))  14.3 us
    all_to_all x1, starting transfers between devices, total_over(): parts = lax.all_to_all(stats, 'blk', 0, 0)  6.09 us
    gather x1, local copies, waits for them, and re-layouts, per_device(): rows = node_latent[sidx.reshape(-1)]  4 us
  transfers between devices with their start and end apart: 25, of which 9 were waited for; matrix products, arithmetic and copies ran while one was open for 1% of the time, Pallas kernels for 0%

profile of v4, /device:TPU:1, one launch (start us, length us, event | category | flops | bytes accessed | tf_op | source)
XLA Modules:
  0.0 160.9 jit_solution(3502427188948804154)
XLA Ops:
  0.6 0.8 fusion.6
  1.5 4.0 %gather_fusion = bf16[1536,128]{1,0:T(8,128)(2,1)S(1)} fusion(bf16[4096,128]{1,0:T(8,128)(2,1)} %refs_0_.5, s32[2048]{0:T(1024)S(1)} %pad_clamp_fusion), kind=kCustom, calls=%fused_computation | custom fusion | bytes 792576 | tf_op jit(solution)/shard_map/gather | solution.py:397
  5.6 6.1 %collective-permute-start.5 = (bf16[256,128]{1,0:T(8,128)(2,1)S(1)}, bf16[256,128]{1,0:T(8,128)(2,1)S(1)}, u32[]{:S(2)}, u32[]{:S(2)}) collective-permute-start(bf16[256,128]{1,0:T(8,128)(2,1)S(1)} %get-tuple-element.58), channel_id=1, source_target_pairs={{0,112},{1,113},{2,114},{3,115},{4,116},{5,117},{6,118},{7,119},{8... | collective-permute-start | bytes 196616 | tf_op jit(solution)/shard_map/ppermute | solution.py:356
  11.7 0.0 collective-permute-start.4
  11.7 6.2 %collective-permute-start.3 = (bf16[256,128]{1,0:T(8,128)(2,1)S(1)}, bf16[256,128]{1,0:T(8,128)(2,1)S(1)}, u32[]{:S(2)}, u32[]{:S(2)}) collective-permute-start(bf16[256,128]{1,0:T(8,128)(2,1)S(1)} %get-tuple-element.60), channel_id=1, source_target_pairs={{0,124},{1,125},{2,126},{3,127},{4,8},{5,9},{6,10},{7,11},{8,4},{9... | collective-permute-start | bytes 196616 | tf_op jit(solution)/shard_map/ppermute | solution.py:356
  17.9 2.1 %collective-permute-start.1 = (bf16[256,128]{1,0:T(8,128)(2,1)S(1)}, bf16[256,128]{1,0:T(8,128)(2,1)S(1)}, u32[]{:S(2)}, u32[]{:S(2)}) collective-permute-start(bf16[256,128]{1,0:T(8,128)(2,1)S(1)} %get-tuple-element.62), channel_id=1, source_target_pairs={{0,127},{1,2},{2,1},{3,4},{4,3},{5,6},{6,5},{7,8},{8,7},{9,10},{10... | collective-permute-start | bytes 196616 | tf_op jit(solution)/shard_map/ppermute | solution.py:356
  20.0 1.6 %collective-permute-start = (bf16[256,128]{1,0:T(8,128)(2,1)S(1)}, bf16[256,128]{1,0:T(8,128)(2,1)S(1)}, u32[]{:S(2)}, u32[]{:S(2)}) collective-permute-start(bf16[256,128]{1,0:T(8,128)(2,1)S(1)} %get-tuple-element.63), channel_id=1, source_target_pairs={{0,1},{1,0},{2,3},{3,2},{4,5},{5,4},{6,7},{7,6},{8,9},{9,8},{10,11... | collective-permute-start | bytes 196616 | tf_op jit(solution)/shard_map/ppermute | solution.py:356
  21.6 0.7 stack.27.face_ref
  22.3 0.0 collective-permute-done.4.refs_5_.refs_9_
  22.3 0.3 collective-permute-done.2.refs_3_.refs_7_
  22.6 0.0 collective-permute-done.1.refs_2_.refs_6_
  22.6 0.0 collective-permute-done.refs_1_.refs_5_
  22.7 0.3 copy-done.2
  22.9 0.0 copy-done.3
  23.0 0.3 copy-done.4
  23.2 0.0 copy-done.5
  23.3 0.0 copy-done.6
  23.3 20.0 %edges.2 = (bf16[128,24576]{1,0:T(8,128)(2,1)}, bf16[4096,128]{1,0:T(8,128)(2,1)}, bf16[256,128]{1,0:T(8,128)(2,1)}, bf16[256,128]{1,0:T(8,128)(2,1)}, bf16[256,...) custom-call(s32[6]{0:T(128)} %stack.27.face_ref, ...), custom_call_target="tpu_custom_call" | custom-call | tf_op jit(solution)/shard_map/edges/pallas_call | solution.py:237
  43.3 5.9 %collective-permute-start.6 = (bf16[256,128]{1,0:T(8,128)(2,1)}, bf16[256,128]{1,0:T(8,128)(2,1)S(1)}, u32[]{:S(2)}, u32[]{:S(2)}) collective-permute-start(bf16[256,128]{1,0:T(8,128)(2,1)} %get-tuple-element.30), channel_id=1, source_target_pairs={{0,1},{1,0},{2,3},{3,2},{4,5},{5,4},{6,7},{7,6},{8,9},{9,8},{10,11... | collective-permute-start | bytes 196616 | tf_op jit(solution)/shard_map/ppermute | solution.py:356
  49.2 0.0 collective-permute-start.8
  49.2 3.4 %collective-permute-start.9 = (bf16[256,128]{1,0:T(8,128)(2,1)}, bf16[256,128]{1,0:T(8,128)(2,1)S(1)}, u32[]{:S(2)}, u32[]{:S(2)}) collective-permute-start(bf16[256,128]{1,0:T(8,128)(2,1)} %get-tuple-element.33), channel_id=1, source_target_pairs={{0,124},{1,125},{2,126},{3,127},{4,8},{5,9},{6,10},{7,11},{8,4},{9... | collective-permute-start | bytes 196616 | tf_op jit(solution)/shard_map/ppermute | solution.py:356
  52.7 0.0 collective-permute-start.10
  52.7 0.0 collective-permute-done.6.refs_2_
  52.7 1.6 %collective-permute-start.11 = (bf16[256,128]{1,0:T(8,128)(2,1)}, bf16[256,128]{1,0:T(8,128)(2,1)S(1)}, u32[]{:S(2)}, u32[]{:S(2)}) collective-permute-start(bf16[256,128]{1,0:T(8,128)(2,1)} %get-tuple-element.35), channel_id=1, source_target_pairs={{0,112},{1,113},{2,114},{3,115},{4,116},{5,117},{6,118},{7,119},{8... | collective-permute-start | bytes 196616 | tf_op jit(solution)/shard_map/ppermute | solution.py:356
  54.3 4.4 %collective-permute-done.9.refs_5_ = bf16[256,128]{1,0:T(8,128)(2,1)S(1)} collective-permute-done((bf16[256,128]{1,0:T(8,128)(2,1)}, bf16[256,128]{1,0:T(8,128)(2,1)S(1)}, u32[]{:S(2)}, u32[]{:S(2)}) %collective-permute-start.9) | collective-permute-done | bytes 65568 | tf_op jit(solution)/shard_map/ppermute | solution.py:356
  58.8 0.0 collective-permute-done.10.refs_6_
  58.8 0.9 collective-permute-done.11.refs_7_
  59.7 0.6 copy-done.24
  60.3 8.7 %nodes.2 = (bf16[4096,128]{1,0:T(8,128)(2,1)}, f32[128,2,128]{2,1,0:T(2,128)}, bf16[128,256]{1,0:T(8,128)(2,1)}, bf16[128,256]{1,0:T(8,128)(2,1)}, bf16[128,256]...) custom-call(bf16[4096,128]{1,0:T(8,128)(2,1)} %refs_0_.5, ...), custom_call_target="tpu_custom_call" | custom-call | tf_op jit(solution)/shard_map/nodes/pallas_call | solution.py:333
  69.1 3.0 %collective-permute-start.12 = (bf16[128,256]{1,0:T(8,128)(2,1)}, bf16[128,256]{1,0:T(8,128)(2,1)S(1)}, u32[]{:S(2)}, u32[]{:S(2)}) collective-permute-start(bf16[128,256]{1,0:T(8,128)(2,1)} %get-tuple-element.38), channel_id=1, source_target_pairs={{0,1},{1,0},{2,3},{3,2},{4,5},{5,4},{6,7},{7,6},{8,9},{9,8},{10,11... | collective-permute-start | bytes 196616 | tf_op jit(solution)/shard_map/ppermute | solution.py:356
  72.0 6.1 %all-to-all-start = ((f32[128,2,128]{2,1,0:T(2,128)}), f32[128,2,128]{2,1,0:T(2,128)S(1)}, u32[]{:S(2)}, u32[]{:S(2)}) async-start(f32[128,2,128]{2,1,0:T(2,128)} %get-tuple-element.37), calls=%async_computation | async-start | bytes 262144 | tf_op jit(solution)/shard_map/all_to_all | solution.py:361
  78.1 1.8 %collective-permute-start.13 = (bf16[128,256]{1,0:T(8,128)(2,1)}, bf16[128,256]{1,0:T(8,128)(2,1)S(1)}, u32[]{:S(2)}, u32[]{:S(2)}) collective-permute-start(bf16[128,256]{1,0:T(8,128)(2,1)} %get-tuple-element.39), channel_id=1, source_target_pairs={{0,127},{1,2},{2,1},{3,4},{4,3},{5,6},{6,5},{7,8},{8,7},{9,10},{10... | collective-permute-start | bytes 196616 | tf_op jit(solution)/shard_map/ppermute | solution.py:356
  80.0 2.9 %collective-permute-start.14 = (bf16[128,256]{1,0:T(8,128)(2,1)}, bf16[128,256]{1,0:T(8,128)(2,1)S(1)}, u32[]{:S(2)}, u32[]{:S(2)}) collective-permute-start(bf16[128,256]{1,0:T(8,128)(2,1)} %get-tuple-element.40), channel_id=1, source_target_pairs={{0,4},{1,5},{2,6},{3,7},{4,0},{5,1},{6,2},{7,3},{8,12},{9,13},{10,... | collective-permute-start | bytes 196616 | tf_op jit(solution)/shard_map/ppermute | solution.py:356
  82.9 4.5 %collective-permute-start.15 = (bf16[128,256]{1,0:T(8,128)(2,1)}, bf16[128,256]{1,0:T(8,128)(2,1)S(1)}, u32[]{:S(2)}, u32[]{:S(2)}) collective-permute-start(bf16[128,256]{1,0:T(8,128)(2,1)} %get-tuple-element.41), channel_id=1, source_target_pairs={{0,124},{1,125},{2,126},{3,127},{4,8},{5,9},{6,10},{7,11},{8,4},{9... | collective-permute-start | bytes 196616 | tf_op jit(solution)/shard_map/ppermute | solution.py:356
  87.4 0.0 collective-permute-start.16
  87.4 0.0 collective-permute-done.12.refs_11_
  87.4 3.2 %collective-permute-start.17 = (bf16[128,256]{1,0:T(8,128)(2,1)}, bf16[128,256]{1,0:T(8,128)(2,1)S(1)}, u32[]{:S(2)}, u32[]{:S(2)}) collective-permute-start(bf16[128,256]{1,0:T(8,128)(2,1)} %get-tuple-element.43), channel_id=1, source_target_pairs={{0,112},{1,113},{2,114},{3,115},{4,116},{5,117},{6,118},{7,119},{8... | collective-permute-start | bytes 196616 | tf_op jit(solution)/shard_map/ppermute | solution.py:356
  90.6 0.0 all-to-all-done
  90.6 0.7 reduce_sum.18.refs_2_
  91.3 0.0 collective-permute-done.13.refs_12_
  91.4 0.7 collective-permute-done.15.refs_14_
  92.1 0.5 collective-permute-done.16.refs_15_
  92.5 1.9 %collective-permute-done.17.refs_16_ = bf16[128,256]{1,0:T(8,128)(2,1)S(1)} collective-permute-done((bf16[128,256]{1,0:T(8,128)(2,1)}, bf16[128,256]{1,0:T(8,128)(2,1)S(1)}, u32[]{:S(2)}, u32[]{:S(2)}) %collective-permute-start.17) | collective-permute-done | bytes 65568 | tf_op jit(solution)/shard_map/ppermute | solution.py:356
  94.5 0.6 copy-done.13
  95.1 20.7 %edges.3 = (bf16[4096,128]{1,0:T(8,128)(2,1)}, bf16[24576,128]{1,0:T(8,128)(2,1)}, bf16[4096,128]{1,0:T(8,128)(2,1)}, bf16[256,128]{1,0:T(8,128)(2,1)}, bf16[256...) custom-call(s32[6]{0:T(128)} %stack.27.face_ref, ...), custom_call_target="tpu_custom_call" | custom-call | tf_op jit(solution)/shard_map/edges/pallas_call | solution.py:237
  115.8 0.0 copy-start.26
  115.8 0.0 copy-start.27
  115.8 0.0 copy-start
  115.8 3.9 %collective-permute-start.18 = (bf16[256,128]{1,0:T(8,128)(2,1)}, bf16[256,128]{1,0:T(8,128)(2,1)S(1)}, u32[]{:S(2)}, u32[]{:S(2)}) collective-permute-start(bf16[256,128]{1,0:T(8,128)(2,1)} %get-tuple-element.47), channel_id=1, source_target_pairs={{0,1},{1,0},{2,3},{3,2},{4,5},{5,4},{6,7},{7,6},{8,9},{9,8},{10,11... | collective-permute-start | bytes 196616 | tf_op jit(solution)/shard_map/ppermute | solution.py:356
  119.7 0.0 collective-permute-start.19
  119.8 0.3 collective-permute-start.20
  120.0 6.2 %collective-permute-start.21 = (bf16[256,128]{1,0:T(8,128)(2,1)}, bf16[256,128]{1,0:T(8,128)(2,1)S(1)}, u32[]{:S(2)}, u32[]{:S(2)}) collective-permute-start(bf16[256,128]{1,0:T(8,128)(2,1)} %get-tuple-element.50), channel_id=1, source_target_pairs={{0,124},{1,125},{2,126},{3,127},{4,8},{5,9},{6,10},{7,11},{8,4},{9... | collective-permute-start | bytes 196616 | tf_op jit(solution)/shard_map/ppermute | solution.py:356
  126.2 0.0 collective-permute-start.22
  126.2 0.0 collective-permute-done.18.refs_2_
  126.2 1.7 %collective-permute-start.23 = (bf16[256,128]{1,0:T(8,128)(2,1)}, bf16[256,128]{1,0:T(8,128)(2,1)S(1)}, u32[]{:S(2)}, u32[]{:S(2)}) collective-permute-start(bf16[256,128]{1,0:T(8,128)(2,1)} %get-tuple-element.52), channel_id=1, source_target_pairs={{0,112},{1,113},{2,114},{3,115},{4,116},{5,117},{6,118},{7,119},{8... | collective-permute-start | bytes 196616 | tf_op jit(solution)/shard_map/ppermute | solution.py:356
  127.9 0.0 collective-permute-done.19.refs_3_
  127.9 1.3 collective-permute-done.21.refs_5_
  129.2 1.8 %collective-permute-done.22.refs_6_ = bf16[256,128]{1,0:T(8,128)(2,1)S(1)} collective-permute-done((bf16[256,128]{1,0:T(8,128)(2,1)}, bf16[256,128]{1,0:T(8,128)(2,1)S(1)}, u32[]{:S(2)}, u32[]{:S(2)}) %collective-permute-start.22) | collective-permute-done | bytes 65568 | tf_op jit(solution)/shard_map/ppermute | solution.py:356
  131.0 2.4 %collective-permute-done.23.refs_7_ = bf16[256,128]{1,0:T(8,128)(2,1)S(1)} collective-permute-done((bf16[256,128]{1,0:T(8,128)(2,1)}, bf16[256,128]{1,0:T(8,128)(2,1)S(1)}, u32[]{:S(2)}, u32[]{:S(2)}) %collective-permute-start.23) | collective-permute-done | bytes 65568 | tf_op jit(solution)/shard_map/ppermute | solution.py:356
  133.4 0.6 copy-done.25
  134.0 6.9 %nodes.3 = (bf16[4096,128]{1,0:T(8,128)(2,1)}, f32[128,2,128]{2,1,0:T(2,128)}) custom-call(bf16[4096,128]{1,0:T(8,128)(2,1)} %get-tuple-element.45.refs_0_, bf16[4096,128]{1,0:T(8,128)(2,1)} %get-tuple-element.46.refs_1_, bf16[256,128]{1,0:T(8,128)(2,1)} %copy-done.16, bf16[256,128]{1,0:T(8,128)(2,1)} %copy-done.18, bf16[256,128]{1,0:T(8,128)(2,1)} %copy-done.20, ...), custom_call_target="tpu_custom_call" | custom-call | tf_op jit(solution)/shard_map/nodes/pallas_call | solution.py:333
  141.0 17.1 %all_to_all.10 = f32[128,2,128]{2,1,0:T(2,128)S(1)} all-to-all(f32[128,2,128]{2,1,0:T(2,128)} %get-tuple-element.54), channel_id=1, replica_groups=mesh['blk'=128] {'blk'}, dimensions={0} | all-to-all | bytes 262144 | tf_op jit(solution)/shard_map/all_to_all | solution.py:361
  158.1 0.1 reduce_sum.19
  158.3 2.6 %add_convert_fusion = bf16[4096,128]{1,0:T(8,128)(2,1)} fusion(bf16[4096,128]{1,0:T(8,128)(2,1)} %get-tuple-element.53, bf16[4096,128]{1,0:T(8,128)(2,1)S(1)} %copy-done, f32[128]{0:T(128)S(1)} %get-tuple-element.56, f32[128]{0:T(128)S(1)} %bitcast.30), kind=kLoop, calls=%fused_computation.1 | loop fusion | flops 3145728 | bytes 3146752 | tf_op jit(solution)/shard_map/convert_element_type | solution.py:419
  (59 shorter events, 0.2 us)
Async XLA Ops:
  1.4 4.1 %copy-start.7 = (s32[6,256]{1,0:T(8,128)}, s32[6,256]{1,0:T(8,128)S(1)}, u32[]{:S(2)}) copy-start(s32[6,256]{1,0:T(8,128)S(1)} %concatenate.3.refs_8_) | copy-start | bytes 18436
  5.6 14.4 %collective-permute-start.5 = (bf16[256,128]{1,0:T(8,128)(2,1)S(1)}, bf16[256,128]{1,0:T(8,128)(2,1)S(1)}, u32[]{:S(2)}, u32[]{:S(2)}) collective-permute-start(bf16[256,128]{1,0:T(8,128)(2,1)S(1)} %get-tuple-element.58), channel_id=1, source_target_pairs={{0,112},{1,113},{2,114},{3,115},{4,116},{5,117},{6,118},{7,119},{8... | collective-permute-start | bytes 196616 | tf_op jit(solution)/shard_map/ppermute | solution.py:356
  11.7 10.7 %collective-permute-start.4 = (bf16[256,128]{1,0:T(8,128)(2,1)S(1)}, bf16[256,128]{1,0:T(8,128)(2,1)S(1)}, u32[]{:S(2)}, u32[]{:S(2)}) collective-permute-start(bf16[256,128]{1,0:T(8,128)(2,1)S(1)} %get-tuple-element.59), channel_id=1, source_target_pairs={{0,16},{1,17},{2,18},{3,19},{4,20},{5,21},{6,22},{7,23},{8,24},{9,... | collective-permute-start | bytes 196616 | tf_op jit(solution)/shard_map/ppermute | solution.py:356
  11.7 10.7 %collective-permute-start.3 = (bf16[256,128]{1,0:T(8,128)(2,1)S(1)}, bf16[256,128]{1,0:T(8,128)(2,1)S(1)}, u32[]{:S(2)}, u32[]{:S(2)}) collective-permute-start(bf16[256,128]{1,0:T(8,128)(2,1)S(1)} %get-tuple-element.60), channel_id=1, source_target_pairs={{0,124},{1,125},{2,126},{3,127},{4,8},{5,9},{6,10},{7,11},{8,4},{9... | collective-permute-start | bytes 196616 | tf_op jit(solution)/shard_map/ppermute | solution.py:356
  17.9 4.8 %collective-permute-start.2 = (bf16[256,128]{1,0:T(8,128)(2,1)S(1)}, bf16[256,128]{1,0:T(8,128)(2,1)S(1)}, u32[]{:S(2)}, u32[]{:S(2)}) collective-permute-start(bf16[256,128]{1,0:T(8,128)(2,1)S(1)} %get-tuple-element.61), channel_id=1, source_target_pairs={{0,4},{1,5},{2,6},{3,7},{4,0},{5,1},{6,2},{7,3},{8,12},{9,13},{10,... | collective-permute-start | bytes 196616 | tf_op jit(solution)/shard_map/ppermute | solution.py:356
  17.9 4.8 %collective-permute-start.1 = (bf16[256,128]{1,0:T(8,128)(2,1)S(1)}, bf16[256,128]{1,0:T(8,128)(2,1)S(1)}, u32[]{:S(2)}, u32[]{:S(2)}) collective-permute-start(bf16[256,128]{1,0:T(8,128)(2,1)S(1)} %get-tuple-element.62), channel_id=1, source_target_pairs={{0,127},{1,2},{2,1},{3,4},{4,3},{5,6},{6,5},{7,8},{8,7},{9,10},{10... | collective-permute-start | bytes 196616 | tf_op jit(solution)/shard_map/ppermute | solution.py:356
  20.0 2.7 %copy-start.1 = (bf16[256,128]{1,0:T(8,128)(2,1)}, bf16[256,128]{1,0:T(8,128)(2,1)S(1)}, u32[]{:S(2)}) copy-start(bf16[256,128]{1,0:T(8,128)(2,1)S(1)} %collective-permute-done.5.refs_6_.refs_10_) | copy-start | bytes 196612
  20.0 2.6 %collective-permute-start = (bf16[256,128]{1,0:T(8,128)(2,1)S(1)}, bf16[256,128]{1,0:T(8,128)(2,1)S(1)}, u32[]{:S(2)}, u32[]{:S(2)}) collective-permute-start(bf16[256,128]{1,0:T(8,128)(2,1)S(1)} %get-tuple-element.63), channel_id=1, source_target_pairs={{0,1},{1,0},{2,3},{3,2},{4,5},{5,4},{6,7},{7,6},{8,9},{9,8},{10,11... | collective-permute-start | bytes 196616 | tf_op jit(solution)/shard_map/ppermute | solution.py:356
  22.3 0.6 copy-start.2
  22.3 0.7 copy-start.3
  22.6 0.6 copy-start.4
  22.6 0.6 copy-start.5
  22.6 0.7 copy-start.6
  43.3 9.4 %collective-permute-start.6 = (bf16[256,128]{1,0:T(8,128)(2,1)}, bf16[256,128]{1,0:T(8,128)(2,1)S(1)}, u32[]{:S(2)}, u32[]{:S(2)}) collective-permute-start(bf16[256,128]{1,0:T(8,128)(2,1)} %get-tuple-element.30), channel_id=1, source_target_pairs={{0,1},{1,0},{2,3},{3,2},{4,5},{5,4},{6,7},{7,6},{8,9},{9,8},{10,11... | collective-permute-start | bytes 196616 | tf_op jit(solution)/shard_map/ppermute | solution.py:356
  49.2 5.1 %collective-permute-start.7 = (bf16[256,128]{1,0:T(8,128)(2,1)}, bf16[256,128]{1,0:T(8,128)(2,1)S(1)}, u32[]{:S(2)}, u32[]{:S(2)}) collective-permute-start(bf16[256,128]{1,0:T(8,128)(2,1)} %get-tuple-element.31), channel_id=1, source_target_pairs={{0,127},{1,2},{2,1},{3,4},{4,3},{5,6},{6,5},{7,8},{8,7},{9,10},{10... | collective-permute-start | bytes 196616 | tf_op jit(solution)/shard_map/ppermute | solution.py:356
  49.2 5.1 %collective-permute-start.8 = (bf16[256,128]{1,0:T(8,128)(2,1)}, bf16[256,128]{1,0:T(8,128)(2,1)S(1)}, u32[]{:S(2)}, u32[]{:S(2)}) collective-permute-start(bf16[256,128]{1,0:T(8,128)(2,1)} %get-tuple-element.32), channel_id=1, source_target_pairs={{0,4},{1,5},{2,6},{3,7},{4,0},{5,1},{6,2},{7,3},{8,12},{9,13},{10,... | collective-permute-start | bytes 196616 | tf_op jit(solution)/shard_map/ppermute | solution.py:356
  49.2 9.5 %collective-permute-start.9 = (bf16[256,128]{1,0:T(8,128)(2,1)}, bf16[256,128]{1,0:T(8,128)(2,1)S(1)}, u32[]{:S(2)}, u32[]{:S(2)}) collective-permute-start(bf16[256,128]{1,0:T(8,128)(2,1)} %get-tuple-element.33), channel_id=1, source_target_pairs={{0,124},{1,125},{2,126},{3,127},{4,8},{5,9},{6,10},{7,11},{8,4},{9... | collective-permute-start | bytes 196616 | tf_op jit(solution)/shard_map/ppermute | solution.py:356
  52.7 6.1 %collective-permute-start.10 = (bf16[256,128]{1,0:T(8,128)(2,1)}, bf16[256,128]{1,0:T(8,128)(2,1)S(1)}, u32[]{:S(2)}, u32[]{:S(2)}) collective-permute-start(bf16[256,128]{1,0:T(8,128)(2,1)} %get-tuple-element.34), channel_id=1, source_target_pairs={{0,16},{1,17},{2,18},{3,19},{4,20},{5,21},{6,22},{7,23},{8,24},{9,... | collective-permute-start | bytes 196616 | tf_op jit(solution)/shard_map/ppermute | solution.py:356
  52.7 7.0 %copy-start.14 = (bf16[256,128]{1,0:T(8,128)(2,1)}, bf16[256,128]{1,0:T(8,128)(2,1)S(1)}, u32[]{:S(2)}) copy-start(bf16[256,128]{1,0:T(8,128)(2,1)S(1)} %collective-permute-done.6.refs_2_) | copy-start | bytes 196612
  52.7 7.0 %collective-permute-start.11 = (bf16[256,128]{1,0:T(8,128)(2,1)}, bf16[256,128]{1,0:T(8,128)(2,1)S(1)}, u32[]{:S(2)}, u32[]{:S(2)}) collective-permute-start(bf16[256,128]{1,0:T(8,128)(2,1)} %get-tuple-element.35), channel_id=1, source_target_pairs={{0,112},{1,113},{2,114},{3,115},{4,116},{5,117},{6,118},{7,119},{8... | collective-permute-start | bytes 196616 | tf_op jit(solution)/shard_map/ppermute | solution.py:356
  54.3 5.4 %copy-start.15 = (bf16[256,128]{1,0:T(8,128)(2,1)}, bf16[256,128]{1,0:T(8,128)(2,1)S(1)}, u32[]{:S(2)}) copy-start(bf16[256,128]{1,0:T(8,128)(2,1)S(1)} %collective-permute-done.7.refs_3_) | copy-start | bytes 196612
  54.3 5.4 %copy-start.17 = (bf16[256,128]{1,0:T(8,128)(2,1)}, bf16[256,128]{1,0:T(8,128)(2,1)S(1)}, u32[]{:S(2)}) copy-start(bf16[256,128]{1,0:T(8,128)(2,1)S(1)} %collective-permute-done.8.refs_4_) | copy-start | bytes 196612
  58.8 1.0 copy-start.19
  58.8 1.0 copy-start.21
  59.7 0.6 copy-start.24
  69.1 18.4 %collective-permute-start.12 = (bf16[128,256]{1,0:T(8,128)(2,1)}, bf16[128,256]{1,0:T(8,128)(2,1)S(1)}, u32[]{:S(2)}, u32[]{:S(2)}) collective-permute-start(bf16[128,256]{1,0:T(8,128)(2,1)} %get-tuple-element.38), channel_id=1, source_target_pairs={{0,1},{1,0},{2,3},{3,2},{4,5},{5,4},{6,7},{7,6},{8,9},{9,8},{10,11... | collective-permute-start | bytes 196616 | tf_op jit(solution)/shard_map/ppermute | solution.py:356
  72.0 18.6 %all-to-all-start = ((f32[128,2,128]{2,1,0:T(2,128)}), f32[128,2,128]{2,1,0:T(2,128)S(1)}, u32[]{:S(2)}, u32[]{:S(2)}) async-start(f32[128,2,128]{2,1,0:T(2,128)} %get-tuple-element.37), calls=%async_computation | async-start | bytes 262144 | tf_op jit(solution)/shard_map/all_to_all | solution.py:361
  78.1 13.2 %collective-permute-start.13 = (bf16[128,256]{1,0:T(8,128)(2,1)}, bf16[128,256]{1,0:T(8,128)(2,1)S(1)}, u32[]{:S(2)}, u32[]{:S(2)}) collective-permute-start(bf16[128,256]{1,0:T(8,128)(2,1)} %get-tuple-element.39), channel_id=1, source_target_pairs={{0,127},{1,2},{2,1},{3,4},{4,3},{5,6},{6,5},{7,8},{8,7},{9,10},{10... | collective-permute-start | bytes 196616 | tf_op jit(solution)/shard_map/ppermute | solution.py:356
  80.0 11.4 %collective-permute-start.14 = (bf16[128,256]{1,0:T(8,128)(2,1)}, bf16[128,256]{1,0:T(8,128)(2,1)S(1)}, u32[]{:S(2)}, u32[]{:S(2)}) collective-permute-start(bf16[128,256]{1,0:T(8,128)(2,1)} %get-tuple-element.40), channel_id=1, source_target_pairs={{0,4},{1,5},{2,6},{3,7},{4,0},{5,1},{6,2},{7,3},{8,12},{9,13},{10,... | collective-permute-start | bytes 196616 | tf_op jit(solution)/shard_map/ppermute | solution.py:356
  82.9 9.2 %collective-permute-start.15 = (bf16[128,256]{1,0:T(8,128)(2,1)}, bf16[128,256]{1,0:T(8,128)(2,1)S(1)}, u32[]{:S(2)}, u32[]{:S(2)}) collective-permute-start(bf16[128,256]{1,0:T(8,128)(2,1)} %get-tuple-element.41), channel_id=1, source_target_pairs={{0,124},{1,125},{2,126},{3,127},{4,8},{5,9},{6,10},{7,11},{8,4},{9... | collective-permute-start | bytes 196616 | tf_op jit(solution)/shard_map/ppermute | solution.py:356
  87.4 5.1 %collective-permute-start.16 = (bf16[128,256]{1,0:T(8,128)(2,1)}, bf16[128,256]{1,0:T(8,128)(2,1)S(1)}, u32[]{:S(2)}, u32[]{:S(2)}) collective-permute-start(bf16[128,256]{1,0:T(8,128)(2,1)} %get-tuple-element.42), channel_id=1, source_target_pairs={{0,16},{1,17},{2,18},{3,19},{4,20},{5,21},{6,22},{7,23},{8,24},{9,... | collective-permute-start | bytes 196616 | tf_op jit(solution)/shard_map/ppermute | solution.py:356
  87.4 7.0 %copy-start.8 = (bf16[128,256]{1,0:T(8,128)(2,1)}, bf16[128,256]{1,0:T(8,128)(2,1)S(1)}, u32[]{:S(2)}) copy-start(bf16[128,256]{1,0:T(8,128)(2,1)S(1)} %collective-permute-done.12.refs_11_) | copy-start | bytes 196612
  87.4 7.0 %collective-permute-start.17 = (bf16[128,256]{1,0:T(8,128)(2,1)}, bf16[128,256]{1,0:T(8,128)(2,1)S(1)}, u32[]{:S(2)}, u32[]{:S(2)}) collective-permute-start(bf16[128,256]{1,0:T(8,128)(2,1)} %get-tuple-element.43), channel_id=1, source_target_pairs={{0,112},{1,113},{2,114},{3,115},{4,116},{5,117},{6,118},{7,119},{8... | collective-permute-start | bytes 196616 | tf_op jit(solution)/shard_map/ppermute | solution.py:356
  91.4 3.1 %copy-start.9 = (bf16[128,256]{1,0:T(8,128)(2,1)}, bf16[128,256]{1,0:T(8,128)(2,1)S(1)}, u32[]{:S(2)}) copy-start(bf16[128,256]{1,0:T(8,128)(2,1)S(1)} %collective-permute-done.13.refs_12_) | copy-start | bytes 196612
  91.4 3.1 %copy-start.10 = (bf16[128,256]{1,0:T(8,128)(2,1)}, bf16[128,256]{1,0:T(8,128)(2,1)S(1)}, u32[]{:S(2)}) copy-start(bf16[128,256]{1,0:T(8,128)(2,1)S(1)} %collective-permute-done.14.refs_13_) | copy-start | bytes 196612
  92.1 2.4 %copy-start.11 = (bf16[128,256]{1,0:T(8,128)(2,1)}, bf16[128,256]{1,0:T(8,128)(2,1)S(1)}, u32[]{:S(2)}) copy-start(bf16[128,256]{1,0:T(8,128)(2,1)S(1)} %collective-permute-done.15.refs_14_) | copy-start | bytes 196612
  92.5 1.9 %copy-start.12 = (bf16[128,256]{1,0:T(8,128)(2,1)}, bf16[128,256]{1,0:T(8,128)(2,1)S(1)}, u32[]{:S(2)}) copy-start(bf16[128,256]{1,0:T(8,128)(2,1)S(1)} %collective-permute-done.16.refs_15_) | copy-start | bytes 196612
  94.4 0.6 copy-start.13
  115.8 42.5 %copy-start.26 = (f32[2,128]{1,0:T(2,128)S(1)}, f32[2,128]{1,0:T(2,128)}, u32[]{:S(2)}) copy-start(f32[2,128]{1,0:T(2,128)} %refs_3_.1) | copy-start | bytes 3076
  115.8 42.5 %copy-start.27 = (f32[2,128]{1,0:T(2,128)S(1)}, f32[2,128]{1,0:T(2,128)}, u32[]{:S(2)}) copy-start(f32[2,128]{1,0:T(2,128)} %refs_4_.1) | copy-start | bytes 3076
  115.8 42.5 %copy-start = (bf16[4096,128]{1,0:T(8,128)(2,1)S(1)}, bf16[4096,128]{1,0:T(8,128)(2,1)}, u32[]{:S(2)}) copy-start(bf16[4096,128]{1,0:T(8,128)(2,1)} %get-tuple-element.45.refs_0_) | copy-start | bytes 3145732
  115.8 10.3 %collective-permute-start.18 = (bf16[256,128]{1,0:T(8,128)(2,1)}, bf16[256,128]{1,0:T(8,128)(2,1)S(1)}, u32[]{:S(2)}, u32[]{:S(2)}) collective-permute-start(bf16[256,128]{1,0:T(8,128)(2,1)} %get-tuple-element.47), channel_id=1, source_target_pairs={{0,1},{1,0},{2,3},{3,2},{4,5},{5,4},{6,7},{7,6},{8,9},{9,8},{10,11... | collective-permute-start | bytes 196616 | tf_op jit(solution)/shard_map/ppermute | solution.py:356
  119.7 8.1 %collective-permute-start.19 = (bf16[256,128]{1,0:T(8,128)(2,1)}, bf16[256,128]{1,0:T(8,128)(2,1)S(1)}, u32[]{:S(2)}, u32[]{:S(2)}) collective-permute-start(bf16[256,128]{1,0:T(8,128)(2,1)} %get-tuple-element.48), channel_id=1, source_target_pairs={{0,127},{1,2},{2,1},{3,4},{4,3},{5,6},{6,5},{7,8},{8,7},{9,10},{10... | collective-permute-start | bytes 196616 | tf_op jit(solution)/shard_map/ppermute | solution.py:356
  119.8 8.1 %collective-permute-start.20 = (bf16[256,128]{1,0:T(8,128)(2,1)}, bf16[256,128]{1,0:T(8,128)(2,1)S(1)}, u32[]{:S(2)}, u32[]{:S(2)}) collective-permute-start(bf16[256,128]{1,0:T(8,128)(2,1)} %get-tuple-element.49), channel_id=1, source_target_pairs={{0,4},{1,5},{2,6},{3,7},{4,0},{5,1},{6,2},{7,3},{8,12},{9,13},{10,... | collective-permute-start | bytes 196616 | tf_op jit(solution)/shard_map/ppermute | solution.py:356
  120.0 9.2 %collective-permute-start.21 = (bf16[256,128]{1,0:T(8,128)(2,1)}, bf16[256,128]{1,0:T(8,128)(2,1)S(1)}, u32[]{:S(2)}, u32[]{:S(2)}) collective-permute-start(bf16[256,128]{1,0:T(8,128)(2,1)} %get-tuple-element.50), channel_id=1, source_target_pairs={{0,124},{1,125},{2,126},{3,127},{4,8},{5,9},{6,10},{7,11},{8,4},{9... | collective-permute-start | bytes 196616 | tf_op jit(solution)/shard_map/ppermute | solution.py:356
  126.2 4.8 %collective-permute-start.22 = (bf16[256,128]{1,0:T(8,128)(2,1)}, bf16[256,128]{1,0:T(8,128)(2,1)S(1)}, u32[]{:S(2)}, u32[]{:S(2)}) collective-permute-start(bf16[256,128]{1,0:T(8,128)(2,1)} %get-tuple-element.51), channel_id=1, source_target_pairs={{0,16},{1,17},{2,18},{3,19},{4,20},{5,21},{6,22},{7,23},{8,24},{9,... | collective-permute-start | bytes 196616 | tf_op jit(solution)/shard_map/ppermute | solution.py:356
  126.2 7.3 %copy-start.16 = (bf16[256,128]{1,0:T(8,128)(2,1)}, bf16[256,128]{1,0:T(8,128)(2,1)S(1)}, u32[]{:S(2)}) copy-start(bf16[256,128]{1,0:T(8,128)(2,1)S(1)} %collective-permute-done.18.refs_2_) | copy-start | bytes 196612
  126.2 7.2 %collective-permute-start.23 = (bf16[256,128]{1,0:T(8,128)(2,1)}, bf16[256,128]{1,0:T(8,128)(2,1)S(1)}, u32[]{:S(2)}, u32[]{:S(2)}) collective-permute-start(bf16[256,128]{1,0:T(8,128)(2,1)} %get-tuple-element.52), channel_id=1, source_target_pairs={{0,112},{1,113},{2,114},{3,115},{4,116},{5,117},{6,118},{7,119},{8... | collective-permute-start | bytes 196616 | tf_op jit(solution)/shard_map/ppermute | solution.py:356
  127.9 5.6 %copy-start.18 = (bf16[256,128]{1,0:T(8,128)(2,1)}, bf16[256,128]{1,0:T(8,128)(2,1)S(1)}, u32[]{:S(2)}) copy-start(bf16[256,128]{1,0:T(8,128)(2,1)S(1)} %collective-permute-done.19.refs_3_) | copy-start | bytes 196612
  127.9 5.6 %copy-start.20 = (bf16[256,128]{1,0:T(8,128)(2,1)}, bf16[256,128]{1,0:T(8,128)(2,1)S(1)}, u32[]{:S(2)}) copy-start(bf16[256,128]{1,0:T(8,128)(2,1)S(1)} %collective-permute-done.20.refs_4_) | copy-start | bytes 196612
  129.2 4.2 %copy-start.22 = (bf16[256,128]{1,0:T(8,128)(2,1)}, bf16[256,128]{1,0:T(8,128)(2,1)S(1)}, u32[]{:S(2)}) copy-start(bf16[256,128]{1,0:T(8,128)(2,1)S(1)} %collective-permute-done.21.refs_5_) | copy-start | bytes 196612
  131.0 2.4 %copy-start.23 = (bf16[256,128]{1,0:T(8,128)(2,1)}, bf16[256,128]{1,0:T(8,128)(2,1)S(1)}, u32[]{:S(2)}) copy-start(bf16[256,128]{1,0:T(8,128)(2,1)S(1)} %collective-permute-done.22.refs_6_) | copy-start | bytes 196612
  133.4 0.6 copy-start.25
